TPU v7x, 128 devices: a whole 4x4x4 slice. The times are simulated.
128 devices in a mesh: rows: 64 (over x_lo, y, z, core), cols: 2 (over x_hi).
Axes of the slice: x: 4 (x_hi: 2, x_lo: 2; x = x_hi * 2 + x_lo), y: 4, z: 4, core: 2. Of those that a mesh axis runs over, the one named last changes fastest.
Arguments:
- design: bfloat16 [131072, 6144], P('rows', 'cols'), may hold values from -0.015625 to 0.015625
- targets: bfloat16 [131072, 128], P('rows'), may hold values from -6 to 6
- col_scale: float32 [6144], P('cols'), may hold values from 0.1 to 1
Outputs:
- solution: float32 [6144, 128], P('cols', 'rows')
- residual: float32 [131072, 128], P('rows')
All inputs are finite; a program needn't handle non-finite values.
Results may differ from a plain program's by a relative error of at most 0.0065.
Values may be sent and summed in bfloat16 or wider, within the bound.
No kernel may reach another device: no remote copies, remote signals or barrier semaphores. Data moves between devices by JAX's collectives and lax.ppermute only.
A program may use at most 128 MiB of HBM per device.

v0:
```python
import functools

import jax
import jax.numpy as jnp
from jax import lax
from jax.sharding import Mesh
from jax.sharding import PartitionSpec as P

ITERS = 6
ROWS = ("rows_0", "rows_1", "rows_2", "rows_3")
ROWS_COLS = ("rows_0", "rows_1", "rows_2", "rows_3", "cols")


def split_up(array, dim, size):
    shape = array.shape
    pieces = array.reshape(*shape[:dim], size, shape[dim] // size, *shape[dim + 1 :])
    return jnp.moveaxis(pieces, dim, 0)


def sent_and_summed(array, axis, dim):
    pieces = split_up(array, dim, lax.axis_size(axis))
    arrived = lax.all_to_all(pieces, axis, split_axis=0, concat_axis=0, tiled=True)
    return arrived.sum(axis=0)


def over_axes(array, axes):
    return functools.reduce(lax.psum, axes, array)


def in_order(pieces, dim):
    pieces = jnp.moveaxis(pieces, 0, dim)
    shape = pieces.shape
    return pieces.reshape(*shape[:dim], shape[dim] * shape[dim + 1], *shape[dim + 2 :])


def from_everyone(array, axis):
    copies = jnp.broadcast_to(array, (lax.axis_size(axis), *array.shape))
    return lax.all_to_all(copies, axis, split_axis=0, concat_axis=0, tiled=True)


def gathered_copies(array, axis, dim):
    return in_order(from_everyone(array, axis), dim)


def of_everyone(array, axis):
    return from_everyone(array, axis).astype(jnp.float32).sum(axis=0)


def taken_together(array, axis):
    everything = from_everyone(array, axis)
    return jnp.sum(everything, axis=0)


def local_back(design, vectors):
    return lax.dot_general(
        design, vectors, (((0,), (0,)), ((), ())), preferred_element_type=jnp.float32
    )


def per_device(design, targets, col_scale):
    width = design.shape[1]
    row_count = lax.axis_size(ROWS)
    residual = targets.astype(jnp.float32)
    share = width // row_count
    scale = lax.dynamic_slice_in_dim(col_scale, lax.axis_index(ROWS) * share, share, 0)[:, None]

    def gradient_of(vectors):
        return scale * sent_and_summed(local_back(design, vectors), ROWS, 0)

    def squared(values):
        return over_axes(jnp.sum(values * values, axis=0), ROWS_COLS)

    gradient = gradient_of(targets)
    gamma = squared(gradient)
    solution = jnp.zeros(gradient.shape, jnp.float32)
    direction = gradient
    for step in range(ITERS):
        scaled_dir = (scale * direction).astype(jnp.bfloat16)
        image = of_everyone(
            jnp.dot(
                design, gathered_copies(scaled_dir, ROWS, 0), preferred_element_type=jnp.float32
            ).astype(jnp.bfloat16),
            "cols",
        ).astype(jnp.float32)
        delta = taken_together(jnp.sum(image * image, axis=0), ROWS)
        alpha = gamma / delta
        solution = solution + alpha * direction
        residual = residual - alpha * image
        if step + 1 < ITERS:
            gradient = gradient_of(residual.astype(jnp.bfloat16))
            gamma_new = squared(gradient)
            direction = gradient + gamma_new / gamma * direction
            gamma = gamma_new
    solution_part = lax.all_to_all(solution, ROWS, split_axis=1, concat_axis=0, tiled=True)
    return (solution_part, residual)


def solution(mesh):
    split = Mesh(
        mesh.devices.reshape(2, 4, 4, 2, mesh.shape["cols"]),
        ("rows_0", "rows_1", "rows_2", "rows_3", "cols"),
    )
    in_specs = (P(ROWS, "cols"), P(ROWS, None), P("cols"))
    out_specs = (P("cols", ROWS), P(ROWS, None))
    return jax.shard_map(
        per_device, mesh=split, in_specs=in_specs, out_specs=out_specs, check_vma=False
    )
```

profile of v0, /device:TPU:1, one launch (start us, length us, event | category | flops | bytes accessed | tf_op | source)
XLA Modules:
  0.0 820.6 jit_solution(13330626564013045601)
XLA Ops:
  0.6 9.3 %fusion.13 = f32[3072,128]{1,0:T(8,128)} fusion(bf16[2048,3072]{1,0:T(8,128)(2,1)} %param.3, bf16[2048,128]{1,0:T(8,128)(2,1)} %param.4), kind=kOutput, calls=%fused_computation.58 | convolution fusion | flops 1610612736 | bytes 14680064 | tf_op jit(solution)/shard_map/dot_general | solution.py:55
  9.9 10.9 %all-to-all-start = ((f32[64,48,128]{2,1,0:T(8,128)}), f32[64,48,128]{2,1,0:T(8,128)S(1)}, u32[]{:S(2)}, u32[]{:S(2)}) async-start(f32[64,48,128]{2,1,0:T(8,128)} %bitcast), calls=%async_computation | async-start | bytes 3145728 | tf_op jit(solution)/shard_map/all_to_all | solution.py:22
  21.6 21.7 %all-to-all-done = f32[64,48,128]{2,1,0:T(8,128)S(1)} async-done(((f32[64,48,128]{2,1,0:T(8,128)}), f32[64,48,128]{2,1,0:T(8,128)S(1)}, u32[]{:S(2)}, u32[]{:S(2)}) %all-to-all-start) | async-done | bytes 1572896 | tf_op jit(solution)/shard_map/all_to_all | solution.py:22
  43.6 20.7 %all_to_all.142 = bf16[64,48,128]{2,1,0:T(8,128)(2,1)S(1)} all-to-all(bf16[64,48,128]{2,1,0:T(8,128)(2,1)S(1)} %broadcast_in_dim.72), channel_id=1, replica_groups=mesh['rows_0'=2,'rows_1'=4,'rows_2'=4,'rows_3'=2,'cols'=2] {'rows_0','ro..., dimensions={0} | all-to-all | bytes 1572864 | tf_op jit(solution)/shard_map/all_to_all | solution.py:38
  64.3 8.9 %fusion = bf16[2048,128]{0,1:T(8,128)(2,1)S(1)} fusion(bf16[3072,128]{1,0:T(8,128)(2,1)S(1)} %bitcast.73, bf16[2048,3072]{1,0:T(8,128)(2,1)} %param.3), kind=kOutput, calls=%fused_computation.11 | convolution fusion | flops 1610874880 | bytes 13893632 | tf_op jit(solution)/shard_map/dot_general | solution.py:80
  73.6 18.5 %all_to_all.143 = bf16[2,2048,128]{2,1,0:T(8,128)(2,1)S(1)} all-to-all(bf16[2,2048,128]{2,1,0:T(8,128)(2,1)S(1)} %broadcast_in_dim.73), channel_id=1, replica_groups=mesh['rows_0'=2,'rows_1'=4,'rows_2'=4,'rows_3'=2,'cols'=2] {'cols'}, dimensions={0} | all-to-all | bytes 2097152 | tf_op jit(solution)/shard_map/all_to_all | solution.py:38
  102.5 8.6 %psum.211 = f32[128]{0:T(128)S(1)} all-reduce(f32[128]{0:T(128)S(1)} %psum.210), channel_id=1, replica_groups=mesh['rows_0'=2,'rows_1'=4,'rows_2'=4,'rows_3'=2,'cols'=2] {'rows_1'}, use_global_device_ids=true, to_apply=%region_3.0 | all-reduce | flops 128 | bytes 1024 | tf_op jit(solution)/shard_map/psum | solution.py:27
  111.0 8.4 %psum.212 = f32[128]{0:T(128)S(1)} all-reduce(f32[128]{0:T(128)S(1)} %psum.211), channel_id=1, replica_groups=mesh['rows_0'=2,'rows_1'=4,'rows_2'=4,'rows_3'=2,'cols'=2] {'rows_2'}, use_global_device_ids=true, to_apply=%region_4.0 | all-reduce | flops 128 | bytes 1024 | tf_op jit(solution)/shard_map/psum | solution.py:27
  119.5 7.4 psum.213
  132.4 7.6 convolution_bitcast_fusion.4
  141.8 28.0 %all_to_all.144 = f32[64,48,128]{2,1,0:T(8,128)} all-to-all(f32[64,48,128]{2,1,0:T(8,128)S(1)} %bitcast.68), channel_id=1, replica_groups=mesh['rows_0'=2,'rows_1'=4,'rows_2'=4,'rows_3'=2,'cols'=2] {'rows_0','ro..., dimensions={0} | all-to-all | bytes 3145728 | tf_op jit(solution)/shard_map/all_to_all | solution.py:22
  182.0 7.1 psum.217
  189.1 8.2 %psum.218 = f32[128]{0:T(128)S(1)} all-reduce(f32[128]{0:T(128)S(1)} %psum.217), channel_id=1, replica_groups=mesh['rows_0'=2,'rows_1'=4,'rows_2'=4,'rows_3'=2,'cols'=2] {'rows_3'}, use_global_device_ids=true, to_apply=%region_15.0 | all-reduce | flops 128 | bytes 1024 | tf_op jit(solution)/shard_map/psum | solution.py:27
  202.8 20.0 %all_to_all.145 = bf16[64,48,128]{2,1,0:T(8,128)(2,1)S(1)} all-to-all(bf16[64,48,128]{2,1,0:T(8,128)(2,1)S(1)} %broadcast_in_dim.75), channel_id=1, replica_groups=mesh['rows_0'=2,'rows_1'=4,'rows_2'=4,'rows_3'=2,'cols'=2] {'rows_0','ro..., dimensions={0} | all-to-all | bytes 1572864 | tf_op jit(solution)/shard_map/all_to_all | solution.py:38
  222.8 8.9 %fusion.1 = bf16[2048,128]{0,1:T(8,128)(2,1)S(1)} fusion(bf16[3072,128]{1,0:T(8,128)(2,1)S(1)} %bitcast.74, bf16[2048,3072]{1,0:T(8,128)(2,1)} %param.3), kind=kOutput, calls=%fused_computation.12 | convolution fusion | flops 1610874880 | bytes 13893632 | tf_op jit(solution)/shard_map/dot_general | solution.py:80
  232.1 17.7 %all_to_all.146 = bf16[2,2048,128]{2,1,0:T(8,128)(2,1)S(1)} all-to-all(bf16[2,2048,128]{2,1,0:T(8,128)(2,1)S(1)} %broadcast_in_dim.76), channel_id=1, replica_groups=mesh['rows_0'=2,'rows_1'=4,'rows_2'=4,'rows_3'=2,'cols'=2] {'cols'}, dimensions={0} | all-to-all | bytes 2097152 | tf_op jit(solution)/shard_map/all_to_all | solution.py:38
  250.3 12.8 %all_to_all.147 = f32[64,1,128]{2,1,0:T(1,128)S(1)} all-to-all(f32[64,1,128]{2,1,0:T(1,128)S(1)} %broadcast_in_dim.77), channel_id=1, replica_groups=mesh['rows_0'=2,'rows_1'=4,'rows_2'=4,'rows_3'=2,'cols'=2] {'rows_0','ro..., dimensions={0} | all-to-all | bytes 65536 | tf_op jit(solution)/shard_map/all_to_all | solution.py:38
  264.3 7.5 convolution_bitcast_fusion.3
  274.9 28.5 %all_to_all.148 = f32[64,48,128]{2,1,0:T(8,128)} all-to-all(f32[64,48,128]{2,1,0:T(8,128)} %bitcast.69), channel_id=1, replica_groups=mesh['rows_0'=2,'rows_1'=4,'rows_2'=4,'rows_3'=2,'cols'=2] {'rows_0','ro..., dimensions={0} | all-to-all | bytes 3145728 | tf_op jit(solution)/shard_map/all_to_all | solution.py:22
  315.7 7.1 psum.222
  322.8 8.2 %psum.223 = f32[128]{0:T(128)S(1)} all-reduce(f32[128]{0:T(128)S(1)} %psum.222), channel_id=1, replica_groups=mesh['rows_0'=2,'rows_1'=4,'rows_2'=4,'rows_3'=2,'cols'=2] {'rows_3'}, use_global_device_ids=true, to_apply=%region_25.0 | all-reduce | flops 128 | bytes 1024 | tf_op jit(solution)/shard_map/psum | solution.py:27
  336.4 20.0 %all_to_all.149 = bf16[64,48,128]{2,1,0:T(8,128)(2,1)S(1)} all-to-all(bf16[64,48,128]{2,1,0:T(8,128)(2,1)S(1)} %broadcast_in_dim.78), channel_id=1, replica_groups=mesh['rows_0'=2,'rows_1'=4,'rows_2'=4,'rows_3'=2,'cols'=2] {'rows_0','ro..., dimensions={0} | all-to-all | bytes 1572864 | tf_op jit(solution)/shard_map/all_to_all | solution.py:38
  356.5 8.9 %fusion.2 = bf16[2048,128]{0,1:T(8,128)(2,1)S(1)} fusion(bf16[3072,128]{1,0:T(8,128)(2,1)S(1)} %bitcast.75, bf16[2048,3072]{1,0:T(8,128)(2,1)} %param.3), kind=kOutput, calls=%fused_computation.13 | convolution fusion | flops 1610874880 | bytes 13893632 | tf_op jit(solution)/shard_map/dot_general | solution.py:80
  365.8 17.7 %all_to_all.150 = bf16[2,2048,128]{2,1,0:T(8,128)(2,1)S(1)} all-to-all(bf16[2,2048,128]{2,1,0:T(8,128)(2,1)S(1)} %broadcast_in_dim.79), channel_id=1, replica_groups=mesh['rows_0'=2,'rows_1'=4,'rows_2'=4,'rows_3'=2,'cols'=2] {'cols'}, dimensions={0} | all-to-all | bytes 2097152 | tf_op jit(solution)/shard_map/all_to_all | solution.py:38
  383.9 12.8 %all_to_all.151 = f32[64,1,128]{2,1,0:T(1,128)S(1)} all-to-all(f32[64,1,128]{2,1,0:T(1,128)S(1)} %broadcast_in_dim.80), channel_id=1, replica_groups=mesh['rows_0'=2,'rows_1'=4,'rows_2'=4,'rows_3'=2,'cols'=2] {'rows_0','ro..., dimensions={0} | all-to-all | bytes 65536 | tf_op jit(solution)/shard_map/all_to_all | solution.py:38
  396.7 7.6 convolution_bitcast_fusion.2
  407.3 28.1 %all_to_all.152 = f32[64,48,128]{2,1,0:T(8,128)} all-to-all(f32[64,48,128]{2,1,0:T(8,128)} %bitcast.70), channel_id=1, replica_groups=mesh['rows_0'=2,'rows_1'=4,'rows_2'=4,'rows_3'=2,'cols'=2] {'rows_0','ro..., dimensions={0} | all-to-all | bytes 3145728 | tf_op jit(solution)/shard_map/all_to_all | solution.py:22
  447.6 7.1 psum.227
  454.7 8.2 %psum.228 = f32[128]{0:T(128)S(1)} all-reduce(f32[128]{0:T(128)S(1)} %psum.227), channel_id=1, replica_groups=mesh['rows_0'=2,'rows_1'=4,'rows_2'=4,'rows_3'=2,'cols'=2] {'rows_3'}, use_global_device_ids=true, to_apply=%region_35.0 | all-reduce | flops 128 | bytes 1024 | tf_op jit(solution)/shard_map/psum | solution.py:27
  468.4 20.2 %all_to_all.153 = bf16[64,48,128]{2,1,0:T(8,128)(2,1)S(1)} all-to-all(bf16[64,48,128]{2,1,0:T(8,128)(2,1)S(1)} %broadcast_in_dim.81), channel_id=1, replica_groups=mesh['rows_0'=2,'rows_1'=4,'rows_2'=4,'rows_3'=2,'cols'=2] {'rows_0','ro..., dimensions={0} | all-to-all | bytes 1572864 | tf_op jit(solution)/shard_map/all_to_all | solution.py:38
  488.6 8.9 %fusion.3 = bf16[2048,128]{0,1:T(8,128)(2,1)S(1)} fusion(bf16[3072,128]{1,0:T(8,128)(2,1)S(1)} %bitcast.76, bf16[2048,3072]{1,0:T(8,128)(2,1)} %param.3), kind=kOutput, calls=%fused_computation.14 | convolution fusion | flops 1610874880 | bytes 13893632 | tf_op jit(solution)/shard_map/dot_general | solution.py:80
  497.9 17.7 %all_to_all.154 = bf16[2,2048,128]{2,1,0:T(8,128)(2,1)S(1)} all-to-all(bf16[2,2048,128]{2,1,0:T(8,128)(2,1)S(1)} %broadcast_in_dim.82), channel_id=1, replica_groups=mesh['rows_0'=2,'rows_1'=4,'rows_2'=4,'rows_3'=2,'cols'=2] {'cols'}, dimensions={0} | all-to-all | bytes 2097152 | tf_op jit(solution)/shard_map/all_to_all | solution.py:38
  517.0 12.8 %all_to_all.155 = f32[64,1,128]{2,1,0:T(1,128)S(1)} all-to-all(f32[64,1,128]{2,1,0:T(1,128)S(1)} %broadcast_in_dim.83), channel_id=1, replica_groups=mesh['rows_0'=2,'rows_1'=4,'rows_2'=4,'rows_3'=2,'cols'=2] {'rows_0','ro..., dimensions={0} | all-to-all | bytes 65536 | tf_op jit(solution)/shard_map/all_to_all | solution.py:38
  531.2 7.6 convolution_bitcast_fusion.1
  540.7 27.2 %all_to_all.156 = f32[64,48,128]{2,1,0:T(8,128)} all-to-all(f32[64,48,128]{2,1,0:T(8,128)S(1)} %bitcast.71), channel_id=1, replica_groups=mesh['rows_0'=2,'rows_1'=4,'rows_2'=4,'rows_3'=2,'cols'=2] {'rows_0','ro..., dimensions={0} | all-to-all | bytes 3145728 | tf_op jit(solution)/shard_map/all_to_all | solution.py:22
  580.1 7.1 psum.232
  587.2 8.2 %psum.233 = f32[128]{0:T(128)S(1)} all-reduce(f32[128]{0:T(128)S(1)} %psum.232), channel_id=1, replica_groups=mesh['rows_0'=2,'rows_1'=4,'rows_2'=4,'rows_3'=2,'cols'=2] {'rows_3'}, use_global_device_ids=true, to_apply=%region_45.0 | all-reduce | flops 128 | bytes 1024 | tf_op jit(solution)/shard_map/psum | solution.py:27
  600.9 20.2 %all_to_all.157 = bf16[64,48,128]{2,1,0:T(8,128)(2,1)S(1)} all-to-all(bf16[64,48,128]{2,1,0:T(8,128)(2,1)S(1)} %broadcast_in_dim.84), channel_id=1, replica_groups=mesh['rows_0'=2,'rows_1'=4,'rows_2'=4,'rows_3'=2,'cols'=2] {'rows_0','ro..., dimensions={0} | all-to-all | bytes 1572864 | tf_op jit(solution)/shard_map/all_to_all | solution.py:38
  621.1 8.9 %fusion.4 = bf16[2048,128]{0,1:T(8,128)(2,1)S(1)} fusion(bf16[3072,128]{1,0:T(8,128)(2,1)S(1)} %bitcast.77, bf16[2048,3072]{1,0:T(8,128)(2,1)} %param.3), kind=kOutput, calls=%fused_computation.15 | convolution fusion | flops 1610874880 | bytes 13893632 | tf_op jit(solution)/shard_map/dot_general | solution.py:80
  630.4 17.7 %all_to_all.158 = bf16[2,2048,128]{2,1,0:T(8,128)(2,1)S(1)} all-to-all(bf16[2,2048,128]{2,1,0:T(8,128)(2,1)S(1)} %broadcast_in_dim.85), channel_id=1, replica_groups=mesh['rows_0'=2,'rows_1'=4,'rows_2'=4,'rows_3'=2,'cols'=2] {'cols'}, dimensions={0} | all-to-all | bytes 2097152 | tf_op jit(solution)/shard_map/all_to_all | solution.py:38
  648.5 12.8 %all_to_all.159 = f32[64,1,128]{2,1,0:T(1,128)S(1)} all-to-all(f32[64,1,128]{2,1,0:T(1,128)S(1)} %broadcast_in_dim.86), channel_id=1, replica_groups=mesh['rows_0'=2,'rows_1'=4,'rows_2'=4,'rows_3'=2,'cols'=2] {'rows_0','ro..., dimensions={0} | all-to-all | bytes 65536 | tf_op jit(solution)/shard_map/all_to_all | solution.py:38
  661.4 7.5 convolution_bitcast_fusion
  671.9 28.1 %all_to_all.160 = f32[64,48,128]{2,1,0:T(8,128)} all-to-all(f32[64,48,128]{2,1,0:T(8,128)} %bitcast.72), channel_id=1, replica_groups=mesh['rows_0'=2,'rows_1'=4,'rows_2'=4,'rows_3'=2,'cols'=2] {'rows_0','ro..., dimensions={0} | all-to-all | bytes 3145728 | tf_op jit(solution)/shard_map/all_to_all | solution.py:22
  719.4 8.2 %psum.238 = f32[128]{0:T(128)S(1)} all-reduce(f32[128]{0:T(128)S(1)} %psum.237), channel_id=1, replica_groups=mesh['rows_0'=2,'rows_1'=4,'rows_2'=4,'rows_3'=2,'cols'=2] {'rows_3'}, use_global_device_ids=true, to_apply=%region_55.0 | all-reduce | flops 128 | bytes 1024 | tf_op jit(solution)/shard_map/psum | solution.py:27
  733.1 20.3 %all_to_all.161 = bf16[64,48,128]{2,1,0:T(8,128)(2,1)S(1)} all-to-all(bf16[64,48,128]{2,1,0:T(8,128)(2,1)S(1)} %broadcast_in_dim.87), channel_id=1, replica_groups=mesh['rows_0'=2,'rows_1'=4,'rows_2'=4,'rows_3'=2,'cols'=2] {'rows_0','ro..., dimensions={0} | all-to-all | bytes 1572864 | tf_op jit(solution)/shard_map/all_to_all | solution.py:38
  753.4 8.9 %fusion.5 = bf16[2048,128]{0,1:T(8,128)(2,1)S(1)} fusion(bf16[3072,128]{1,0:T(8,128)(2,1)S(1)} %bitcast.78, bf16[2048,3072]{1,0:T(8,128)(2,1)} %param.3), kind=kOutput, calls=%fused_computation.16 | convolution fusion | flops 1610874880 | bytes 13893632 | tf_op jit(solution)/shard_map/dot_general | solution.py:80
  762.7 17.7 %all_to_all.162 = bf16[2,2048,128]{2,1,0:T(8,128)(2,1)S(1)} all-to-all(bf16[2,2048,128]{2,1,0:T(8,128)(2,1)S(1)} %broadcast_in_dim.88), channel_id=1, replica_groups=mesh['rows_0'=2,'rows_1'=4,'rows_2'=4,'rows_3'=2,'cols'=2] {'cols'}, dimensions={0} | all-to-all | bytes 2097152 | tf_op jit(solution)/shard_map/all_to_all | solution.py:38
  802.3 9.0 %all-to-all-start.24 = ((f32[48,64,2]{0,2,1:T(2,128)}), f32[48,64,2]{0,2,1:T(2,128)S(1)}, u32[]{:S(2)}, u32[]{:S(2)}) async-start(f32[48,64,2]{0,2,1:T(2,128)} %multiply_add_fusion), calls=%async_computation.24 | async-start | bytes 131072 | tf_op jit(solution)/shard_map/all_to_all | solution.py:94
  (142 shorter events, 163.8 us)
Async XLA Ops:
  9.9 33.4 %all-to-all-start = ((f32[64,48,128]{2,1,0:T(8,128)}), f32[64,48,128]{2,1,0:T(8,128)S(1)}, u32[]{:S(2)}, u32[]{:S(2)}) async-start(f32[64,48,128]{2,1,0:T(8,128)} %bitcast), calls=%async_computation | async-start | bytes 3145728 | tf_op jit(solution)/shard_map/all_to_all | solution.py:22
  21.6 711.2 %copy-start.2 = (f32[48]{0:T(128)}, f32[48]{0:T(128)S(1)}, u32[]{:S(2)}) copy-start(f32[48]{0:T(128)S(1)} %dynamic_slice.3) | copy-start | bytes 580
  21.6 110.7 %copy-start.1 = (bf16[2048,128]{1,0:T(8,128)(2,1)S(1)}, bf16[2048,128]{1,0:T(8,128)(2,1)}, u32[]{:S(2)}) copy-start(bf16[2048,128]{1,0:T(8,128)(2,1)} %param.4) | copy-start | bytes 1572868
  93.2 39.2 %all-to-all-start.3 = ((f32[64,1,128]{2,1,0:T(1,128)}), f32[64,1,128]{2,1,0:T(1,128)S(1)}, u32[]{:S(2)}, u32[]{:S(2)}) async-start(f32[64,1,128]{2,1,0:T(1,128)} %broadcast_in_dim.74), calls=%async_computation.3 | async-start | bytes 65536 | tf_op jit(solution)/shard_map/all_to_all | solution.py:38
  468.2 63.0 %copy-start.5 = (f32[128]{0:T(128)}, f32[128]{0:T(128)S(1)}, u32[]{:S(2)}) copy-start(f32[128]{0:T(128)S(1)} %div.38) | copy-start | bytes 1540
  515.7 1.0 copy-start
  529.9 10.8 %copy-start.6 = (f32[128]{0:T(128)}, f32[128]{0:T(128)S(1)}, u32[]{:S(2)}) copy-start(f32[128]{0:T(128)S(1)} %div.39) | copy-start | bytes 1540
  600.7 132.2 %copy-start.4 = (f32[128]{0:T(128)}, f32[128]{0:T(128)S(1)}, u32[]{:S(2)}) copy-start(f32[128]{0:T(128)S(1)} %div.40) | copy-start | bytes 1540
  661.4 10.6 %copy-start.3 = (f32[128]{0:T(128)}, f32[128]{0:T(128)S(1)}, u32[]{:S(2)}) copy-start(f32[128]{0:T(128)S(1)} %div.41) | copy-start | bytes 1540
  732.8 47.5 %copy-start.9 = (f32[128]{0:T(128)}, f32[128]{0:T(128)S(1)}, u32[]{:S(2)}) copy-start(f32[128]{0:T(128)S(1)} %psum.239) | copy-start | bytes 1540
  732.9 48.5 %copy-start.7 = (f32[128]{0:T(128)}, f32[128]{0:T(128)S(1)}, u32[]{:S(2)}) copy-start(f32[128]{0:T(128)S(1)} %div.42) | copy-start | bytes 1540
  781.4 16.9 %all-to-all-start.23 = ((f32[64,1,128]{2,1,0:T(1,128)}), f32[64,1,128]{2,1,0:T(1,128)}, u32[]{:S(2)}, u32[]{:S(2)}) async-start(f32[64,1,128]{2,1,0:T(1,128)} %broadcast_in_dim.89), calls=%async_computation.23 | async-start | bytes 65536 | tf_op jit(solution)/shard_map/all_to_all | solution.py:38
  799.7 2.6 copy-start.8
  802.3 17.2 %all-to-all-start.24 = ((f32[48,64,2]{0,2,1:T(2,128)}), f32[48,64,2]{0,2,1:T(2,128)S(1)}, u32[]{:S(2)}, u32[]{:S(2)}) async-start(f32[48,64,2]{0,2,1:T(2,128)} %multiply_add_fusion), calls=%async_computation.24 | async-start | bytes 131072 | tf_op jit(solution)/shard_map/all_to_all | solution.py:94
where the time goes:
time: 831 us; the launch traced here: 821 us
  blocking collectives  609 us (73%)
  matrix products  101 us (12%)
  starting transfers between devices  30.7 us (4%)
  local copies, waits for them, and re-layouts  30.7 us (4%)
  waiting for transfers between devices  28.1 us (3%)
  other arithmetic  19.8 us (2%)
    all_to_all x16, blocking collectives, from_everyone(): return lax.all_to_all(copies, axis, split_axis=0, concat_axis=0, tiled=True)  280 us
    psum x30, blocking collectives, over_axes(): return functools.reduce(lax.psum, axes, array)  190 us
    all_to_all x5, blocking collectives, sent_and_summed(): lax.all_to_all(pieces, axis, split_axis=0, concat_axis=0, tiled=True)  140 us
    dot_general x6, matrix products, per_device(): jnp.dot(design, gathered_copies(scaled_dir, ROWS, 0), preferred_element_t...  53.5 us
    dot_general x6, matrix products, local_back(): lax.dot_general(design, vectors, (((0,), (0,)), ((), ())), preferred_elem...  47 us
    all_to_all x1, waiting for transfers between devices, sent_and_summed(): lax.all_to_all(pieces, axis, split_axis=0, concat_axis=0, tiled=True)  21.7 us
  transfers between devices with their start and end apart: 4, of which 2 were waited for; matrix products, arithmetic and copies ran while one was open for 2% of the time, Pallas kernels for 0%

commit v1 on v0

v1 whole, which is shorter than its diff:
```python
import functools

import jax
import jax.numpy as jnp
from jax import lax
from jax.sharding import Mesh
from jax.sharding import PartitionSpec as P

ITERS = 6
CHIPS = ("rows_0", "rows_1", "rows_2")
CORE = "rows_3"
ROWS = ("rows_0", "rows_1", "rows_2", "rows_3")
COLS = "cols"
BF16 = jnp.bfloat16
F32 = jnp.float32


def swapped(array, axis):
    return lax.ppermute(array, axis, ((0, 1), (1, 0)))


def local_back(design, vectors):
    return lax.dot_general(
        design, vectors, (((0,), (0,)), ((), ())), preferred_element_type=F32
    )


def local_image(design, vectors):
    return jnp.dot(design, vectors, preferred_element_type=F32)


def sum_over_rows(partial, square):
    core = lax.axis_index(CORE)
    chips = lax.axis_size(CHIPS)
    width, fits = partial.shape
    halves = partial.astype(BF16).reshape(2, width // 2, fits)
    kept = lax.dynamic_index_in_dim(halves, core, 0, False)
    given = lax.dynamic_index_in_dim(halves, 1 - core, 0, False)
    both = kept.astype(F32) + swapped(given, CORE).astype(F32)
    pieces = both.astype(BF16).reshape(chips, -1, fits)
    arrived = lax.all_to_all(pieces, CHIPS, split_axis=0, concat_axis=0, tiled=True)
    share = arrived.astype(F32).sum(axis=0)
    own = lax.axis_index(CORE) * chips + lax.axis_index(CHIPS)
    rows = share.shape[0]
    scaled = share * lax.dynamic_slice_in_dim(square, own * rows, rows, 0)
    copies = jnp.broadcast_to(scaled.astype(BF16), (chips, rows, fits))
    half = lax.all_to_all(copies, CHIPS, split_axis=0, concat_axis=0, tiled=True)
    half = half.reshape(width // 2, fits)
    other = swapped(half, CORE)
    low = jnp.where(core == 0, half, other)
    high = jnp.where(core == 0, other, half)
    return jnp.concatenate([low, high], axis=0)


def sum_over_cols(array):
    return array.astype(F32) + swapped(array, COLS).astype(F32)


def per_device(design, targets, col_scale):
    scale = col_scale[:, None]
    square = scale * scale
    weight = 1.0 / square
    width = design.shape[1]
    residual = targets.astype(F32)

    start = sum_over_rows(local_back(design, targets), square)
    gradient = start.astype(F32)
    gamma = sum_over_cols(jnp.sum(gradient * gradient * weight, axis=0))
    direction = gradient
    fit = jnp.zeros_like(gradient)
    moved = local_image(design, start)
    partial = moved
    for step in range(ITERS):
        image = sum_over_cols(partial.astype(BF16))
        if step + 1 < ITERS:
            back = sum_over_rows(local_back(design, image.astype(BF16)), square)
            back_image = local_image(design, back)
            back = back.astype(F32)
            weighted = back * weight
            sums = jnp.stack(
                [
                    jnp.sum(direction * weighted, axis=0),
                    jnp.sum(gradient * weighted, axis=0),
                    jnp.sum(back * weighted, axis=0),
                ]
            )
            sums = sum_over_cols(sums)
            delta = sums[0]
        else:
            delta = jnp.sum(image * image, axis=0)
            copies = jnp.broadcast_to(delta, (lax.axis_size(ROWS), 1, *delta.shape))
            delta = lax.all_to_all(copies, ROWS, split_axis=0, concat_axis=0, tiled=True)
            delta = delta.sum(axis=(0, 1))
        alpha = gamma / delta
        fit = fit + alpha * direction
        residual = residual - alpha * image
        if step + 1 < ITERS:
            gamma_new = gamma - 2.0 * alpha * sums[1] + alpha * alpha * sums[2]
            ratio = gamma_new / gamma
            gradient = gradient - alpha * back
            direction = gradient + ratio * direction
            moved = moved - alpha * back_image
            partial = moved + ratio * partial
            gamma = gamma_new
    fits = targets.shape[1]
    count = fits // lax.axis_size(ROWS)
    part = lax.dynamic_slice_in_dim(fit, lax.axis_index(ROWS) * count, count, 1)
    return part / scale, residual


def solution(mesh):
    split = Mesh(
        mesh.devices.reshape(2, 4, 4, 2, mesh.shape["cols"]),
        ("rows_0", "rows_1", "rows_2", "rows_3", "cols"),
    )
    in_specs = (P(ROWS, "cols"), P(ROWS, None), P("cols"))
    out_specs = (P("cols", ROWS), P(ROWS, None))
    return jax.shard_map(
        per_device, mesh=split, in_specs=in_specs, out_specs=out_specs, check_vma=False
    )
```

time: 831 us -> 484 us (0.58)
  blocking collectives: 609 us -> 141 us
  waiting for transfers between devices: 28.1 us -> 110 us
  starting transfers between devices: 30.7 us -> 66.5 us
  other arithmetic: 19.8 us -> 51.6 us
  matrix products: 101 us -> 83.3 us
  local copies, waits for them, and re-layouts: 30.7 us -> 20 us
    all_to_all x21 -> x11, blocking collectives: 419 us -> 141 us  [the longest x6 77.4 us: sum_over_rows(): lax.all_to_all(copies, CHIPS, split_axis=0, concat_axis=0, tiled=True)]
    psum x30 -> x0, blocking collectives: 190 us -> none  [over_axes(): return functools.reduce(lax.psum, axes, array)]
    ppermute x0 -> x24, waiting for transfers between devices: none -> 94.5 us  [swapped(): return lax.ppermute(array, axis, ((0, 1), (1, 0)))]
    ppermute x0 -> x24, starting transfers between devices: none -> 50.9 us  [swapped(): return lax.ppermute(array, axis, ((0, 1), (1, 0)))]
    dot_general x6, matrix products: 47 us -> 22.1 us  [local_back(): lax.dot_general(design, vectors, (((0,), (0,)), ((), ())), preferred_elem...]
    all_to_all x4 -> x2, starting transfers between devices: 30.7 us -> 15.7 us  [the longest x1 9.09 us: sum_over_rows(): lax.all_to_all(pieces, CHIPS, split_axis=0, concat_axis=0, tiled=True)]
    reduce_sum x30 -> x13, other arithmetic: 12 us -> 26.2 us  [the longest x5 24.3 us: per_device(): jnp.sum(direction * weighted, axis=0)]
    convert_element_type x5 -> x19, other arithmetic: 0.4 us -> 13.4 us  [the longest x5 9.01 us: per_device(): image = sum_over_cols(partial.astype(BF16))]
  transfers between devices with their start and end apart: 4 -> 26, of which waited for: 2 -> 24; matrix products, arithmetic and copies ran while one was open for 2% -> 5% of each run, Pallas kernels for 0% -> 0%
where the time goes in v1:
time: 484 us; the launch traced here: 474 us
  blocking collectives  141 us (29%)
  waiting for transfers between devices  110 us (23%)
  matrix products  83.3 us (17%)
  starting transfers between devices  66.5 us (14%)
  other arithmetic  51.6 us (11%)
  local copies, waits for them, and re-layouts  20 us (4%)
    ppermute x24, waiting for transfers between devices, swapped(): return lax.ppermute(array, axis, ((0, 1), (1, 0)))  94.5 us
    all_to_all x6, blocking collectives, sum_over_rows(): lax.all_to_all(copies, CHIPS, split_axis=0, concat_axis=0, tiled=True)  77.4 us
    all_to_all x5, blocking collectives, sum_over_rows(): lax.all_to_all(pieces, CHIPS, split_axis=0, concat_axis=0, tiled=True)  63.8 us
    dot_general x6, matrix products, local_image(): return jnp.dot(design, vectors, preferred_element_type=F32)  61.2 us
    ppermute x24, starting transfers between devices, swapped(): return lax.ppermute(array, axis, ((0, 1), (1, 0)))  50.9 us
    reduce_sum x5, other arithmetic, per_device(): jnp.sum(direction * weighted, axis=0)  24.3 us
    dot_general x6, matrix products, local_back(): lax.dot_general(design, vectors, (((0,), (0,)), ((), ())), preferred_elem...  22.1 us
    unnamed x121, local copies, waits for them, and re-layouts  10.7 us
  transfers between devices with their start and end apart: 26, of which 24 were waited for; matrix products, arithmetic and copies ran while one was open for 5% of the time, Pallas kernels for 0%

profile of v1, /device:TPU:1, one launch (start us, length us, event | category | flops | bytes accessed | tf_op | source)
XLA Modules:
  0.0 474.5 jit_solution(15394201205140212498)
XLA Ops:
  0.6 8.1 %convolution_convert_fusion.5 = bf16[3072,128]{1,0:T(8,128)(2,1)S(1)} fusion(bf16[2048,3072]{1,0:T(8,128)(2,1)} %param.3, bf16[2048,128]{1,0:T(8,128)(2,1)} %param.4), kind=kOutput, calls=%fused_computation.5 | convolution fusion | flops 1611005952 | bytes 13893632 | tf_op jit(solution)/shard_map/dot_general | solution.py:23
  12.5 9.1 %all-to-all-start = ((bf16[32,48,128]{2,1,0:T(8,128)(2,1)}), bf16[32,48,128]{2,1,0:T(8,128)(2,1)S(1)}, u32[]{:S(2)}, u32[]{:S(2)}) async-start(bf16[32,48,128]{2,1,0:T(8,128)(2,1)} %bitcast.3), calls=%async_computation | async-start | bytes 786432 | tf_op jit(solution)/shard_map/all_to_all | solution.py:41
  21.7 9.0 %all-to-all-done = bf16[32,48,128]{2,1,0:T(8,128)(2,1)S(1)} async-done(((bf16[32,48,128]{2,1,0:T(8,128)(2,1)}), bf16[32,48,128]{2,1,0:T(8,128)(2,1)S(1)}, u32[]{:S(2)}, u32[]{:S(2)}) %all-to-all-start) | async-done | bytes 393248 | tf_op jit(solution)/shard_map/all_to_all | solution.py:41
  30.9 12.8 %all_to_all.65 = bf16[32,48,128]{2,1,0:T(8,128)(2,1)S(1)} all-to-all(bf16[32,48,128]{2,1,0:T(8,128)(2,1)S(1)} %broadcast_in_dim.14), channel_id=1, replica_groups=mesh['rows_0'=2,'rows_1'=4,'rows_2'=4,'rows_3'=2,'cols'=2] {'rows_0','ro..., dimensions={0} | all-to-all | bytes 786432 | tf_op jit(solution)/shard_map/all_to_all | solution.py:47
  43.7 2.8 collective-permute-start.1
  47.9 9.1 %fusion.78 = f32[128,2048]{1,0:T(8,128)S(1)} fusion(bf16[2048,3072]{1,0:T(8,128)(2,1)} %param.3, bf16[1536,128]{1,0:T(8,128)(2,1)S(1)} %get-tuple-element.61, bf16[1536,128]{1,0:T(8,128)(2,1)S(1)} %get-tuple-element.60), kind=kOutput, calls=%fused_computation.189 | convolution fusion | flops 1612185600 | bytes 14417920 | tf_op jit(solution)/shard_map/dot_general | solution.py:29
  59.6 12.2 %collective-permute-done.3 = bf16[2048,128]{0,1:T(8,128)(2,1)S(1)} collective-permute-done((bf16[2048,128]{0,1:T(8,128)(2,1)S(1)}, bf16[2048,128]{0,1:T(8,128)(2,1)S(1)}, u32[]{:S(2)}, u32[]{:S(2)}) %collective-permute-start.3) | collective-permute-done | bytes 524320 | tf_op jit(solution)/shard_map/ppermute | solution.py:19
  71.8 2.8 fusion
  78.9 13.1 %all_to_all.66 = bf16[32,48,128]{2,1,0:T(8,128)(2,1)S(1)} all-to-all(bf16[32,48,128]{2,1,0:T(8,128)(2,1)S(1)} %bitcast.212), channel_id=1, replica_groups=mesh['rows_0'=2,'rows_1'=4,'rows_2'=4,'rows_3'=2,'cols'=2] {'rows_0','ro..., dimensions={0} | all-to-all | bytes 786432 | tf_op jit(solution)/shard_map/all_to_all | solution.py:41
  92.3 12.8 %all_to_all.67 = bf16[32,48,128]{2,1,0:T(8,128)(2,1)S(1)} all-to-all(bf16[32,48,128]{2,1,0:T(8,128)(2,1)S(1)} %broadcast_in_dim.15), channel_id=1, replica_groups=mesh['rows_0'=2,'rows_1'=4,'rows_2'=4,'rows_3'=2,'cols'=2] {'rows_0','ro..., dimensions={0} | all-to-all | bytes 786432 | tf_op jit(solution)/shard_map/all_to_all | solution.py:47
  105.1 2.8 collective-permute-start.5
  109.3 4.0 fusion.15
  115.9 9.9 %fusion.76 = f32[128,2048]{1,0:T(8,128)} fusion(bf16[2048,3072]{1,0:T(8,128)(2,1)} %param.3, bf16[1536,128]{1,0:T(8,128)(2,1)S(1)} %get-tuple-element.59, bf16[1536,128]{1,0:T(8,128)(2,1)S(1)} %get-tuple-element.58), kind=kOutput, calls=%fused_computation.187 | convolution fusion | flops 1612185600 | bytes 14417920 | tf_op jit(solution)/shard_map/dot_general | solution.py:29
  126.6 3.1 collective-permute-done.2
  133.1 12.4 %collective-permute-done.7 = bf16[2048,128]{0,1:T(8,128)(2,1)S(1)} collective-permute-done((bf16[2048,128]{0,1:T(8,128)(2,1)S(1)}, bf16[2048,128]{0,1:T(8,128)(2,1)S(1)}, u32[]{:S(2)}, u32[]{:S(2)}) %collective-permute-start.7) | collective-permute-done | bytes 524320 | tf_op jit(solution)/shard_map/ppermute | solution.py:19
  146.2 2.8 fusion.1
  150.6 2.7 collective-permute-start.8
  154.8 12.6 %all_to_all.68 = bf16[32,48,128]{2,1,0:T(8,128)(2,1)S(1)} all-to-all(bf16[32,48,128]{2,1,0:T(8,128)(2,1)S(1)} %bitcast.213), channel_id=1, replica_groups=mesh['rows_0'=2,'rows_1'=4,'rows_2'=4,'rows_3'=2,'cols'=2] {'rows_0','ro..., dimensions={0} | all-to-all | bytes 786432 | tf_op jit(solution)/shard_map/all_to_all | solution.py:41
  167.6 12.8 %all_to_all.69 = bf16[32,48,128]{2,1,0:T(8,128)(2,1)S(1)} all-to-all(bf16[32,48,128]{2,1,0:T(8,128)(2,1)S(1)} %broadcast_in_dim.16), channel_id=1, replica_groups=mesh['rows_0'=2,'rows_1'=4,'rows_2'=4,'rows_3'=2,'cols'=2] {'rows_0','ro..., dimensions={0} | all-to-all | bytes 786432 | tf_op jit(solution)/shard_map/all_to_all | solution.py:47
  180.4 3.1 collective-permute-start.9
  185.1 5.0 %fusion.18 = (f32[128]{0:T(128)S(1)}, f32[128]{0:T(128)S(1)}, f32[128]{0:T(128)S(1)}, f32[3072,128]{1,0:T(8,128)}) fusion(f32[3072]{0:T(1024)S(1)} %get-tuple-element.62, bf16[1536,128]{1,0:T(8,128)(2,1)S(1)} %get-tuple-element.57, bf16[1536,128]{1,0:T(8,128)(2,1)S(1)} %get-tuple-element.56, bf16[1536,128]{1,0:T(8,128)(2,1)S(1)} %get-tuple-element.59, ...), kind=kLoop, calls=%fused_computation.39 | loop fusion | flops 9043584 | bytes 3947008 | tf_op jit(solution)/shard_map/reduce_sum | solution.py:82
  194.1 10.8 %multiply_subtract_fusion.3 = f32[128,2048]{1,0:T(8,128)} fusion(f32[128,2048]{1,0:T(8,128)} %copy-done.1, f32[128,2048]{1,0:T(8,128)} %fusion.76, f32[128]{0:T(128)S(1)} %get-tuple-element.43, f32[128]{0:T(128)S(1)} %get-tuple-element.49, bf16[2048,3072]{1,0:T(8,128)(2,1)} %param.3, bf16[1536,128]{1,0:T(8,128)(2,1)} %copy-done.34, ...), kind=kOutput, calls=%fused_computation.82 | convolution fusion | flops 1613234176 | bytes 16516096 | tf_op jit(solution)/shard_map/dot_general | solution.py:29
  208.6 11.7 %collective-permute-done.11 = bf16[2048,128]{0,1:T(8,128)(2,1)S(1)} collective-permute-done((bf16[2048,128]{0,1:T(8,128)(2,1)S(1)}, bf16[2048,128]{0,1:T(8,128)(2,1)S(1)}, u32[]{:S(2)}, u32[]{:S(2)}) %collective-permute-start.11) | collective-permute-done | bytes 524320 | tf_op jit(solution)/shard_map/ppermute | solution.py:19
  221.0 2.8 fusion.2
  229.3 12.8 %all_to_all.70 = bf16[32,48,128]{2,1,0:T(8,128)(2,1)S(1)} all-to-all(bf16[32,48,128]{2,1,0:T(8,128)(2,1)S(1)} %bitcast.214), channel_id=1, replica_groups=mesh['rows_0'=2,'rows_1'=4,'rows_2'=4,'rows_3'=2,'cols'=2] {'rows_0','ro..., dimensions={0} | all-to-all | bytes 786432 | tf_op jit(solution)/shard_map/all_to_all | solution.py:41
  242.3 13.0 %all_to_all.71 = bf16[32,48,128]{2,1,0:T(8,128)(2,1)S(1)} all-to-all(bf16[32,48,128]{2,1,0:T(8,128)(2,1)S(1)} %broadcast_in_dim.17), channel_id=1, replica_groups=mesh['rows_0'=2,'rows_1'=4,'rows_2'=4,'rows_3'=2,'cols'=2] {'rows_0','ro..., dimensions={0} | all-to-all | bytes 786432 | tf_op jit(solution)/shard_map/all_to_all | solution.py:47
  255.3 2.9 collective-permute-start.13
  259.7 5.0 %fusion.22 = (f32[128]{0:T(128)S(1)}, f32[128]{0:T(128)S(1)}, f32[128]{0:T(128)S(1)}, f32[3072,128]{1,0:T(8,128)S(1)}, f32[3072,128]{1,0:T(8,128)}) fusion(f32[3072]{0:T(1024)S(1)} %get-tuple-element.62, bf16[1536,128]{1,0:T(8,128)(2,1)S(1)} %get-tuple-element.55, bf16[1536,128]{1,0:T(8,128)(2,1)S(1)} %get-tuple-element.54, f32[3072,128]{1,0:T(8,128)S(1)} %copy-done.7, ...), kind=kLoop, calls=%fused_computation.43 | loop fusion | flops 11402880 | bytes 7879680 | tf_op jit(solution)/shard_map/reduce_sum | solution.py:82
  266.7 10.8 %fusion.77 = f32[128,2048]{1,0:T(8,128)} fusion(bf16[2048,3072]{1,0:T(8,128)(2,1)} %param.3, bf16[1536,128]{1,0:T(8,128)(2,1)} %copy-done.16, bf16[1536,128]{1,0:T(8,128)(2,1)S(1)} %get-tuple-element.54), kind=kOutput, calls=%fused_computation.188 | convolution fusion | flops 1612185600 | bytes 14417920 | tf_op jit(solution)/shard_map/dot_general | solution.py:29
  277.5 3.1 convert_bitcast_fusion
  281.8 13.2 %collective-permute-done.15 = bf16[2048,128]{0,1:T(8,128)(2,1)S(1)} collective-permute-done((bf16[2048,128]{0,1:T(8,128)(2,1)S(1)}, bf16[2048,128]{0,1:T(8,128)(2,1)S(1)}, u32[]{:S(2)}, u32[]{:S(2)}) %collective-permute-start.15) | collective-permute-done | bytes 524320 | tf_op jit(solution)/shard_map/ppermute | solution.py:19
  295.8 2.8 fusion.3
  303.1 12.5 %all_to_all.72 = bf16[32,48,128]{2,1,0:T(8,128)(2,1)S(1)} all-to-all(bf16[32,48,128]{2,1,0:T(8,128)(2,1)S(1)} %bitcast.215), channel_id=1, replica_groups=mesh['rows_0'=2,'rows_1'=4,'rows_2'=4,'rows_3'=2,'cols'=2] {'rows_0','ro..., dimensions={0} | all-to-all | bytes 786432 | tf_op jit(solution)/shard_map/all_to_all | solution.py:41
  315.9 13.0 %all_to_all.73 = bf16[32,48,128]{2,1,0:T(8,128)(2,1)S(1)} all-to-all(bf16[32,48,128]{2,1,0:T(8,128)(2,1)S(1)} %broadcast_in_dim.18), channel_id=1, replica_groups=mesh['rows_0'=2,'rows_1'=4,'rows_2'=4,'rows_3'=2,'cols'=2] {'rows_0','ro..., dimensions={0} | all-to-all | bytes 786432 | tf_op jit(solution)/shard_map/all_to_all | solution.py:47
  328.9 3.0 collective-permute-start.17
  333.3 5.0 %fusion.26 = (f32[128]{0:T(128)S(1)}, f32[128]{0:T(128)S(1)}, f32[128]{0:T(128)S(1)}, f32[3072,128]{1,0:T(8,128)}) fusion(f32[3072]{0:T(1024)S(1)} %get-tuple-element.62, bf16[1536,128]{1,0:T(8,128)(2,1)S(1)} %get-tuple-element.53, bf16[1536,128]{1,0:T(8,128)(2,1)S(1)} %get-tuple-element.52, f32[3072,128]{1,0:T(8,128)S(1)} %copy-done.12, ...), kind=kLoop, calls=%fused_computation.47 | loop fusion | flops 7470720 | bytes 6306304 | tf_op jit(solution)/shard_map/reduce_sum | solution.py:82
  342.4 10.8 %multiply_subtract_fusion.1 = f32[128,2048]{1,0:T(8,128)} fusion(f32[128]{0:T(128)S(1)} %get-tuple-element.32, f32[128,2048]{1,0:T(8,128)} %multiply_subtract_fusion.3, f32[128,2048]{1,0:T(8,128)} %fusion.77, f32[128]{0:T(128)S(1)} %get-tuple-element.38, bf16[2048,3072]{1,0:T(8,128)(2,1)} %param.3, bf16[1536,128]{1,0:T(8,128)(2,1)} %copy-done.38, ...), kind=kOutput, calls=%fused_computation.77 | convolution fusion | flops 1613234176 | bytes 16516096 | tf_op jit(solution)/shard_map/dot_general | solution.py:29
  356.9 11.6 %collective-permute-done.19 = bf16[2048,128]{0,1:T(8,128)(2,1)S(1)} collective-permute-done((bf16[2048,128]{0,1:T(8,128)(2,1)S(1)}, bf16[2048,128]{0,1:T(8,128)(2,1)S(1)}, u32[]{:S(2)}, u32[]{:S(2)}) %collective-permute-start.19) | collective-permute-done | bytes 524320 | tf_op jit(solution)/shard_map/ppermute | solution.py:19
  377.6 12.8 %all_to_all.74 = bf16[32,48,128]{2,1,0:T(8,128)(2,1)S(1)} all-to-all(bf16[32,48,128]{2,1,0:T(8,128)(2,1)S(1)} %bitcast.211), channel_id=1, replica_groups=mesh['rows_0'=2,'rows_1'=4,'rows_2'=4,'rows_3'=2,'cols'=2] {'rows_0','ro..., dimensions={0} | all-to-all | bytes 786432 | tf_op jit(solution)/shard_map/all_to_all | solution.py:41
  390.6 13.0 %all_to_all.75 = bf16[32,48,128]{2,1,0:T(8,128)(2,1)S(1)} all-to-all(bf16[32,48,128]{2,1,0:T(8,128)(2,1)S(1)} %broadcast_in_dim.19), channel_id=1, replica_groups=mesh['rows_0'=2,'rows_1'=4,'rows_2'=4,'rows_3'=2,'cols'=2] {'rows_0','ro..., dimensions={0} | all-to-all | bytes 786432 | tf_op jit(solution)/shard_map/all_to_all | solution.py:47
  403.5 3.0 collective-permute-start.21
  408.0 5.3 %fusion.12 = (f32[128]{0:T(128)S(1)}, f32[128]{0:T(128)S(1)}, f32[128]{0:T(128)S(1)}, f32[3072,128]{1,0:T(8,128)}, f32[3072,128]{1,0:T(8,128)}) fusion(f32[3072]{0:T(1024)S(1)} %get-tuple-element.62, bf16[1536,128]{1,0:T(8,128)(2,1)S(1)} %get-tuple-element.51, bf16[1536,128]{1,0:T(8,128)(2,1)S(1)} %get-tuple-element.50, f32[3072,128]{1,0:T(8,128)S(1)} %copy-done.11, ...), kind=kLoop, calls=%fused_computation.33 | loop fusion | flops 9830016 | bytes 8666112 | tf_op jit(solution)/shard_map/reduce_sum | solution.py:82
  417.4 9.8 %fusion.56 = bf16[2048,128]{0,1:T(8,128)(2,1)} fusion(f32[128,2048]{1,0:T(8,128)S(1)} %copy-done.23, f32[128,2048]{1,0:T(8,128)S(1)} %copy-done.24, f32[128]{0:T(128)S(1)} %get-tuple-element.25, f32[128]{0:T(128)S(1)} %get-tuple-element.30, f32[128]{0:T(128)S(1)} %get-tuple-element.27, bf16[2048,3072]{1,0:T(8,128)(2,1)} %param.3, ...), kind=kOutput, calls=%fused_computation.118 | convolution fusion | flops 1614020608 | bytes 15992320 | tf_op jit(solution)/shard_map/dot_general | solution.py:29
  432.8 8.1 %collective-permute-done.23 = bf16[2048,128]{0,1:T(8,128)(2,1)S(1)} collective-permute-done((bf16[2048,128]{0,1:T(8,128)(2,1)}, bf16[2048,128]{0,1:T(8,128)(2,1)S(1)}, u32[]{:S(2)}, u32[]{:S(2)}) %collective-permute-start.23) | collective-permute-done | bytes 524320 | tf_op jit(solution)/shard_map/ppermute | solution.py:19
  443.1 6.6 %all-to-all-start.12 = ((f32[64,1,128]{2,1,0:T(1,128)}), f32[64,1,128]{2,1,0:T(1,128)S(1)}, u32[]{:S(2)}, u32[]{:S(2)}) async-start(f32[64,1,128]{2,1,0:T(1,128)} %broadcast_in_dim.20), calls=%async_computation.12 | async-start | bytes 65536 | tf_op jit(solution)/shard_map/all_to_all | solution.py:92
  451.1 6.4 %all-to-all-done.12 = f32[64,1,128]{2,1,0:T(1,128)S(1)} async-done(((f32[64,1,128]{2,1,0:T(1,128)}), f32[64,1,128]{2,1,0:T(1,128)S(1)}, u32[]{:S(2)}, u32[]{:S(2)}) %all-to-all-start.12) | async-done | bytes 32800 | tf_op jit(solution)/shard_map/all_to_all | solution.py:92
  457.6 4.8 %multiply_subtract_fusion = f32[2048,128]{0,1:T(8,128)} fusion(bf16[2048,128]{0,1:T(8,128)(2,1)} %copy.44, bf16[2048,128]{0,1:T(8,128)(2,1)} %copy-done.40, bf16[2048,128]{0,1:T(8,128)(2,1)} %copy-done.41, bf16[2048,128]{0,1:T(8,128)(2,1)S(1)} %copy-done.26, bf16[2048,128]{0,1:T(8,128)(2,1)} %copy-done.42, bf16[2048,128]{0,1:T(8,128)(2,1)} %copy-done.27, ...), kind=kLoop, calls=%fused_computation.73 | loop fusion | flops 8388608 | bytes 8391680 | tf_op jit(solution)/shard_map/sub | solution.py:96
  465.1 6.4 %fusion.33 = f32[3072,2]{1,0:T(8,128)} fusion(f32[3072,128]{1,0:T(8,128)} %get-tuple-element.29, s32[]{:T(128)S(6)} %select_n.96, f32[3072,128]{1,0:T(8,128)} %get-tuple-element.33, f32[3072,128]{1,0:T(8,128)} %fusion.73, f32[3072,128]{1,0:T(8,128)S(1)} %copy-done.10, f32[3072,128]{1,0:T(8,128)S(1)} %copy-done.8, f32[3072,128]{1,0:T(8,128)} %fusion.79, ...), kind=kLoop, calls=%fused_computation.55 | loop fusion | flops 98304 | bytes 208956 | tf_op jit(solution)/shard_map/div | solution.py:108
  (235 shorter events, 88.7 us)
Async XLA Ops:
  8.8 2.8 collective-permute-start
  12.5 18.2 %all-to-all-start = ((bf16[32,48,128]{2,1,0:T(8,128)(2,1)}), bf16[32,48,128]{2,1,0:T(8,128)(2,1)S(1)}, u32[]{:S(2)}, u32[]{:S(2)}) async-start(bf16[32,48,128]{2,1,0:T(8,128)(2,1)} %bitcast.3), calls=%async_computation | async-start | bytes 786432 | tf_op jit(solution)/shard_map/all_to_all | solution.py:41
  43.7 4.1 collective-permute-start.1
  47.9 137.1 %copy-start.4 = (bf16[1536,128]{1,0:T(8,128)(2,1)}, bf16[1536,128]{1,0:T(8,128)(2,1)S(1)}, u32[]{:S(2)}) copy-start(bf16[1536,128]{1,0:T(8,128)(2,1)S(1)} %get-tuple-element.61) | copy-start | bytes 1179652
  57.0 72.7 %copy-start.1 = (f32[128,2048]{1,0:T(8,128)}, f32[128,2048]{1,0:T(8,128)S(1)}, u32[]{:S(2)}) copy-start(f32[128,2048]{1,0:T(8,128)S(1)} %fusion.78) | copy-start | bytes 3145732
  57.1 14.7 %collective-permute-start.3 = (bf16[2048,128]{0,1:T(8,128)(2,1)S(1)}, bf16[2048,128]{0,1:T(8,128)(2,1)S(1)}, u32[]{:S(2)}, u32[]{:S(2)}) collective-permute-start(bf16[2048,128]{0,1:T(8,128)(2,1)S(1)} %convert_bitcast_fusion.3), channel_id=1, source_target_pairs={{0,1},{1,0},{2,3},{3,2},{4,5},{5,4},{6,7},{7,6},{8,9},{9,8},{10,11... | collective-permute-start | bytes 1572872 | tf_op jit(solution)/shard_map/ppermute | solution.py:19
  76.1 2.7 collective-permute-start.4
  78.9 67.3 %slice-start = ((s8[12582912]{0:T(1024)(128)(4,1)}), s8[4194304]{0:T(1024)(128)(4,1)S(1)}, s32[]{:S(2)}) async-start(s8[12582912]{0:T(1024)(128)(4,1)} %bitcast.187), calls=%async_computation.13 | async-start | bytes 8388608
  105.1 4.1 collective-permute-start.5
  109.3 75.7 %copy-start.19 = (bf16[1536,128]{1,0:T(8,128)(2,1)}, bf16[1536,128]{1,0:T(8,128)(2,1)S(1)}, u32[]{:S(2)}) copy-start(bf16[1536,128]{1,0:T(8,128)(2,1)S(1)} %get-tuple-element.58) | copy-start | bytes 1179652
  109.3 75.7 %copy-start.21 = (bf16[1536,128]{1,0:T(8,128)(2,1)}, bf16[1536,128]{1,0:T(8,128)(2,1)S(1)}, u32[]{:S(2)}) copy-start(bf16[1536,128]{1,0:T(8,128)(2,1)S(1)} %get-tuple-element.59) | copy-start | bytes 1179652
  113.4 32.9 %slice-start.1 = ((s8[12582912]{0:T(1024)(128)(4,1)}), s8[4194304]{0:T(1024)(128)(4,1)S(1)}, s32[]{:S(2)}) async-start(s8[12582912]{0:T(1024)(128)(4,1)} %bitcast.187), calls=%async_computation.14 | async-start | bytes 8388608
  113.4 32.9 %slice-start.2 = ((s8[12582912]{0:T(1024)(128)(4,1)}), s8[4194304]{0:T(1024)(128)(4,1)S(1)}, s32[]{:S(2)}) async-start(s8[12582912]{0:T(1024)(128)(4,1)} %bitcast.187), calls=%async_computation.15 | async-start | bytes 8388608
  113.4 13.2 %collective-permute-start.6 = (f32[3,128]{1,0:T(4,128)S(1)}, f32[3,128]{1,0:T(4,128)S(1)}, u32[]{:S(2)}, u32[]{:S(2)}) collective-permute-start(f32[3,128]{1,0:T(4,128)S(1)} %pad_maximum_fusion.6), channel_id=1, source_target_pairs={{0,1},{1,0},{2,3},{3,2},{4,5},{5,4},{6,7},{7,6},{8,9},{9,8},{10,11... | collective-permute-start | bytes 4616 | tf_op jit(solution)/shard_map/ppermute | solution.py:19
  125.8 3.9 collective-permute-start.2
  132.3 13.2 %collective-permute-start.7 = (bf16[2048,128]{0,1:T(8,128)(2,1)S(1)}, bf16[2048,128]{0,1:T(8,128)(2,1)S(1)}, u32[]{:S(2)}, u32[]{:S(2)}) collective-permute-start(bf16[2048,128]{0,1:T(8,128)(2,1)S(1)} %get-tuple-element.45), channel_id=1, source_target_pairs={{0,1},{1,0},{2,3},{3,2},{4,5},{5,4},{6,7},{7,6},{8,9},{9,8},{10,11... | collective-permute-start | bytes 1572872 | tf_op jit(solution)/shard_map/ppermute | solution.py:19
  150.6 4.1 collective-permute-start.8
  180.4 4.5 collective-permute-start.9
  185.1 36.0 %slice-start.3 = ((s8[12582912]{0:T(1024)(128)(4,1)}), s8[4194304]{0:T(1024)(128)(4,1)S(1)}, s32[]{:S(2)}) async-start(s8[12582912]{0:T(1024)(128)(4,1)} %bitcast.189), calls=%async_computation.16 | async-start | bytes 8388608
  190.1 4.0 collective-permute-start.10
  194.1 26.9 %slice-start.4 = ((s8[12582912]{0:T(1024)(128)(4,1)}), s8[4194304]{0:T(1024)(128)(4,1)S(1)}, s32[]{:S(2)}) async-start(s8[12582912]{0:T(1024)(128)(4,1)} %bitcast.189), calls=%async_computation.17 | async-start | bytes 8388608
  206.7 13.5 %collective-permute-start.11 = (bf16[2048,128]{0,1:T(8,128)(2,1)S(1)}, bf16[2048,128]{0,1:T(8,128)(2,1)S(1)}, u32[]{:S(2)}, u32[]{:S(2)}) collective-permute-start(bf16[2048,128]{0,1:T(8,128)(2,1)S(1)} %convert_bitcast_fusion.1), channel_id=1, source_target_pairs={{0,1},{1,0},{2,3},{3,2},{4,5},{5,4},{6,7},{7,6},{8,9},{9,8},{10,11... | collective-permute-start | bytes 1572872 | tf_op jit(solution)/shard_map/ppermute | solution.py:19
  225.3 3.8 collective-permute-start.12
  229.3 30.4 %copy-start.35 = (bf16[1536,128]{1,0:T(8,128)(2,1)S(1)}, bf16[1536,128]{1,0:T(8,128)(2,1)}, u32[]{:S(2)}) copy-start(bf16[1536,128]{1,0:T(8,128)(2,1)} %copy-done.34) | copy-start | bytes 1179652
  255.3 4.3 collective-permute-start.13
  259.6 73.7 %copy-start.14 = (bf16[1536,128]{1,0:T(8,128)(2,1)}, bf16[1536,128]{1,0:T(8,128)(2,1)S(1)}, u32[]{:S(2)}) copy-start(bf16[1536,128]{1,0:T(8,128)(2,1)S(1)} %get-tuple-element.54) | copy-start | bytes 1179652
  259.7 36.1 %slice-start.6 = ((s8[12582912]{0:T(1024)(128)(4,1)}), s8[4194304]{0:T(1024)(128)(4,1)S(1)}, s32[]{:S(2)}) async-start(s8[12582912]{0:T(1024)(128)(4,1)} %bitcast.191), calls=%async_computation.19 | async-start | bytes 8388608
  264.8 68.5 %copy-start.9 = (f32[3072,128]{1,0:T(8,128)}, f32[3072,128]{1,0:T(8,128)S(1)}, u32[]{:S(2)}) copy-start(f32[3072,128]{1,0:T(8,128)S(1)} %get-tuple-element.39) | copy-start | bytes 4718596
  264.8 31.0 %slice-start.7 = ((s8[12582912]{0:T(1024)(128)(4,1)}), s8[4194304]{0:T(1024)(128)(4,1)S(1)}, s32[]{:S(2)}) async-start(s8[12582912]{0:T(1024)(128)(4,1)} %bitcast.191), calls=%async_computation.20 | async-start | bytes 8388608
  264.8 31.0 %slice-start.8 = ((s8[12582912]{0:T(1024)(128)(4,1)}), s8[4194304]{0:T(1024)(128)(4,1)S(1)}, s32[]{:S(2)}) async-start(s8[12582912]{0:T(1024)(128)(4,1)} %bitcast.191), calls=%async_computation.21 | async-start | bytes 8388608
  264.8 12.7 %collective-permute-start.14 = (f32[3,128]{1,0:T(4,128)S(1)}, f32[3,128]{1,0:T(4,128)S(1)}, u32[]{:S(2)}, u32[]{:S(2)}) collective-permute-start(f32[3,128]{1,0:T(4,128)S(1)} %pad_maximum_fusion.8), channel_id=1, source_target_pairs={{0,1},{1,0},{2,3},{3,2},{4,5},{5,4},{6,7},{7,6},{8,9},{9,8},{10,11... | collective-permute-start | bytes 4616 | tf_op jit(solution)/shard_map/ppermute | solution.py:19
  280.6 14.4 %collective-permute-start.15 = (bf16[2048,128]{0,1:T(8,128)(2,1)S(1)}, bf16[2048,128]{0,1:T(8,128)(2,1)S(1)}, u32[]{:S(2)}, u32[]{:S(2)}) collective-permute-start(bf16[2048,128]{0,1:T(8,128)(2,1)S(1)} %get-tuple-element.34), channel_id=1, source_target_pairs={{0,1},{1,0},{2,3},{3,2},{4,5},{5,4},{6,7},{7,6},{8,9},{9,8},{10,11... | collective-permute-start | bytes 1572872 | tf_op jit(solution)/shard_map/ppermute | solution.py:19
  300.1 2.9 collective-permute-start.16
  328.9 4.3 collective-permute-start.17
  333.3 36.0 %slice-start.9 = ((s8[12582912]{0:T(1024)(128)(4,1)}), s8[4194304]{0:T(1024)(128)(4,1)S(1)}, s32[]{:S(2)}) async-start(s8[12582912]{0:T(1024)(128)(4,1)} %bitcast.193), calls=%async_computation.22 | async-start | bytes 8388608
  338.3 4.0 collective-permute-start.18
  342.4 26.9 %slice-start.10 = ((s8[12582912]{0:T(1024)(128)(4,1)}), s8[4194304]{0:T(1024)(128)(4,1)S(1)}, s32[]{:S(2)}) async-start(s8[12582912]{0:T(1024)(128)(4,1)} %bitcast.193), calls=%async_computation.23 | async-start | bytes 8388608
  342.4 26.9 %slice-start.11 = ((s8[12582912]{0:T(1024)(128)(4,1)}), s8[4194304]{0:T(1024)(128)(4,1)S(1)}, s32[]{:S(2)}) async-start(s8[12582912]{0:T(1024)(128)(4,1)} %bitcast.193), calls=%async_computation.24 | async-start | bytes 8388608
  354.9 13.5 %collective-permute-start.19 = (bf16[2048,128]{0,1:T(8,128)(2,1)S(1)}, bf16[2048,128]{0,1:T(8,128)(2,1)S(1)}, u32[]{:S(2)}, u32[]{:S(2)}) collective-permute-start(bf16[2048,128]{0,1:T(8,128)(2,1)S(1)} %fusion.50), channel_id=1, source_target_pairs={{0,1},{1,0},{2,3},{3,2},{4,5},{5,4},{6,7},{7,6},{8,9},{9,8},{10,11... | collective-permute-start | bytes 1572872 | tf_op jit(solution)/shard_map/ppermute | solution.py:19
  373.6 3.8 collective-permute-start.20
  377.4 30.5 %copy-start.37 = (bf16[1536,128]{1,0:T(8,128)(2,1)S(1)}, bf16[1536,128]{1,0:T(8,128)(2,1)}, u32[]{:S(2)}) copy-start(bf16[1536,128]{1,0:T(8,128)(2,1)} %copy-done.36) | copy-start | bytes 1179652
  377.4 30.5 %copy-start.39 = (bf16[1536,128]{1,0:T(8,128)(2,1)S(1)}, bf16[1536,128]{1,0:T(8,128)(2,1)}, u32[]{:S(2)}) copy-start(bf16[1536,128]{1,0:T(8,128)(2,1)} %copy-done.38) | copy-start | bytes 1179652
  377.5 30.4 %copy-start.15 = (bf16[1536,128]{1,0:T(8,128)(2,1)S(1)}, bf16[1536,128]{1,0:T(8,128)(2,1)}, u32[]{:S(2)}) copy-start(bf16[1536,128]{1,0:T(8,128)(2,1)} %copy-done.14) | copy-start | bytes 1179652
  377.5 30.4 %copy-start.18 = (bf16[1536,128]{1,0:T(8,128)(2,1)S(1)}, bf16[1536,128]{1,0:T(8,128)(2,1)}, u32[]{:S(2)}) copy-start(bf16[1536,128]{1,0:T(8,128)(2,1)} %copy-done.16) | copy-start | bytes 1179652
  403.5 4.3 collective-permute-start.21
  413.4 4.0 collective-permute-start.22
  427.3 13.7 %collective-permute-start.23 = (bf16[2048,128]{0,1:T(8,128)(2,1)}, bf16[2048,128]{0,1:T(8,128)(2,1)S(1)}, u32[]{:S(2)}, u32[]{:S(2)}) collective-permute-start(bf16[2048,128]{0,1:T(8,128)(2,1)} %fusion.56), channel_id=1, source_target_pairs={{0,1},{1,0},{2,3},{3,2},{4,5},{5,4},{6,7},{7,6},{8,9},{9,8},{10,11... | collective-permute-start | bytes 1572872 | tf_op jit(solution)/shard_map/ppermute | solution.py:19
  443.1 14.5 %all-to-all-start.12 = ((f32[64,1,128]{2,1,0:T(1,128)}), f32[64,1,128]{2,1,0:T(1,128)S(1)}, u32[]{:S(2)}, u32[]{:S(2)}) async-start(f32[64,1,128]{2,1,0:T(1,128)} %broadcast_in_dim.20), calls=%async_computation.12 | async-start | bytes 65536 | tf_op jit(solution)/shard_map/all_to_all | solution.py:92
  (37 other events, 454.8 us)

commit v2 on v1

v2 whole, which is shorter than its diff:
```python
import jax
import jax.numpy as jnp
from jax import lax
from jax.experimental import pallas as pl
from jax.experimental.pallas import tpu as pltpu
from jax.sharding import Mesh
from jax.sharding import PartitionSpec as P

ITERS = 6
CHIPS = ("rows_0", "rows_1", "rows_2")
CORE = "rows_3"
ROWS = ("rows_0", "rows_1", "rows_2", "rows_3")
COLS = "cols"
BF16 = jnp.bfloat16
F32 = jnp.float32
EXTRA = 16
ROW_BLOCK = 256
COL_BLOCK = 768


def swapped(array, axis):
    return lax.ppermute(array, axis, ((0, 1), (1, 0)))


def settings():
    return pltpu.CompilerParams(
        dimension_semantics=("arbitrary",), vmem_limit_bytes=24 * 1024 * 1024
    )


def price(rows, cols, fits):
    return pl.CostEstimate(
        flops=2 * rows * cols * fits, bytes_accessed=2 * rows * cols, transcendentals=0
    )


def whole(shape):
    return pl.BlockSpec(shape, lambda i, *_: (0,) * len(shape))


def image_step(design, vector, chunk, moved=None, alpha=None):
    rows, width = design.shape[0] // 2, design.shape[1]
    fits = vector.shape[1]
    steps = rows // ROW_BLOCK
    block = pl.BlockSpec((ROW_BLOCK, fits), lambda i: (i, 0))

    def kernel(d, v, *rest):
        product = jnp.dot(d[...], v[...], preferred_element_type=F32)
        if moved is not None:
            u, a, out, short = rest
            product = u[...] - a[...] * product
        else:
            out, short = rest
        out[...] = product
        short[...] = product.astype(BF16)

    in_specs = [
        pl.BlockSpec((ROW_BLOCK, width), lambda i: (chunk * steps + i, 0)),
        whole((width, fits)),
    ]
    args = [design, vector]
    if moved is not None:
        in_specs += [block, whole((1, fits))]
        args += [moved, alpha]
    return pl.pallas_call(
        kernel,
        grid=(steps,),
        in_specs=in_specs,
        out_specs=[block, block],
        out_shape=[
            jax.ShapeDtypeStruct((rows, fits), F32),
            jax.ShapeDtypeStruct((rows, fits), BF16),
        ],
        compiler_params=settings(),
        cost_estimate=price(rows, width, fits),
    )(*args)


def start_back(side, design, vectors):
    rows, width = design.shape
    fits = vectors.shape[1]
    half, block = width // 2, COL_BLOCK // 2
    steps = half // block

    def kernel(s, d, v, out, turned):
        @pl.when(pl.program_id(0) == 0)
        def _():
            turned[...] = v[...].T

        out[...] = jnp.dot(turned[...], d[...], preferred_element_type=F32).T.astype(BF16)

    return pl.pallas_call(
        kernel,
        grid_spec=pltpu.PrefetchScalarGridSpec(
            num_scalar_prefetch=1,
            grid=(steps,),
            in_specs=[
                pl.BlockSpec((rows, block), lambda i, s: (0, s[0] * steps + i)),
                whole((rows, fits)),
            ],
            out_specs=pl.BlockSpec((block, fits), lambda i, s: (i, 0)),
            scratch_shapes=[pltpu.VMEM((fits, rows), BF16)],
        ),
        out_shape=jax.ShapeDtypeStruct((half, fits), BF16),
        compiler_params=settings(),
        cost_estimate=price(rows, half, fits),
    )(side, design, vectors)


def joined(own, other, prior, ratio):
    total = own[...].astype(F32) + other[...].astype(F32)
    if prior is not None:
        total = total + ratio[...] * prior[...]
    return total


def back_first(design, own, other, prior, ratio):
    rows, width = own.shape[0], design.shape[1]
    fits = own.shape[1]
    steps = width // COL_BLOCK
    follow = prior is not None

    def kernel(d, own_ref, other_ref, *rest):
        if follow:
            prior_ref, ratio_ref, out, image, norm, turned = rest
        else:
            prior_ref = ratio_ref = None
            out, image, norm, turned = rest

        @pl.when(pl.program_id(0) == 0)
        def _():
            total = joined(own_ref, other_ref, prior_ref, ratio_ref)
            image[...] = total
            norm[...] = jnp.sum(total * total, axis=0, keepdims=True)
            turned[...] = total.astype(BF16).T

        out[...] = jnp.dot(turned[...], d[...], preferred_element_type=F32).T

    piece = whole((rows, fits))
    in_specs = [pl.BlockSpec((rows, COL_BLOCK), lambda i: (0, i)), piece, piece]
    args = [design, own, other]
    if follow:
        in_specs += [piece, whole((1, fits))]
        args += [prior, ratio]
    return pl.pallas_call(
        kernel,
        grid=(steps,),
        in_specs=in_specs,
        out_specs=[
            pl.BlockSpec((COL_BLOCK, fits), lambda i: (i, 0)),
            piece,
            whole((1, fits)),
        ],
        out_shape=[
            jax.ShapeDtypeStruct((width, fits), F32),
            jax.ShapeDtypeStruct((rows, fits), F32),
            jax.ShapeDtypeStruct((1, fits), F32),
        ],
        scratch_shapes=[pltpu.VMEM((fits, rows), BF16)],
        compiler_params=settings(),
        cost_estimate=price(rows, width, fits),
    )(*args)


def back_given(side, design, own, other, prior, ratio, begun, norm_first):
    rows, width = own.shape[0], design.shape[1]
    fits = own.shape[1]
    half = width // 2
    steps = half // COL_BLOCK
    follow = prior is not None

    def kernel(s, d, own_ref, other_ref, begun_ref, norm_ref, *rest):
        if follow:
            prior_ref, ratio_ref, out, image, turned, norm = rest
        else:
            prior_ref = ratio_ref = None
            out, image, turned, norm = rest

        step = pl.program_id(0)

        @pl.when(step == 0)
        def _():
            total = joined(own_ref, other_ref, prior_ref, ratio_ref)
            image[...] = total
            turned[...] = total.astype(BF16).T
            norms = norm_ref[...] + jnp.sum(total * total, axis=0, keepdims=True)
            norm[...] = norms
            high = norms.astype(BF16).astype(F32)
            middle = (norms - high).astype(BF16).astype(F32)
            low = norms - high - middle
            row = lax.broadcasted_iota(jnp.int32, (EXTRA, fits), 0)
            below = jnp.where(row == 0, high, jnp.where(row == 1, middle, low))
            out[pl.ds(half, EXTRA), :] = jnp.where(row < 3, below, 0.0).astype(BF16)

        product = jnp.dot(turned[...], d[...], preferred_element_type=F32).T
        where = pl.multiple_of(step * COL_BLOCK, COL_BLOCK)
        out[pl.ds(where, COL_BLOCK), :] = (product + begun_ref[...]).astype(BF16)

    piece = whole((rows, fits))
    block = lambda i, s: (s[0] * steps + i, 0)
    in_specs = [
        pl.BlockSpec((rows, COL_BLOCK), lambda i, s: (1, s[0] * steps + i)),
        piece,
        piece,
        pl.BlockSpec((COL_BLOCK, fits), block),
        whole((1, fits)),
    ]
    args = [design, own, other, begun, norm_first]
    if follow:
        in_specs += [piece, whole((1, fits))]
        args += [prior, ratio]
    return pl.pallas_call(
        kernel,
        grid_spec=pltpu.PrefetchScalarGridSpec(
            num_scalar_prefetch=1,
            grid=(steps,),
            in_specs=in_specs,
            out_specs=[
                whole((half + EXTRA, fits)),
                piece,
                whole((fits, rows)),
                whole((1, fits)),
            ],
        ),
        out_shape=[
            jax.ShapeDtypeStruct((half + EXTRA, fits), BF16),
            jax.ShapeDtypeStruct((rows, fits), F32),
            jax.ShapeDtypeStruct((fits, rows), BF16),
            jax.ShapeDtypeStruct((1, fits), F32),
        ],
        compiler_params=settings(),
        cost_estimate=price(rows, half, fits),
    )(side, *args)


def back_kept(side, design, turned, begun):
    fits, rows = turned.shape
    half = design.shape[1] // 2
    steps = half // COL_BLOCK

    def kernel(s, d, t, begun_ref, out):
        product = jnp.dot(t[...], d[...], preferred_element_type=F32).T
        out[...] = product + begun_ref[...]

    block = lambda i, s: (s[0] * steps + i, 0)
    return pl.pallas_call(
        kernel,
        grid_spec=pltpu.PrefetchScalarGridSpec(
            num_scalar_prefetch=1,
            grid=(steps,),
            in_specs=[
                pl.BlockSpec((rows, COL_BLOCK), lambda i, s: (1, s[0] * steps + i)),
                whole((fits, rows)),
                pl.BlockSpec((COL_BLOCK, fits), block),
            ],
            out_specs=pl.BlockSpec((COL_BLOCK, fits), lambda i, s: (i, 0)),
        ),
        out_shape=jax.ShapeDtypeStruct((half, fits), F32),
        compiler_params=settings(),
        cost_estimate=price(rows, half, fits),
    )(side, design, turned, begun)


def exchanged(pieces):
    return lax.all_to_all(pieces, CHIPS, split_axis=0, concat_axis=0, tiled=True)


def whole_half(share, square):
    core = lax.axis_index(CORE)
    chips = lax.axis_size(CHIPS)
    rows, fits = share.shape
    scaled = (share * square).astype(BF16)
    half = exchanged(jnp.broadcast_to(scaled, (chips, rows, fits))).reshape(-1, fits)
    other = swapped(half, CORE)
    low = jnp.where(core == 0, half, other)
    high = jnp.where(core == 0, other, half)
    return jnp.concatenate([low, high], axis=0)


def per_device(design, targets, col_scale):
    core = lax.axis_index(CORE)
    chips = lax.axis_size(CHIPS)
    width, fits = design.shape[1], targets.shape[1]
    depth = targets.shape[0] // 2
    half = width // 2
    mine = core.astype(jnp.int32).reshape(1)
    theirs = 1 - mine
    rows = half // chips
    own = core * chips + lax.axis_index(CHIPS)
    square = lax.dynamic_slice_in_dim(col_scale, own * rows, rows, 0)[:, None]
    square = square * square
    weight = 1.0 / (col_scale * col_scale)[:, None]
    count = fits // lax.axis_size(ROWS)
    first = lax.axis_index(ROWS) * count
    picks = lax.broadcasted_iota(jnp.int32, (count, fits), 1)
    picks = picks == first + lax.broadcasted_iota(jnp.int32, (count, fits), 0)
    picks = picks.astype(BF16)

    def picked(vector):
        return lax.dot_general(
            picks, vector, (((1,), (1,)), ((), ())), preferred_element_type=F32
        )

    def picked_row(values):
        return lax.dynamic_slice_in_dim(values, first, count, 1).reshape(count, 1)

    def weighed(values):
        return jnp.sum(values * values * weight, axis=0, keepdims=True)

    given = start_back(theirs, design, targets)
    arrived = swapped(given, CORE)
    kept = start_back(mine, design, targets)
    both = (kept.astype(F32) + arrived.astype(F32)).astype(BF16)
    share = exchanged(both.reshape(chips, rows, fits)).astype(F32).sum(axis=0)
    back = whole_half(share, square)
    gradient = back.astype(F32)
    narrow = picked(back)
    narrow_dir = narrow
    narrow_fit = jnp.zeros_like(narrow)
    residual = [targets[:depth].astype(F32), targets[depth:].astype(F32)]
    alpha = ratio = gamma = None
    moved, image = [None, None], [None, None]
    for step in range(ITERS):
        moved_first, short_first = image_step(design, back, 0, moved[0], alpha)
        other_first = swapped(short_first, COLS)
        if step:
            gradient = gradient - alpha * back.astype(F32)
        part = weighed(gradient)
        part, later = lax.optimization_barrier((part, back))
        gamma_new = part + swapped(part, COLS)
        moved_second, short_second = image_step(design, later, 1, moved[1], alpha)
        other_second = swapped(short_second, COLS)
        moved = [moved_first, moved_second]
        if step:
            residual = [r - alpha * q for r, q in zip(residual, image)]
            narrow_alpha = picked_row(alpha)
            narrow_fit = narrow_fit + narrow_alpha * narrow_dir
            narrow = narrow - narrow_alpha * picked(back)
            ratio = gamma_new / gamma
            narrow_dir = narrow + picked_row(ratio) * narrow_dir
            (residual, narrow, narrow_fit, narrow_dir, gradient, other_second) = (
                lax.optimization_barrier(
                    (residual, narrow, narrow_fit, narrow_dir, gradient, other_second)
                )
            )
        gamma = gamma_new
        if step + 1 < ITERS:
            begun, image_first, norm = back_first(
                design, short_first, other_first, image[0], ratio
            )
            given, image_second, turned, norm = back_given(
                theirs, design, short_second, other_second, image[1], ratio, begun, norm
            )
            arrived = swapped(given, CORE)
            kept = back_kept(mine, design, turned, begun)
            image = [image_first, image_second]
            both = (kept + arrived[:half].astype(F32)).astype(BF16)
            norms = norm + jnp.sum(arrived[half:].astype(F32), axis=0, keepdims=True)
            high = lax.reduce_precision(norms, 8, 7)
            middle = lax.reduce_precision(norms - high, 8, 7)
            low = norms - high - middle
            below = jnp.concatenate([high, middle, low], axis=0).astype(BF16)
            below = jnp.pad(below, ((0, EXTRA - 3), (0, 0)))
            pieces = jnp.concatenate(
                [
                    both.reshape(chips, rows, fits),
                    jnp.broadcast_to(below, (chips, EXTRA, fits)),
                ],
                axis=1,
            )
            sums = exchanged(pieces).astype(F32).sum(axis=0)
            delta = jnp.sum(sums[rows:], axis=0, keepdims=True)
            alpha = gamma / delta
            back = whole_half(sums[:rows], square)
        else:
            pairs = zip((short_first, short_second), (other_first, other_second), image)
            image = [a.astype(F32) + b.astype(F32) + ratio * q for a, b, q in pairs]
            norm = sum(jnp.sum(q * q, axis=0) for q in image)
            copies = jnp.broadcast_to(norm, (lax.axis_size(ROWS), 1, fits))
            copies = lax.all_to_all(copies, ROWS, split_axis=0, concat_axis=0, tiled=True)
            delta = copies.sum(axis=0)
            alpha = gamma / delta
    residual = [r - alpha * q for r, q in zip(residual, image)]
    narrow_fit = narrow_fit + picked_row(alpha) * narrow_dir
    part = (narrow_fit / col_scale).T
    return part, jnp.concatenate(residual, axis=0)


def solution(mesh):
    split = Mesh(
        mesh.devices.reshape(2, 4, 4, 2, mesh.shape["cols"]),
        ("rows_0", "rows_1", "rows_2", "rows_3", "cols"),
    )
    in_specs = (P(ROWS, "cols"), P(ROWS, None), P("cols"))
    out_specs = (P("cols", ROWS), P(ROWS, None))
    return jax.shard_map(
        per_device, mesh=split, in_specs=in_specs, out_specs=out_specs, check_vma=False
    )
```

time: 484 us -> 441 us (0.911)
  matrix products: 83.3 us -> 2.67 us
  Pallas kernels: 0 us -> 61.3 us
  blocking collectives: 141 us -> 81.1 us
  starting transfers between devices: 66.5 us -> 94.6 us
  local copies, waits for them, and re-layouts: 20 us -> 43.1 us
  other arithmetic: 51.6 us -> 33 us
  waiting for transfers between devices: 110 us -> 115 us
    dot_general x12 -> x6, matrix products: 83.3 us -> 2.67 us  [picked(): lax.dot_general(picks, vector, (((1,), (1,)), ((), ())), preferred_elemen...]
    pallas_call x0 -> x29, Pallas kernels: none -> 61.3 us  [the longest x12 28.7 us: image_step(): pl.pallas_call(kernel, grid=(steps,), in_specs=in_specs, out_specs=[block...]
    all_to_all x11 -> x6, blocking collectives: 141 us -> 81.1 us  [the longest x5 68.1 us: exchanged(): lax.all_to_all(pieces, CHIPS, split_axis=0, concat_axis=0, tiled=True)]
    all_to_all x2 -> x7, waiting for transfers between devices: 15.4 us -> 55 us  [exchanged(): lax.all_to_all(pieces, CHIPS, split_axis=0, concat_axis=0, tiled=True)]
    ppermute x24 -> x30, waiting for transfers between devices: 94.5 us -> 59.7 us  [swapped(): return lax.ppermute(array, axis, ((0, 1), (1, 0)))]
    unnamed x121 -> x134, local copies, waits for them, and re-layouts: 10.7 us -> 38.1 us
    all_to_all x2 -> x7, starting transfers between devices: 15.7 us -> 37 us  [exchanged(): lax.all_to_all(pieces, CHIPS, split_axis=0, concat_axis=0, tiled=True)]
    reduce_sum x13 -> x24, other arithmetic: 26.2 us -> 13.9 us  [the longest x6 11.2 us: weighed(): return jnp.sum(values * values * weight, axis=0, keepdims=True)]
  transfers between devices with their start and end apart: 26 -> 37, of which waited for: 24 -> 29; matrix products, arithmetic and copies ran while one was open for 5% -> 4% of each run, Pallas kernels for 0% -> 8%
where the time goes in v2:
time: 441 us; the launch traced here: 433 us
  waiting for transfers between devices  115 us (26%)
  starting transfers between devices  94.6 us (21%)
  blocking collectives  81.1 us (18%)
  Pallas kernels  61.3 us (14%)
  local copies, waits for them, and re-layouts  43.1 us (10%)
  other arithmetic  33 us (7%)
    all_to_all x5, blocking collectives, exchanged(): lax.all_to_all(pieces, CHIPS, split_axis=0, concat_axis=0, tiled=True)  68.1 us
    ppermute x30, waiting for transfers between devices, swapped(): return lax.ppermute(array, axis, ((0, 1), (1, 0)))  59.7 us
    ppermute x30, starting transfers between devices, swapped(): return lax.ppermute(array, axis, ((0, 1), (1, 0)))  57.6 us
    all_to_all x7, waiting for transfers between devices, exchanged(): lax.all_to_all(pieces, CHIPS, split_axis=0, concat_axis=0, tiled=True)  55 us
    unnamed x134, local copies, waits for them, and re-layouts  38.1 us
    all_to_all x7, starting transfers between devices, exchanged(): lax.all_to_all(pieces, CHIPS, split_axis=0, concat_axis=0, tiled=True)  37 us
    pallas_call x12, Pallas kernels, image_step(): pl.pallas_call(kernel, grid=(steps,), in_specs=in_specs, out_specs=[block...  28.7 us
    all_to_all x1, blocking collectives, per_device(): lax.all_to_all(copies, ROWS, split_axis=0, concat_axis=0, tiled=True)  12.9 us
  transfers between devices with their start and end apart: 37, of which 29 were waited for; matrix products, arithmetic and copies ran while one was open for 4% of the time, Pallas kernels for 8%

profile of v2, /device:TPU:1, one launch (start us, length us, event | category | flops | bytes accessed | tf_op | source)
XLA Modules:
  0.0 432.6 jit_solution(7196790912021274856)
XLA Ops:
  0.6 4.6 %copy-done = bf16[2048,3072]{1,0:T(8,128)(2,1)S(1)} copy-done((bf16[2048,3072]{1,0:T(8,128)(2,1)S(1)}, bf16[2048,3072]{1,0:T(8,128)(2,1)}, u32[]{:S(2)}) %copy-start) | copy-done | bytes 12582936
  6.3 3.3 shard_map.51
  11.0 3.2 shard_map.50
  15.1 9.7 %all-to-all-start = ((bf16[32,48,128]{2,1,0:T(8,128)(2,1)}), bf16[32,48,128]{2,1,0:T(8,128)(2,1)S(1)}, u32[]{:S(2)}, u32[]{:S(2)}) async-start(bf16[32,48,128]{2,1,0:T(8,128)(2,1)} %bitcast.1), calls=%async_computation | async-start | bytes 786432 | tf_op jit(solution)/shard_map/all_to_all | solution.py:265
  24.9 8.6 %all-to-all-done = bf16[32,48,128]{2,1,0:T(8,128)(2,1)S(1)} async-done(((bf16[32,48,128]{2,1,0:T(8,128)(2,1)}), bf16[32,48,128]{2,1,0:T(8,128)(2,1)S(1)}, u32[]{:S(2)}, u32[]{:S(2)}) %all-to-all-start) | async-done | bytes 393248 | tf_op jit(solution)/shard_map/all_to_all | solution.py:265
  33.7 12.6 %all_to_all.65 = bf16[32,48,128]{2,1,0:T(8,128)(2,1)S(1)} all-to-all(bf16[32,48,128]{2,1,0:T(8,128)(2,1)S(1)} %broadcast_in_dim.87), channel_id=1, replica_groups=mesh['rows_0'=2,'rows_1'=4,'rows_2'=4,'rows_3'=2,'cols'=2] {'rows_0','ro..., dimensions={0} | all-to-all | bytes 786432 | tf_op jit(solution)/shard_map/all_to_all | solution.py:265
  46.3 3.4 collective-permute-start.1
  52.2 4.6 %copy-done.2 = bf16[2048,3072]{1,0:T(8,128)(2,1)S(1)} copy-done((bf16[2048,3072]{1,0:T(8,128)(2,1)S(1)}, bf16[2048,3072]{1,0:T(8,128)(2,1)}, u32[]{:S(2)}) %copy-start.2) | copy-done | bytes 12582936
  64.5 3.7 collective-permute-done.4.other_ref
  70.7 3.1 collective-permute-done.3.other_ref
  78.9 4.6 %all-to-all-start.2 = ((bf16[32,64,128]{2,1,0:T(8,128)(2,1)}), bf16[32,64,128]{2,1,0:T(8,128)(2,1)}, u32[]{:S(2)}, u32[]{:S(2)}) async-start(bf16[32,64,128]{2,1,0:T(8,128)(2,1)} %pad_maximum_fusion.7), calls=%async_computation.2 | async-start | bytes 1048576 | tf_op jit(solution)/shard_map/all_to_all | solution.py:265
  83.5 10.2 %all-to-all-done.2 = bf16[32,64,128]{2,1,0:T(8,128)(2,1)} async-done(((bf16[32,64,128]{2,1,0:T(8,128)(2,1)}), bf16[32,64,128]{2,1,0:T(8,128)(2,1)}, u32[]{:S(2)}, u32[]{:S(2)}) %all-to-all-start.2) | async-done | bytes 524320 | tf_op jit(solution)/shard_map/all_to_all | solution.py:265
  95.7 4.8 %all-to-all-start.3 = ((bf16[32,48,128]{2,1,0:T(8,128)(2,1)}), bf16[32,48,128]{2,1,0:T(8,128)(2,1)}, u32[]{:S(2)}, u32[]{:S(2)}) async-start(bf16[32,48,128]{2,1,0:T(8,128)(2,1)} %broadcast_in_dim.92), calls=%async_computation.3 | async-start | bytes 786432 | tf_op jit(solution)/shard_map/all_to_all | solution.py:265
  105.9 3.2 all-to-all-done.3
  109.2 3.1 collective-permute-start.6
  114.9 5.0 %multiply_reduce_fusion.4 = (f32[128]{0:T(128)S(1)}, f32[3072,128]{1,0:T(8,128)}) fusion(f32[3072]{0:T(1024)S(1)} %multiply_divide_fusion, bf16[1536,128]{1,0:T(8,128)(2,1)S(1)} %get-tuple-element.247, bf16[1536,128]{1,0:T(8,128)(2,1)S(1)} %get-tuple-element.246, f32[128]{0:T(128)S(1)} %bitcast.126, bf16[1536,128]{1,0:T(8,128)(2,1)S(1)} %get-tuple-element.249, ...), kind=kLoop, calls=%fused_computation.18 | loop fusion | flops 5111680 | bytes 3159040 | tf_op jit(solution)/shard_map/reduce_sum | solution.py:308
  119.9 4.6 %copy-done.3 = bf16[2048,3072]{1,0:T(8,128)(2,1)S(1)} copy-done((bf16[2048,3072]{1,0:T(8,128)(2,1)S(1)}, bf16[2048,3072]{1,0:T(8,128)(2,1)}, u32[]{:S(2)}) %copy-start.3) | copy-done | bytes 12582936
  137.4 3.8 collective-permute-done.8.other_ref
  148.4 14.4 %all_to_all.66 = bf16[32,64,128]{2,1,0:T(8,128)(2,1)S(1)} all-to-all(bf16[32,64,128]{2,1,0:T(8,128)(2,1)S(1)} %pad_maximum_fusion.8), channel_id=1, replica_groups=mesh['rows_0'=2,'rows_1'=4,'rows_2'=4,'rows_3'=2,'cols'=2] {'rows_0','ro..., dimensions={0} | all-to-all | bytes 1048576 | tf_op jit(solution)/shard_map/all_to_all | solution.py:265
  163.8 4.5 %all-to-all-start.5 = ((bf16[32,48,128]{2,1,0:T(8,128)(2,1)}), bf16[32,48,128]{2,1,0:T(8,128)(2,1)S(1)}, u32[]{:S(2)}, u32[]{:S(2)}) async-start(bf16[32,48,128]{2,1,0:T(8,128)(2,1)} %broadcast_in_dim.97), calls=%async_computation.5 | async-start | bytes 786432 | tf_op jit(solution)/shard_map/all_to_all | solution.py:265
  168.4 8.6 %all-to-all-done.5 = bf16[32,48,128]{2,1,0:T(8,128)(2,1)S(1)} async-done(((bf16[32,48,128]{2,1,0:T(8,128)(2,1)}), bf16[32,48,128]{2,1,0:T(8,128)(2,1)S(1)}, u32[]{:S(2)}, u32[]{:S(2)}) %all-to-all-start.5) | async-done | bytes 393248 | tf_op jit(solution)/shard_map/all_to_all | solution.py:265
  176.9 3.0 collective-permute-start.11
  186.5 4.6 %copy-done.4 = bf16[2048,3072]{1,0:T(8,128)(2,1)S(1)} copy-done((bf16[2048,3072]{1,0:T(8,128)(2,1)S(1)}, bf16[2048,3072]{1,0:T(8,128)(2,1)}, u32[]{:S(2)}) %copy-start.4) | copy-done | bytes 12582936
  200.2 4.6 %collective-permute-done.13.other_ref = bf16[1024,128]{1,0:T(8,128)(2,1)S(1)} collective-permute-done((bf16[1024,128]{1,0:T(8,128)(2,1)S(1)}, bf16[1024,128]{1,0:T(8,128)(2,1)S(1)}, u32[]{:S(2)}, u32[]{:S(2)}) %collective-permute-start.13) | collective-permute-done | bytes 262176 | tf_op jit(solution)/shard_map/ppermute | solution.py:22
  204.9 5.6 %collective-permute-done.14.other_ref = bf16[1024,128]{1,0:T(8,128)(2,1)S(1)} collective-permute-done((bf16[1024,128]{1,0:T(8,128)(2,1)S(1)}, bf16[1024,128]{1,0:T(8,128)(2,1)S(1)}, u32[]{:S(2)}, u32[]{:S(2)}) %collective-permute-start.14) | collective-permute-done | bytes 262176 | tf_op jit(solution)/shard_map/ppermute | solution.py:22
  217.3 13.6 %all_to_all.67 = bf16[32,64,128]{2,1,0:T(8,128)(2,1)S(1)} all-to-all(bf16[32,64,128]{2,1,0:T(8,128)(2,1)S(1)} %pad_maximum_fusion.9), channel_id=1, replica_groups=mesh['rows_0'=2,'rows_1'=4,'rows_2'=4,'rows_3'=2,'cols'=2] {'rows_0','ro..., dimensions={0} | all-to-all | bytes 1048576 | tf_op jit(solution)/shard_map/all_to_all | solution.py:265
  232.0 4.5 %all-to-all-start.7 = ((bf16[32,48,128]{2,1,0:T(8,128)(2,1)}), bf16[32,48,128]{2,1,0:T(8,128)(2,1)S(1)}, u32[]{:S(2)}, u32[]{:S(2)}) async-start(bf16[32,48,128]{2,1,0:T(8,128)(2,1)} %broadcast_in_dim.102), calls=%async_computation.7 | async-start | bytes 786432 | tf_op jit(solution)/shard_map/all_to_all | solution.py:265
  236.5 8.6 %all-to-all-done.7 = bf16[32,48,128]{2,1,0:T(8,128)(2,1)S(1)} async-done(((bf16[32,48,128]{2,1,0:T(8,128)(2,1)}), bf16[32,48,128]{2,1,0:T(8,128)(2,1)S(1)}, u32[]{:S(2)}, u32[]{:S(2)}) %all-to-all-start.7) | async-done | bytes 393248 | tf_op jit(solution)/shard_map/all_to_all | solution.py:265
  245.1 3.0 collective-permute-start.16
  255.4 4.6 %copy-done.5 = bf16[2048,3072]{1,0:T(8,128)(2,1)S(1)} copy-done((bf16[2048,3072]{1,0:T(8,128)(2,1)S(1)}, bf16[2048,3072]{1,0:T(8,128)(2,1)}, u32[]{:S(2)}) %copy-start.5) | copy-done | bytes 12582936
  269.0 4.8 %collective-permute-done.18.other_ref = bf16[1024,128]{1,0:T(8,128)(2,1)S(1)} collective-permute-done((bf16[1024,128]{1,0:T(8,128)(2,1)S(1)}, bf16[1024,128]{1,0:T(8,128)(2,1)S(1)}, u32[]{:S(2)}, u32[]{:S(2)}) %collective-permute-start.18) | collective-permute-done | bytes 262176 | tf_op jit(solution)/shard_map/ppermute | solution.py:22
  273.8 5.6 %collective-permute-done.19.other_ref = bf16[1024,128]{1,0:T(8,128)(2,1)S(1)} collective-permute-done((bf16[1024,128]{1,0:T(8,128)(2,1)S(1)}, bf16[1024,128]{1,0:T(8,128)(2,1)S(1)}, u32[]{:S(2)}, u32[]{:S(2)}) %collective-permute-start.19) | collective-permute-done | bytes 262176 | tf_op jit(solution)/shard_map/ppermute | solution.py:22
  286.3 13.8 %all_to_all.68 = bf16[32,64,128]{2,1,0:T(8,128)(2,1)S(1)} all-to-all(bf16[32,64,128]{2,1,0:T(8,128)(2,1)S(1)} %pad_maximum_fusion.10), channel_id=1, replica_groups=mesh['rows_0'=2,'rows_1'=4,'rows_2'=4,'rows_3'=2,'cols'=2] {'rows_0','ro..., dimensions={0} | all-to-all | bytes 1048576 | tf_op jit(solution)/shard_map/all_to_all | solution.py:265
  301.0 4.5 %all-to-all-start.9 = ((bf16[32,48,128]{2,1,0:T(8,128)(2,1)}), bf16[32,48,128]{2,1,0:T(8,128)(2,1)S(1)}, u32[]{:S(2)}, u32[]{:S(2)}) async-start(bf16[32,48,128]{2,1,0:T(8,128)(2,1)} %broadcast_in_dim.107), calls=%async_computation.9 | async-start | bytes 786432 | tf_op jit(solution)/shard_map/all_to_all | solution.py:265
  305.6 8.6 %all-to-all-done.9 = bf16[32,48,128]{2,1,0:T(8,128)(2,1)S(1)} async-done(((bf16[32,48,128]{2,1,0:T(8,128)(2,1)}), bf16[32,48,128]{2,1,0:T(8,128)(2,1)S(1)}, u32[]{:S(2)}, u32[]{:S(2)}) %all-to-all-start.9) | async-done | bytes 393248 | tf_op jit(solution)/shard_map/all_to_all | solution.py:265
  324.8 4.6 %copy-done.6 = bf16[2048,3072]{1,0:T(8,128)(2,1)S(1)} copy-done((bf16[2048,3072]{1,0:T(8,128)(2,1)S(1)}, bf16[2048,3072]{1,0:T(8,128)(2,1)}, u32[]{:S(2)}) %copy-start.6) | copy-done | bytes 12582936
  338.3 4.8 %collective-permute-done.23.other_ref = bf16[1024,128]{1,0:T(8,128)(2,1)S(1)} collective-permute-done((bf16[1024,128]{1,0:T(8,128)(2,1)S(1)}, bf16[1024,128]{1,0:T(8,128)(2,1)S(1)}, u32[]{:S(2)}, u32[]{:S(2)}) %collective-permute-start.23) | collective-permute-done | bytes 262176 | tf_op jit(solution)/shard_map/ppermute | solution.py:22
  343.2 5.6 %collective-permute-done.24.other_ref = bf16[1024,128]{1,0:T(8,128)(2,1)S(1)} collective-permute-done((bf16[1024,128]{1,0:T(8,128)(2,1)S(1)}, bf16[1024,128]{1,0:T(8,128)(2,1)S(1)}, u32[]{:S(2)}, u32[]{:S(2)}) %collective-permute-start.24) | collective-permute-done | bytes 262176 | tf_op jit(solution)/shard_map/ppermute | solution.py:22
  355.6 13.6 %all_to_all.69 = bf16[32,64,128]{2,1,0:T(8,128)(2,1)S(1)} all-to-all(bf16[32,64,128]{2,1,0:T(8,128)(2,1)S(1)} %pad_maximum_fusion.11), channel_id=1, replica_groups=mesh['rows_0'=2,'rows_1'=4,'rows_2'=4,'rows_3'=2,'cols'=2] {'rows_0','ro..., dimensions={0} | all-to-all | bytes 1048576 | tf_op jit(solution)/shard_map/all_to_all | solution.py:265
  370.3 4.5 %all-to-all-start.11 = ((bf16[32,48,128]{2,1,0:T(8,128)(2,1)}), bf16[32,48,128]{2,1,0:T(8,128)(2,1)S(1)}, u32[]{:S(2)}, u32[]{:S(2)}) async-start(bf16[32,48,128]{2,1,0:T(8,128)(2,1)} %broadcast_in_dim.112), calls=%async_computation.11 | async-start | bytes 786432 | tf_op jit(solution)/shard_map/all_to_all | solution.py:265
  376.1 7.3 %all-to-all-done.11 = bf16[32,48,128]{2,1,0:T(8,128)(2,1)S(1)} async-done(((bf16[32,48,128]{2,1,0:T(8,128)(2,1)}), bf16[32,48,128]{2,1,0:T(8,128)(2,1)S(1)}, u32[]{:S(2)}, u32[]{:S(2)}) %all-to-all-start.11) | async-done | bytes 393248 | tf_op jit(solution)/shard_map/all_to_all | solution.py:265
  383.4 3.0 collective-permute-start.26
  391.5 4.6 %copy-done.7 = bf16[2048,3072]{1,0:T(8,128)(2,1)S(1)} copy-done((bf16[2048,3072]{1,0:T(8,128)(2,1)S(1)}, bf16[2048,3072]{1,0:T(8,128)(2,1)}, u32[]{:S(2)}) %copy-start.7) | copy-done | bytes 12582936
  396.1 3.0 shard_map.78
  399.1 3.0 shard_map.77
  405.3 5.9 %collective-permute-done.28 = bf16[1024,128]{1,0:T(8,128)(2,1)S(1)} collective-permute-done((bf16[1024,128]{1,0:T(8,128)(2,1)S(1)}, bf16[1024,128]{1,0:T(8,128)(2,1)S(1)}, u32[]{:S(2)}, u32[]{:S(2)}) %collective-permute-start.28) | collective-permute-done | bytes 262176 | tf_op jit(solution)/shard_map/ppermute | solution.py:22
  411.3 5.6 %collective-permute-done.29 = bf16[1024,128]{1,0:T(8,128)(2,1)S(1)} collective-permute-done((bf16[1024,128]{1,0:T(8,128)(2,1)S(1)}, bf16[1024,128]{1,0:T(8,128)(2,1)S(1)}, u32[]{:S(2)}, u32[]{:S(2)}) %collective-permute-start.29) | collective-permute-done | bytes 262176 | tf_op jit(solution)/shard_map/ppermute | solution.py:22
  417.2 12.9 %all_to_all.70 = f32[64,1,128]{2,1,0:T(1,128)S(1)} all-to-all(f32[64,1,128]{2,1,0:T(1,128)S(1)} %broadcast_in_dim.114), channel_id=1, replica_groups=mesh['rows_0'=2,'rows_1'=4,'rows_2'=4,'rows_3'=2,'cols'=2] {'rows_0','ro..., dimensions={0} | all-to-all | bytes 65536 | tf_op jit(solution)/shard_map/all_to_all | solution.py:380
  (319 shorter events, 139.2 us)
Async XLA Ops:
  9.5 4.7 %collective-permute-start = (bf16[1536,128]{1,0:T(8,128)(2,1)S(1)}, bf16[1536,128]{1,0:T(8,128)(2,1)S(1)}, u32[]{:S(2)}, u32[]{:S(2)}) collective-permute-start(bf16[1536,128]{1,0:T(8,128)(2,1)S(1)} %shard_map.51), channel_id=1, source_target_pairs={{0,2},{2,0},{1,3},{3,1},{4,6},{6,4},{5,7},{7,5},{8,10},{10,8},{9,1... | collective-permute-start | bytes 1179656 | tf_op jit(solution)/shard_map/ppermute | solution.py:22
  15.1 18.4 %all-to-all-start = ((bf16[32,48,128]{2,1,0:T(8,128)(2,1)}), bf16[32,48,128]{2,1,0:T(8,128)(2,1)S(1)}, u32[]{:S(2)}, u32[]{:S(2)}) async-start(bf16[32,48,128]{2,1,0:T(8,128)(2,1)} %bitcast.1), calls=%async_computation | async-start | bytes 786432 | tf_op jit(solution)/shard_map/all_to_all | solution.py:265
  24.9 138.0 %copy-start.39 = (f32[48]{0:T(128)}, f32[48]{0:T(128)S(1)}, u32[]{:S(2)}) copy-start(f32[48]{0:T(128)S(1)} %dynamic-slice_multiply_fusion) | copy-start | bytes 580
  46.3 4.7 %collective-permute-start.1 = (bf16[1536,128]{1,0:T(8,128)(2,1)S(1)}, bf16[1536,128]{1,0:T(8,128)(2,1)S(1)}, u32[]{:S(2)}, u32[]{:S(2)}) collective-permute-start(bf16[1536,128]{1,0:T(8,128)(2,1)S(1)} %bitcast.139), channel_id=1, source_target_pairs={{0,2},{2,0},{1,3},{3,1},{4,6},{6,4},{5,7},{7,5},{8,10},{10,8},{9,1... | collective-permute-start | bytes 1179656 | tf_op jit(solution)/shard_map/ppermute | solution.py:22
  59.0 9.1 %collective-permute-start.4 = (bf16[1024,128]{1,0:T(8,128)(2,1)S(1)}, bf16[1024,128]{1,0:T(8,128)(2,1)S(1)}, u32[]{:S(2)}, u32[]{:S(2)}) collective-permute-start(bf16[1024,128]{1,0:T(8,128)(2,1)S(1)} %get-tuple-element.107.own_ref), channel_id=1, source_target_pairs={{0,1},{1,0},{2,3},{3,2},{4,5},{5,4},{6,7},{7,6},{8,9},{9,8},{10,11... | collective-permute-start | bytes 786440 | tf_op jit(solution)/shard_map/ppermute | solution.py:22
  63.9 9.9 %collective-permute-start.3 = (bf16[1024,128]{1,0:T(8,128)(2,1)S(1)}, bf16[1024,128]{1,0:T(8,128)(2,1)S(1)}, u32[]{:S(2)}, u32[]{:S(2)}) collective-permute-start(bf16[1024,128]{1,0:T(8,128)(2,1)S(1)} %get-tuple-element.106.own_ref), channel_id=1, source_target_pairs={{0,1},{1,0},{2,3},{3,2},{4,5},{5,4},{6,7},{7,6},{8,9},{9,8},{10,11... | collective-permute-start | bytes 786440 | tf_op jit(solution)/shard_map/ppermute | solution.py:22
  75.2 2.6 collective-permute-start.5
  78.9 14.8 %all-to-all-start.2 = ((bf16[32,64,128]{2,1,0:T(8,128)(2,1)}), bf16[32,64,128]{2,1,0:T(8,128)(2,1)}, u32[]{:S(2)}, u32[]{:S(2)}) async-start(bf16[32,64,128]{2,1,0:T(8,128)(2,1)} %pad_maximum_fusion.7), calls=%async_computation.2 | async-start | bytes 1048576 | tf_op jit(solution)/shard_map/all_to_all | solution.py:265
  83.5 52.9 %copy-start.47 = (s32[2]{0:T(128)}, s32[2]{0:T(128)S(1)}, u32[]{:S(2)}) copy-start(s32[2]{0:T(128)S(1)} %iota_add_fusion) | copy-start | bytes 28
  95.7 13.4 %all-to-all-start.3 = ((bf16[32,48,128]{2,1,0:T(8,128)(2,1)}), bf16[32,48,128]{2,1,0:T(8,128)(2,1)}, u32[]{:S(2)}, u32[]{:S(2)}) async-start(bf16[32,48,128]{2,1,0:T(8,128)(2,1)} %broadcast_in_dim.92), calls=%async_computation.3 | async-start | bytes 786432 | tf_op jit(solution)/shard_map/all_to_all | solution.py:265
  100.9 5.0 %collective-permute-start.2 = (f32[1,128]{1,0:T(1,128)S(1)}, f32[1,128]{1,0:T(1,128)S(1)}, u32[]{:S(2)}, u32[]{:S(2)}) collective-permute-start(f32[1,128]{1,0:T(1,128)S(1)} %bitcast.158), channel_id=1, source_target_pairs={{0,1},{1,0},{2,3},{3,2},{4,5},{5,4},{6,7},{7,6},{8,9},{9,8},{10,11... | collective-permute-start | bytes 1544 | tf_op jit(solution)/shard_map/ppermute | solution.py:22
  109.2 4.7 %collective-permute-start.6 = (bf16[1536,128]{1,0:T(8,128)(2,1)}, bf16[1536,128]{1,0:T(8,128)(2,1)S(1)}, u32[]{:S(2)}, u32[]{:S(2)}) collective-permute-start(bf16[1536,128]{1,0:T(8,128)(2,1)} %bitcast.9), channel_id=1, source_target_pairs={{0,2},{2,0},{1,3},{3,1},{4,6},{6,4},{5,7},{7,5},{8,10},{10,8},{9,1... | collective-permute-start | bytes 1179656 | tf_op jit(solution)/shard_map/ppermute | solution.py:22
  126.7 14.4 %collective-permute-start.9 = (bf16[1024,128]{1,0:T(8,128)(2,1)S(1)}, bf16[1024,128]{1,0:T(8,128)(2,1)S(1)}, u32[]{:S(2)}, u32[]{:S(2)}) collective-permute-start(bf16[1024,128]{1,0:T(8,128)(2,1)S(1)} %get-tuple-element.122.own_ref), channel_id=1, source_target_pairs={{0,1},{1,0},{2,3},{3,2},{4,5},{5,4},{6,7},{7,6},{8,9},{9,8},{10,11... | collective-permute-start | bytes 786440 | tf_op jit(solution)/shard_map/ppermute | solution.py:22
  129.3 6.5 %collective-permute-start.7 = (f32[1,128]{1,0:T(1,128)S(1)}, f32[1,128]{1,0:T(1,128)S(1)}, u32[]{:S(2)}, u32[]{:S(2)}) collective-permute-start(f32[1,128]{1,0:T(1,128)S(1)} %bitcast.156), channel_id=1, source_target_pairs={{0,1},{1,0},{2,3},{3,2},{4,5},{5,4},{6,7},{7,6},{8,9},{9,8},{10,11... | collective-permute-start | bytes 1544 | tf_op jit(solution)/shard_map/ppermute | solution.py:22
  132.1 9.1 %collective-permute-start.8 = (bf16[1024,128]{1,0:T(8,128)(2,1)S(1)}, bf16[1024,128]{1,0:T(8,128)(2,1)S(1)}, u32[]{:S(2)}, u32[]{:S(2)}) collective-permute-start(bf16[1024,128]{1,0:T(8,128)(2,1)S(1)} %get-tuple-element.118.own_ref), channel_id=1, source_target_pairs={{0,1},{1,0},{2,3},{3,2},{4,5},{5,4},{6,7},{7,6},{8,9},{9,8},{10,11... | collective-permute-start | bytes 786440 | tf_op jit(solution)/shard_map/ppermute | solution.py:22
  145.2 2.9 collective-permute-start.10
  148.4 31.6 %copy-start.22 = (f32[1024,128]{1,0:T(8,128)S(1)}, f32[1024,128]{1,0:T(8,128)}, u32[]{:S(2)}) copy-start(f32[1024,128]{1,0:T(8,128)} %get-tuple-element.129) | copy-start | bytes 1572868
  148.4 31.6 %copy-start.23 = (f32[1024,128]{1,0:T(8,128)S(1)}, f32[1024,128]{1,0:T(8,128)}, u32[]{:S(2)}) copy-start(f32[1024,128]{1,0:T(8,128)} %get-tuple-element.119) | copy-start | bytes 1572868
  163.8 13.1 %all-to-all-start.5 = ((bf16[32,48,128]{2,1,0:T(8,128)(2,1)}), bf16[32,48,128]{2,1,0:T(8,128)(2,1)S(1)}, u32[]{:S(2)}, u32[]{:S(2)}) async-start(bf16[32,48,128]{2,1,0:T(8,128)(2,1)} %broadcast_in_dim.97), calls=%async_computation.5 | async-start | bytes 786432 | tf_op jit(solution)/shard_map/all_to_all | solution.py:265
  176.9 4.3 collective-permute-start.11
  184.4 14.5 %collective-permute-start.12 = (f32[1,128]{1,0:T(1,128)S(1)}, f32[1,128]{1,0:T(1,128)S(1)}, u32[]{:S(2)}, u32[]{:S(2)}) collective-permute-start(f32[1,128]{1,0:T(1,128)S(1)} %bitcast.150), channel_id=1, source_target_pairs={{0,1},{1,0},{2,3},{3,2},{4,5},{5,4},{6,7},{7,6},{8,9},{9,8},{10,11... | collective-permute-start | bytes 1544 | tf_op jit(solution)/shard_map/ppermute | solution.py:22
  193.4 19.7 %slice-start.6 = ((s8[12582912]{0:T(1024)(128)(4,1)}), s8[4194304]{0:T(1024)(128)(4,1)S(1)}, s32[]{:S(2)}) async-start(s8[12582912]{0:T(1024)(128)(4,1)} %bitcast.119), calls=%async_computation.19 | async-start | bytes 8388608
  195.7 9.2 %collective-permute-start.13 = (bf16[1024,128]{1,0:T(8,128)(2,1)S(1)}, bf16[1024,128]{1,0:T(8,128)(2,1)S(1)}, u32[]{:S(2)}, u32[]{:S(2)}) collective-permute-start(bf16[1024,128]{1,0:T(8,128)(2,1)S(1)} %get-tuple-element.138.own_ref), channel_id=1, source_target_pairs={{0,1},{1,0},{2,3},{3,2},{4,5},{5,4},{6,7},{7,6},{8,9},{9,8},{10,11... | collective-permute-start | bytes 786440 | tf_op jit(solution)/shard_map/ppermute | solution.py:22
  196.7 13.8 %collective-permute-start.14 = (bf16[1024,128]{1,0:T(8,128)(2,1)S(1)}, bf16[1024,128]{1,0:T(8,128)(2,1)S(1)}, u32[]{:S(2)}, u32[]{:S(2)}) collective-permute-start(bf16[1024,128]{1,0:T(8,128)(2,1)S(1)} %get-tuple-element.142.own_ref), channel_id=1, source_target_pairs={{0,1},{1,0},{2,3},{3,2},{4,5},{5,4},{6,7},{7,6},{8,9},{9,8},{10,11... | collective-permute-start | bytes 786440 | tf_op jit(solution)/shard_map/ppermute | solution.py:22
  214.5 2.6 collective-permute-start.15
  232.0 13.1 %all-to-all-start.7 = ((bf16[32,48,128]{2,1,0:T(8,128)(2,1)}), bf16[32,48,128]{2,1,0:T(8,128)(2,1)S(1)}, u32[]{:S(2)}, u32[]{:S(2)}) async-start(bf16[32,48,128]{2,1,0:T(8,128)(2,1)} %broadcast_in_dim.102), calls=%async_computation.7 | async-start | bytes 786432 | tf_op jit(solution)/shard_map/all_to_all | solution.py:265
  245.1 5.4 %collective-permute-start.16 = (bf16[1536,128]{1,0:T(8,128)(2,1)S(1)}, bf16[1536,128]{1,0:T(8,128)(2,1)S(1)}, u32[]{:S(2)}, u32[]{:S(2)}) collective-permute-start(bf16[1536,128]{1,0:T(8,128)(2,1)S(1)} %bitcast.137), channel_id=1, source_target_pairs={{0,2},{2,0},{1,3},{3,1},{4,6},{6,4},{5,7},{7,5},{8,10},{10,8},{9,1... | collective-permute-start | bytes 1179656 | tf_op jit(solution)/shard_map/ppermute | solution.py:22
  253.8 13.9 %collective-permute-start.17 = (f32[1,128]{1,0:T(1,128)S(1)}, f32[1,128]{1,0:T(1,128)S(1)}, u32[]{:S(2)}, u32[]{:S(2)}) collective-permute-start(f32[1,128]{1,0:T(1,128)S(1)} %bitcast.152), channel_id=1, source_target_pairs={{0,1},{1,0},{2,3},{3,2},{4,5},{5,4},{6,7},{7,6},{8,9},{9,8},{10,11... | collective-permute-start | bytes 1544 | tf_op jit(solution)/shard_map/ppermute | solution.py:22
  262.3 19.7 %slice-start.9 = ((s8[12582912]{0:T(1024)(128)(4,1)}), s8[4194304]{0:T(1024)(128)(4,1)S(1)}, s32[]{:S(2)}) async-start(s8[12582912]{0:T(1024)(128)(4,1)} %bitcast.121), calls=%async_computation.22 | async-start | bytes 8388608
  262.3 19.7 %slice-start.10 = ((s8[12582912]{0:T(1024)(128)(4,1)}), s8[4194304]{0:T(1024)(128)(4,1)S(1)}, s32[]{:S(2)}) async-start(s8[12582912]{0:T(1024)(128)(4,1)} %bitcast.121), calls=%async_computation.23 | async-start | bytes 8388608
  264.6 9.2 %collective-permute-start.18 = (bf16[1024,128]{1,0:T(8,128)(2,1)S(1)}, bf16[1024,128]{1,0:T(8,128)(2,1)S(1)}, u32[]{:S(2)}, u32[]{:S(2)}) collective-permute-start(bf16[1024,128]{1,0:T(8,128)(2,1)S(1)} %get-tuple-element.158.own_ref), channel_id=1, source_target_pairs={{0,1},{1,0},{2,3},{3,2},{4,5},{5,4},{6,7},{7,6},{8,9},{9,8},{10,11... | collective-permute-start | bytes 786440 | tf_op jit(solution)/shard_map/ppermute | solution.py:22
  266.1 13.3 %collective-permute-start.19 = (bf16[1024,128]{1,0:T(8,128)(2,1)S(1)}, bf16[1024,128]{1,0:T(8,128)(2,1)S(1)}, u32[]{:S(2)}, u32[]{:S(2)}) collective-permute-start(bf16[1024,128]{1,0:T(8,128)(2,1)S(1)} %get-tuple-element.162.own_ref), channel_id=1, source_target_pairs={{0,1},{1,0},{2,3},{3,2},{4,5},{5,4},{6,7},{7,6},{8,9},{9,8},{10,11... | collective-permute-start | bytes 786440 | tf_op jit(solution)/shard_map/ppermute | solution.py:22
  283.5 2.6 collective-permute-start.20
  286.3 30.9 %copy-start.21 = (f32[1024,128]{1,0:T(8,128)S(1)}, f32[1024,128]{1,0:T(8,128)}, u32[]{:S(2)}) copy-start(f32[1024,128]{1,0:T(8,128)} %get-tuple-element.169) | copy-start | bytes 1572868
  301.0 13.1 %all-to-all-start.9 = ((bf16[32,48,128]{2,1,0:T(8,128)(2,1)}), bf16[32,48,128]{2,1,0:T(8,128)(2,1)S(1)}, u32[]{:S(2)}, u32[]{:S(2)}) async-start(bf16[32,48,128]{2,1,0:T(8,128)(2,1)} %broadcast_in_dim.107), calls=%async_computation.9 | async-start | bytes 786432 | tf_op jit(solution)/shard_map/all_to_all | solution.py:265
  314.1 5.0 %collective-permute-start.21 = (bf16[1536,128]{1,0:T(8,128)(2,1)S(1)}, bf16[1536,128]{1,0:T(8,128)(2,1)S(1)}, u32[]{:S(2)}, u32[]{:S(2)}) collective-permute-start(bf16[1536,128]{1,0:T(8,128)(2,1)S(1)} %bitcast.138), channel_id=1, source_target_pairs={{0,2},{2,0},{1,3},{3,1},{4,6},{6,4},{5,7},{7,5},{8,10},{10,8},{9,1... | collective-permute-start | bytes 1179656 | tf_op jit(solution)/shard_map/ppermute | solution.py:22
  322.5 14.6 %collective-permute-start.22 = (f32[1,128]{1,0:T(1,128)S(1)}, f32[1,128]{1,0:T(1,128)S(1)}, u32[]{:S(2)}, u32[]{:S(2)}) collective-permute-start(f32[1,128]{1,0:T(1,128)S(1)} %bitcast.154), channel_id=1, source_target_pairs={{0,1},{1,0},{2,3},{3,2},{4,5},{5,4},{6,7},{7,6},{8,9},{9,8},{10,11... | collective-permute-start | bytes 1544 | tf_op jit(solution)/shard_map/ppermute | solution.py:22
  331.7 19.7 %slice-start.12 = ((s8[12582912]{0:T(1024)(128)(4,1)}), s8[4194304]{0:T(1024)(128)(4,1)S(1)}, s32[]{:S(2)}) async-start(s8[12582912]{0:T(1024)(128)(4,1)} %bitcast.123), calls=%async_computation.25 | async-start | bytes 8388608
  334.0 9.2 %collective-permute-start.23 = (bf16[1024,128]{1,0:T(8,128)(2,1)S(1)}, bf16[1024,128]{1,0:T(8,128)(2,1)S(1)}, u32[]{:S(2)}, u32[]{:S(2)}) collective-permute-start(bf16[1024,128]{1,0:T(8,128)(2,1)S(1)} %get-tuple-element.178.own_ref), channel_id=1, source_target_pairs={{0,1},{1,0},{2,3},{3,2},{4,5},{5,4},{6,7},{7,6},{8,9},{9,8},{10,11... | collective-permute-start | bytes 786440 | tf_op jit(solution)/shard_map/ppermute | solution.py:22
  335.0 13.8 %collective-permute-start.24 = (bf16[1024,128]{1,0:T(8,128)(2,1)S(1)}, bf16[1024,128]{1,0:T(8,128)(2,1)S(1)}, u32[]{:S(2)}, u32[]{:S(2)}) collective-permute-start(bf16[1024,128]{1,0:T(8,128)(2,1)S(1)} %get-tuple-element.182.own_ref), channel_id=1, source_target_pairs={{0,1},{1,0},{2,3},{3,2},{4,5},{5,4},{6,7},{7,6},{8,9},{9,8},{10,11... | collective-permute-start | bytes 786440 | tf_op jit(solution)/shard_map/ppermute | solution.py:22
  352.8 2.6 collective-permute-start.25
  370.3 13.1 %all-to-all-start.11 = ((bf16[32,48,128]{2,1,0:T(8,128)(2,1)}), bf16[32,48,128]{2,1,0:T(8,128)(2,1)S(1)}, u32[]{:S(2)}, u32[]{:S(2)}) async-start(bf16[32,48,128]{2,1,0:T(8,128)(2,1)} %broadcast_in_dim.112), calls=%async_computation.11 | async-start | bytes 786432 | tf_op jit(solution)/shard_map/all_to_all | solution.py:265
  383.4 4.3 collective-permute-start.26
  389.9 15.3 %collective-permute-start.27 = (f32[1,128]{1,0:T(1,128)S(1)}, f32[1,128]{1,0:T(1,128)S(1)}, u32[]{:S(2)}, u32[]{:S(2)}) collective-permute-start(f32[1,128]{1,0:T(1,128)S(1)} %bitcast.148), channel_id=1, source_target_pairs={{0,1},{1,0},{2,3},{3,2},{4,5},{5,4},{6,7},{7,6},{8,9},{9,8},{10,11... | collective-permute-start | bytes 1544 | tf_op jit(solution)/shard_map/ppermute | solution.py:22
  402.2 28.0 %copy-start.18 = (f32[1024,128]{1,0:T(8,128)S(1)}, f32[1024,128]{1,0:T(8,128)}, u32[]{:S(2)}) copy-start(f32[1024,128]{1,0:T(8,128)} %get-tuple-element.205) | copy-start | bytes 1572868
  402.2 28.0 %copy-start.19 = (f32[1024,128]{1,0:T(8,128)S(1)}, f32[1024,128]{1,0:T(8,128)}, u32[]{:S(2)}) copy-start(f32[1024,128]{1,0:T(8,128)} %get-tuple-element.204) | copy-start | bytes 1572868
  402.2 9.1 %collective-permute-start.28 = (bf16[1024,128]{1,0:T(8,128)(2,1)S(1)}, bf16[1024,128]{1,0:T(8,128)(2,1)S(1)}, u32[]{:S(2)}, u32[]{:S(2)}) collective-permute-start(bf16[1024,128]{1,0:T(8,128)(2,1)S(1)} %get-tuple-element.198), channel_id=1, source_target_pairs={{0,1},{1,0},{2,3},{3,2},{4,5},{5,4},{6,7},{7,6},{8,9},{9,8},{10,11... | collective-permute-start | bytes 786440 | tf_op jit(solution)/shard_map/ppermute | solution.py:22
  403.5 13.4 %collective-permute-start.29 = (bf16[1024,128]{1,0:T(8,128)(2,1)S(1)}, bf16[1024,128]{1,0:T(8,128)(2,1)S(1)}, u32[]{:S(2)}, u32[]{:S(2)}) collective-permute-start(bf16[1024,128]{1,0:T(8,128)(2,1)S(1)} %get-tuple-element.201), channel_id=1, source_target_pairs={{0,1},{1,0},{2,3},{3,2},{4,5},{5,4},{6,7},{7,6},{8,9},{9,8},{10,11... | collective-permute-start | bytes 786440 | tf_op jit(solution)/shard_map/ppermute | solution.py:22
  (56 other events, 399.8 us)

commit v3 on v2

v3 whole, which is shorter than its diff:
```python
import jax
import jax.numpy as jnp
from jax import lax
from jax.experimental import pallas as pl
from jax.experimental.pallas import tpu as pltpu
from jax.sharding import Mesh
from jax.sharding import PartitionSpec as P

ITERS = 6
CHIPS = ("rows_0", "rows_1", "rows_2")
CORE = "rows_3"
ROWS = ("rows_0", "rows_1", "rows_2", "rows_3")
COLS = "cols"
BF16 = jnp.bfloat16
F32 = jnp.float32
EXTRA = 16
ROW_BLOCK = 128
COL_BLOCK = 512
VMEM = 48 * 1024 * 1024


def swapped(array, axis):
    return lax.ppermute(array, axis, ((0, 1), (1, 0)))


def settings():
    return pltpu.CompilerParams(vmem_limit_bytes=VMEM)


def price(rows, cols, fits):
    return pl.CostEstimate(
        flops=2 * rows * cols * fits, bytes_accessed=2 * rows * cols, transcendentals=0
    )


ANYWHERE = pl.BlockSpec(memory_space=pltpu.HBM)
NEAR = pl.BlockSpec(memory_space=pltpu.VMEM)
SCALAR = pl.BlockSpec(memory_space=pltpu.SMEM)


def called(kernel, ins, specs, outs, held, steps, cost, extra=()):
    return pl.pallas_call(
        kernel,
        in_specs=specs,
        out_specs=[NEAR] * len(outs),
        out_shape=[jax.ShapeDtypeStruct(shape, dtype) for shape, dtype in outs],
        scratch_shapes=[
            pltpu.VMEM(held, BF16),
            pltpu.SemaphoreType.DMA((steps,)),
            *extra,
        ],
        compiler_params=settings(),
        cost_estimate=cost,
    )(*ins)


def started(fetch, steps):
    @pl.loop(0, steps)
    def _(i):
        fetch(i).start()


def image_step(design, vector, chunk, moved=None, alpha=None):
    rows, width = design.shape[0] // 2, design.shape[1]
    fits = vector.shape[1]
    steps = rows // ROW_BLOCK

    def kernel(d, v, *rest):
        if moved is not None:
            u, a, out, short, held, sems = rest
        else:
            out, short, held, sems = rest

        def fetch(i):
            return pltpu.make_async_copy(
                d.at[pl.ds(chunk * rows + i * ROW_BLOCK, ROW_BLOCK), :],
                held.at[i],
                sems.at[i],
            )

        started(fetch, steps)

        @pl.loop(0, steps)
        def _(i):
            fetch(i).wait()
            where = pl.ds(pl.multiple_of(i * ROW_BLOCK, ROW_BLOCK), ROW_BLOCK)
            product = jnp.dot(held[i], v[...], preferred_element_type=F32)
            if moved is not None:
                product = u[where, :] - a[...] * product
            out[where, :] = product
            short[where, :] = product.astype(BF16)

    args, specs = [design, vector], [ANYWHERE, NEAR]
    if moved is not None:
        args, specs = args + [moved, alpha], specs + [NEAR, NEAR]
    return called(
        kernel,
        args,
        specs,
        [((rows, fits), F32), ((rows, fits), BF16)],
        (steps, ROW_BLOCK, width),
        steps,
        price(rows, width, fits),
    )


def fetcher(d, held, sems, first_row, rows, first_col, block):
    def fetch(i):
        return pltpu.make_async_copy(
            d.at[
                pl.ds(first_row, rows),
                pl.ds(pl.multiple_of(first_col + i * block, block), block),
            ],
            held.at[i],
            sems.at[i],
        )

    return fetch


def start_back(side, design, vectors):
    rows, width = design.shape
    fits = vectors.shape[1]
    half, block = width // 2, COL_BLOCK // 2
    steps = half // block

    def kernel(s, d, v, out, held, sems, turned):
        fetch = fetcher(d, held, sems, 0, rows, s[0] * half, block)
        started(fetch, steps)
        turned[...] = v[...].T

        @pl.loop(0, steps)
        def _(i):
            fetch(i).wait()
            product = jnp.dot(turned[...], held[i], preferred_element_type=F32)
            out[pl.ds(pl.multiple_of(i * block, block), block), :] = product.T.astype(BF16)

    return called(
        kernel,
        [side, design, vectors],
        [SCALAR, ANYWHERE, NEAR],
        [((half, fits), BF16)],
        (steps, rows, block),
        steps,
        price(rows, half, fits),
        [pltpu.VMEM((fits, rows), BF16)],
    )[0]


def joined(own, other, prior, ratio):
    total = own[...].astype(F32) + other[...].astype(F32)
    if prior is not None:
        total = total + ratio[...] * prior[...]
    return total


def back_first(design, own, other, prior, ratio):
    rows, width = own.shape[0], design.shape[1]
    fits = own.shape[1]
    steps = width // COL_BLOCK
    follow = prior is not None

    def kernel(d, own_ref, other_ref, *rest):
        prior_ref = ratio_ref = None
        if follow:
            prior_ref, ratio_ref, *rest = rest
        out, image, norm, held, sems, turned = rest
        fetch = fetcher(d, held, sems, 0, rows, 0, COL_BLOCK)
        started(fetch, steps)
        total = joined(own_ref, other_ref, prior_ref, ratio_ref)
        image[...] = total
        norm[...] = jnp.sum(total * total, axis=0, keepdims=True)
        turned[...] = total.astype(BF16).T

        @pl.loop(0, steps)
        def _(i):
            fetch(i).wait()
            product = jnp.dot(turned[...], held[i], preferred_element_type=F32)
            out[pl.ds(pl.multiple_of(i * COL_BLOCK, COL_BLOCK), COL_BLOCK), :] = product.T

    args, specs = [design, own, other], [ANYWHERE, NEAR, NEAR]
    if follow:
        args, specs = args + [prior, ratio], specs + [NEAR, NEAR]
    return called(
        kernel,
        args,
        specs,
        [((width, fits), F32), ((rows, fits), F32), ((1, fits), F32)],
        (steps, rows, COL_BLOCK),
        steps,
        price(rows, width, fits),
        [pltpu.VMEM((fits, rows), BF16)],
    )


def back_given(side, design, own, other, prior, ratio, begun, norm_first):
    rows, width = own.shape[0], design.shape[1]
    fits = own.shape[1]
    half = width // 2
    steps = half // COL_BLOCK
    follow = prior is not None

    def kernel(s, d, own_ref, other_ref, begun_ref, norm_ref, *rest):
        prior_ref = ratio_ref = None
        if follow:
            prior_ref, ratio_ref, *rest = rest
        out, image, turned, norm, held, sems = rest
        fetch = fetcher(d, held, sems, rows, rows, s[0] * half, COL_BLOCK)
        started(fetch, steps)
        total = joined(own_ref, other_ref, prior_ref, ratio_ref)
        image[...] = total
        turned[...] = total.astype(BF16).T
        norms = norm_ref[...] + jnp.sum(total * total, axis=0, keepdims=True)
        norm[...] = norms
        high = norms.astype(BF16).astype(F32)
        middle = (norms - high).astype(BF16).astype(F32)
        low = norms - high - middle
        row = lax.broadcasted_iota(jnp.int32, (EXTRA, fits), 0)
        below = jnp.where(row == 0, high, jnp.where(row == 1, middle, low))
        out[pl.ds(half, EXTRA), :] = jnp.where(row < 3, below, 0.0).astype(BF16)

        @pl.loop(0, steps)
        def _(i):
            fetch(i).wait()
            where = pl.multiple_of(s[0] * half + i * COL_BLOCK, COL_BLOCK)
            product = jnp.dot(turned[...], held[i], preferred_element_type=F32).T
            product = product + begun_ref[pl.ds(where, COL_BLOCK), :]
            out[pl.ds(pl.multiple_of(i * COL_BLOCK, COL_BLOCK), COL_BLOCK), :] = product.astype(BF16)

    args = [side, design, own, other, begun, norm_first]
    specs = [SCALAR, ANYWHERE, NEAR, NEAR, NEAR, NEAR]
    if follow:
        args, specs = args + [prior, ratio], specs + [NEAR, NEAR]
    return called(
        kernel,
        args,
        specs,
        [
            ((half + EXTRA, fits), BF16),
            ((rows, fits), F32),
            ((fits, rows), BF16),
            ((1, fits), F32),
        ],
        (steps, rows, COL_BLOCK),
        steps,
        price(rows, half, fits),
    )


def back_kept(side, design, turned, begun):
    fits, rows = turned.shape
    half = design.shape[1] // 2
    steps = half // COL_BLOCK

    def kernel(s, d, t, begun_ref, out, held, sems):
        fetch = fetcher(d, held, sems, rows, rows, s[0] * half, COL_BLOCK)
        started(fetch, steps)

        @pl.loop(0, steps)
        def _(i):
            fetch(i).wait()
            where = pl.multiple_of(s[0] * half + i * COL_BLOCK, COL_BLOCK)
            product = jnp.dot(t[...], held[i], preferred_element_type=F32).T
            product = product + begun_ref[pl.ds(where, COL_BLOCK), :]
            out[pl.ds(pl.multiple_of(i * COL_BLOCK, COL_BLOCK), COL_BLOCK), :] = product

    return called(
        kernel,
        [side, design, turned, begun],
        [SCALAR, ANYWHERE, NEAR, NEAR],
        [((half, fits), F32)],
        (steps, rows, COL_BLOCK),
        steps,
        price(rows, half, fits),
    )[0]


def exchanged(pieces):
    return lax.all_to_all(pieces, CHIPS, split_axis=0, concat_axis=0, tiled=True)


def whole_half(share, square):
    core = lax.axis_index(CORE)
    chips = lax.axis_size(CHIPS)
    rows, fits = share.shape
    scaled = (share * square).astype(BF16)
    half = exchanged(jnp.broadcast_to(scaled, (chips, rows, fits))).reshape(-1, fits)
    other = swapped(half, CORE)
    low = jnp.where(core == 0, half, other)
    high = jnp.where(core == 0, other, half)
    return jnp.concatenate([low, high], axis=0)


def per_device(design, targets, col_scale):
    core = lax.axis_index(CORE)
    chips = lax.axis_size(CHIPS)
    width, fits = design.shape[1], targets.shape[1]
    depth = targets.shape[0] // 2
    half = width // 2
    mine = core.astype(jnp.int32).reshape(1)
    theirs = 1 - mine
    rows = half // chips
    own = core * chips + lax.axis_index(CHIPS)
    square = lax.dynamic_slice_in_dim(col_scale, own * rows, rows, 0)[:, None]
    square = square * square
    weight = 1.0 / (col_scale * col_scale)[:, None]
    count = fits // lax.axis_size(ROWS)
    first = lax.axis_index(ROWS) * count
    picks = lax.broadcasted_iota(jnp.int32, (count, fits), 1)
    picks = picks == first + lax.broadcasted_iota(jnp.int32, (count, fits), 0)
    picks = picks.astype(BF16)

    def picked(vector):
        return lax.dot_general(
            picks, vector, (((1,), (1,)), ((), ())), preferred_element_type=F32
        )

    def picked_row(values):
        return lax.dynamic_slice_in_dim(values, first, count, 1).reshape(count, 1)

    def weighed(values):
        return jnp.sum(values * values * weight, axis=0, keepdims=True)

    given = start_back(theirs, design, targets)
    arrived = swapped(given, CORE)
    kept = start_back(mine, design, targets)
    both = (kept.astype(F32) + arrived.astype(F32)).astype(BF16)
    share = exchanged(both.reshape(chips, rows, fits)).astype(F32).sum(axis=0)
    back = whole_half(share, square)
    gradient = back.astype(F32)
    narrow = picked(back)
    narrow_dir = narrow
    narrow_fit = jnp.zeros_like(narrow)
    residual = [targets[:depth].astype(F32), targets[depth:].astype(F32)]
    alpha = ratio = gamma = None
    moved, image = [None, None], [None, None]
    for step in range(ITERS):
        moved_first, short_first = image_step(design, back, 0, moved[0], alpha)
        other_first = swapped(short_first, COLS)
        short_first, back = lax.optimization_barrier((short_first, back))
        if step:
            gradient = gradient - alpha * back.astype(F32)
        part = weighed(gradient)
        part, back, gradient = lax.optimization_barrier((part, back, gradient))
        gamma_new = part + swapped(part, COLS)
        moved_second, short_second = image_step(design, back, 1, moved[1], alpha)
        other_second = swapped(short_second, COLS)
        moved = [moved_first, moved_second]
        if step:
            image, back, short_second = lax.optimization_barrier(
                (image, back, short_second)
            )
            residual = [r - alpha * q for r, q in zip(residual, image)]
            narrow_alpha = picked_row(alpha)
            narrow_fit = narrow_fit + narrow_alpha * narrow_dir
            narrow = narrow - narrow_alpha * picked(back)
            ratio = gamma_new / gamma
            narrow_dir = narrow + picked_row(ratio) * narrow_dir
            (residual, narrow, narrow_fit, narrow_dir, gradient, other_second) = (
                lax.optimization_barrier(
                    (residual, narrow, narrow_fit, narrow_dir, gradient, other_second)
                )
            )
        gamma = gamma_new
        if step + 1 < ITERS:
            begun, image_first, norm = back_first(design, short_first, other_first, image[0], ratio)
            given, image_second, turned, norm = back_given(
                theirs, design, short_second, other_second, image[1], ratio, begun, norm
            )
            arrived = swapped(given, CORE)
            kept = back_kept(mine, design, turned, begun)
            image = [image_first, image_second]
            both = (kept + arrived[:half].astype(F32)).astype(BF16)
            norms = norm + jnp.sum(arrived[half:].astype(F32), axis=0, keepdims=True)
            high = lax.reduce_precision(norms, 8, 7)
            middle = lax.reduce_precision(norms - high, 8, 7)
            low = norms - high - middle
            below = jnp.concatenate([high, middle, low], axis=0).astype(BF16)
            below = jnp.pad(below, ((0, EXTRA - 3), (0, 0)))
            pieces = jnp.concatenate(
                [both.reshape(chips, rows, fits), jnp.broadcast_to(below, (chips, EXTRA, fits))],
                axis=1,
            )
            sums = exchanged(pieces).astype(F32).sum(axis=0)
            delta = jnp.sum(sums[rows:], axis=0, keepdims=True)
            alpha = gamma / delta
            back = whole_half(sums[:rows], square)
        else:
            pairs = zip((short_first, short_second), (other_first, other_second), image)
            image = [a.astype(F32) + b.astype(F32) + ratio * q for a, b, q in pairs]
            norm = sum(jnp.sum(q * q, axis=0) for q in image)
            copies = jnp.broadcast_to(norm, (lax.axis_size(ROWS), 1, fits))
            copies = lax.all_to_all(copies, ROWS, split_axis=0, concat_axis=0, tiled=True)
            delta = copies.sum(axis=0)
            alpha = gamma / delta
    residual = [r - alpha * q for r, q in zip(residual, image)]
    narrow_fit = narrow_fit + picked_row(alpha) * narrow_dir
    part = (narrow_fit / col_scale).T
    return part, jnp.concatenate(residual, axis=0)


def solution(mesh):
    split = Mesh(
        mesh.devices.reshape(2, 4, 4, 2, mesh.shape["cols"]),
        ("rows_0", "rows_1", "rows_2", "rows_3", "cols"),
    )
    in_specs = (P(ROWS, "cols"), P(ROWS, None), P("cols"))
    out_specs = (P("cols", ROWS), P(ROWS, None))
    return jax.shard_map(
        per_device, mesh=split, in_specs=in_specs, out_specs=out_specs, check_vma=False
    )
```

time: 441 us -> 399 us (0.905); the launches traced: 433 us -> 398 us
  blocking collectives: 81.1 us -> 149 us
  waiting for transfers between devices: 115 us -> 61.2 us
  Pallas kernels: 61.3 us -> 103 us
  local copies, waits for them, and re-layouts: 43.1 us -> 3.07 us
  starting transfers between devices: 94.6 us -> 66.8 us
  other arithmetic: 33 us -> 12.2 us
    all_to_all x5 -> x10, blocking collectives: 68.1 us -> 135 us  [exchanged(): lax.all_to_all(pieces, CHIPS, split_axis=0, concat_axis=0, tiled=True)]
    pallas_call x29, Pallas kernels: 61.3 us -> 103 us  [called(): pl.pallas_call(kernel, in_specs=specs, out_specs=[NEAR] * len(outs), out_...]
    all_to_all x7 -> x2, waiting for transfers between devices: 55 us -> 16.1 us  [exchanged(): lax.all_to_all(pieces, CHIPS, split_axis=0, concat_axis=0, tiled=True)]
    unnamed x134 -> x8, local copies, waits for them, and re-layouts: 38.1 us -> 1.05 us
    all_to_all x7 -> x2, starting transfers between devices: 37 us -> 13.9 us  [exchanged(): lax.all_to_all(pieces, CHIPS, split_axis=0, concat_axis=0, tiled=True)]
    ppermute x30, waiting for transfers between devices: 59.7 us -> 45.1 us  [swapped(): return lax.ppermute(array, axis, ((0, 1), (1, 0)))]
    reduce_sum x6, other arithmetic: 11.2 us -> 3.03 us  [weighed(): return jnp.sum(values * values * weight, axis=0, keepdims=True)]
    sub x6, other arithmetic: 7.73 us -> 0.77 us  [per_device(): residual = [r - alpha * q for r, q in zip(residual, image)]]
  transfers between devices with their start and end apart: 37 -> 32, of which waited for: 29 -> 15; matrix products, arithmetic and copies ran while one was open for 4% -> 2% of each run, Pallas kernels for 8% -> 11%
where the time goes in v3:
time: 399 us; the launch traced here: 398 us
  blocking collectives  149 us (37%)
  Pallas kernels  103 us (26%)
  starting transfers between devices  66.8 us (17%)
  waiting for transfers between devices  61.2 us (15%)
  other arithmetic  12.2 us (3%)
    all_to_all x10, blocking collectives, exchanged(): lax.all_to_all(pieces, CHIPS, split_axis=0, concat_axis=0, tiled=True)  135 us
    pallas_call x29, Pallas kernels, called(): pl.pallas_call(kernel, in_specs=specs, out_specs=[NEAR] * len(outs), out_...  103 us
    ppermute x30, starting transfers between devices, swapped(): return lax.ppermute(array, axis, ((0, 1), (1, 0)))  52.9 us
    ppermute x30, waiting for transfers between devices, swapped(): return lax.ppermute(array, axis, ((0, 1), (1, 0)))  45.1 us
    all_to_all x2, waiting for transfers between devices, exchanged(): lax.all_to_all(pieces, CHIPS, split_axis=0, concat_axis=0, tiled=True)  16.1 us
    all_to_all x2, starting transfers between devices, exchanged(): lax.all_to_all(pieces, CHIPS, split_axis=0, concat_axis=0, tiled=True)  13.9 us
    all_to_all x1, blocking collectives, per_device(): lax.all_to_all(copies, ROWS, split_axis=0, concat_axis=0, tiled=True)  13.7 us
  transfers between devices with their start and end apart: 32, of which 15 were waited for; matrix products, arithmetic and copies ran while one was open for 2% of the time, Pallas kernels for 11%

profile of v3, /device:TPU:1, one launch (start us, length us, event | category | flops | bytes accessed | tf_op | source)
XLA Modules:
  0.0 398.3 jit_solution(2076629506492592071)
XLA Ops:
  1.7 3.6 shard_map.51
  6.8 3.6 shard_map.50
  11.2 9.1 %all-to-all-start = ((bf16[32,48,128]{2,1,0:T(8,128)(2,1)}), bf16[32,48,128]{2,1,0:T(8,128)(2,1)S(1)}, u32[]{:S(2)}, u32[]{:S(2)}) async-start(bf16[32,48,128]{2,1,0:T(8,128)(2,1)} %bitcast.1), calls=%async_computation | async-start | bytes 786432 | tf_op jit(solution)/shard_map/all_to_all | solution.py:279
  20.4 9.1 %all-to-all-done = bf16[32,48,128]{2,1,0:T(8,128)(2,1)S(1)} async-done(((bf16[32,48,128]{2,1,0:T(8,128)(2,1)}), bf16[32,48,128]{2,1,0:T(8,128)(2,1)S(1)}, u32[]{:S(2)}, u32[]{:S(2)}) %all-to-all-start) | async-done | bytes 393248 | tf_op jit(solution)/shard_map/all_to_all | solution.py:279
  29.8 12.7 %all_to_all.65 = bf16[32,48,128]{2,1,0:T(8,128)(2,1)S(1)} all-to-all(bf16[32,48,128]{2,1,0:T(8,128)(2,1)S(1)} %broadcast_in_dim.87), channel_id=1, replica_groups=mesh['rows_0'=2,'rows_1'=4,'rows_2'=4,'rows_3'=2,'cols'=2] {'rows_0','ro..., dimensions={0} | all-to-all | bytes 786432 | tf_op jit(solution)/shard_map/all_to_all | solution.py:279
  42.5 2.7 collective-permute-start.1
  48.0 4.1 %shard_map.52 = (f32[1024,128]{1,0:T(8,128)S(1)}, bf16[1024,128]{1,0:T(8,128)(2,1)S(1)}) custom-call(bf16[2048,3072]{1,0:T(8,128)(2,1)} %d.57, bf16[3072,128]{1,0:T(8,128)(2,1)S(1)} %get-tuple-element.144.v), custom_call_target="tpu_custom_call" | custom-call | flops 805306368 | bytes 6291456 | tf_op jit(solution)/shard_map/pallas_call | solution.py:42
  52.1 2.5 collective-permute-start.4
  55.1 4.1 %shard_map.53 = (f32[1024,128]{1,0:T(8,128)S(1)}, bf16[1024,128]{1,0:T(8,128)(2,1)S(1)}) custom-call(bf16[2048,3072]{1,0:T(8,128)(2,1)} %d.57, bf16[3072,128]{1,0:T(8,128)(2,1)S(1)} %get-tuple-element.144.v), custom_call_target="tpu_custom_call" | custom-call | flops 805306368 | bytes 6291456 | tf_op jit(solution)/shard_map/pallas_call | solution.py:42
  61.1 3.8 shard_map.54
  64.9 3.0 collective-permute-done.3.other_ref
  74.8 13.9 %all_to_all.66 = bf16[32,64,128]{2,1,0:T(8,128)(2,1)S(1)} all-to-all(bf16[32,64,128]{2,1,0:T(8,128)(2,1)S(1)} %pad_maximum_fusion.7), channel_id=1, replica_groups=mesh['rows_0'=2,'rows_1'=4,'rows_2'=4,'rows_3'=2,'cols'=2] {'rows_0','ro..., dimensions={0} | all-to-all | bytes 1048576 | tf_op jit(solution)/shard_map/all_to_all | solution.py:279
  89.6 4.8 %all-to-all-start.3 = ((bf16[32,48,128]{2,1,0:T(8,128)(2,1)}), bf16[32,48,128]{2,1,0:T(8,128)(2,1)}, u32[]{:S(2)}, u32[]{:S(2)}) async-start(bf16[32,48,128]{2,1,0:T(8,128)(2,1)} %broadcast_in_dim.92), calls=%async_computation.3 | async-start | bytes 786432 | tf_op jit(solution)/shard_map/all_to_all | solution.py:279
  96.2 7.0 %all-to-all-done.3 = bf16[32,48,128]{2,1,0:T(8,128)(2,1)} async-done(((bf16[32,48,128]{2,1,0:T(8,128)(2,1)}), bf16[32,48,128]{2,1,0:T(8,128)(2,1)}, u32[]{:S(2)}, u32[]{:S(2)}) %all-to-all-start.3) | async-done | bytes 393248 | tf_op jit(solution)/shard_map/all_to_all | solution.py:279
  103.2 2.7 collective-permute-start.6
  108.6 4.2 %shard_map.57 = (f32[1024,128]{1,0:T(8,128)S(1)}, bf16[1024,128]{1,0:T(8,128)(2,1)S(1)}) custom-call(bf16[2048,3072]{1,0:T(8,128)(2,1)} %d.57, bf16[3072,128]{1,0:T(8,128)(2,1)S(1)} %pad_maximum_fusion.2.v, f32[1024,128]{1,0:T(8,128)S(1)} %get-tuple-element.155.rest_0_, f32[1,128]{1,0:T(1,128)S(1)} %get-tuple-element.310.rest_1_), custom_call_target="tpu_custom_call" | custom-call | flops 805306368 | bytes 6291456 | tf_op jit(solution)/shard_map/pallas_call | solution.py:42
  116.4 4.1 %shard_map.58 = (f32[1024,128]{1,0:T(8,128)S(1)}, bf16[1024,128]{1,0:T(8,128)(2,1)S(1)}) custom-call(bf16[2048,3072]{1,0:T(8,128)(2,1)} %d.57, bf16[3072,128]{1,0:T(8,128)(2,1)S(1)} %pad_maximum_fusion.2.v, f32[1024,128]{1,0:T(8,128)S(1)} %get-tuple-element.159.rest_0_, f32[1,128]{1,0:T(1,128)S(1)} %get-tuple-element.310.rest_1_), custom_call_target="tpu_custom_call" | custom-call | flops 805306368 | bytes 6291456 | tf_op jit(solution)/shard_map/pallas_call | solution.py:42
  122.4 6.6 %collective-permute-done.8.other_ref = bf16[1024,128]{1,0:T(8,128)(2,1)S(1)} collective-permute-done((bf16[1024,128]{1,0:T(8,128)(2,1)S(1)}, bf16[1024,128]{1,0:T(8,128)(2,1)S(1)}, u32[]{:S(2)}, u32[]{:S(2)}) %collective-permute-start.8) | collective-permute-done | bytes 262176 | tf_op jit(solution)/shard_map/ppermute | solution.py:23
  129.0 3.8 shard_map.59
  132.8 2.5 shard_map.60
  137.4 2.5 shard_map.61
  140.2 13.9 %all_to_all.67 = bf16[32,64,128]{2,1,0:T(8,128)(2,1)S(1)} all-to-all(bf16[32,64,128]{2,1,0:T(8,128)(2,1)S(1)} %pad_maximum_fusion.8), channel_id=1, replica_groups=mesh['rows_0'=2,'rows_1'=4,'rows_2'=4,'rows_3'=2,'cols'=2] {'rows_0','ro..., dimensions={0} | all-to-all | bytes 1048576 | tf_op jit(solution)/shard_map/all_to_all | solution.py:279
  154.3 13.2 %all_to_all.68 = bf16[32,48,128]{2,1,0:T(8,128)(2,1)S(1)} all-to-all(bf16[32,48,128]{2,1,0:T(8,128)(2,1)S(1)} %broadcast_in_dim.97), channel_id=1, replica_groups=mesh['rows_0'=2,'rows_1'=4,'rows_2'=4,'rows_3'=2,'cols'=2] {'rows_0','ro..., dimensions={0} | all-to-all | bytes 786432 | tf_op jit(solution)/shard_map/all_to_all | solution.py:279
  171.5 4.2 %shard_map.62 = (f32[1024,128]{1,0:T(8,128)S(1)}, bf16[1024,128]{1,0:T(8,128)(2,1)S(1)}) custom-call(bf16[2048,3072]{1,0:T(8,128)(2,1)} %d.57, bf16[3072,128]{1,0:T(8,128)(2,1)S(1)} %pad_maximum_fusion.3.v, f32[1024,128]{1,0:T(8,128)S(1)} %get-tuple-element.178.rest_0_, f32[1,128]{1,0:T(1,128)S(1)} %bitcast_divide_fusion.4.rest_1_), custom_call_target="tpu_custom_call" | custom-call | flops 805306368 | bytes 6291456 | tf_op jit(solution)/shard_map/pallas_call | solution.py:42
  179.4 4.2 %shard_map.63 = (f32[1024,128]{1,0:T(8,128)S(1)}, bf16[1024,128]{1,0:T(8,128)(2,1)S(1)}) custom-call(bf16[2048,3072]{1,0:T(8,128)(2,1)} %d.57, bf16[3072,128]{1,0:T(8,128)(2,1)S(1)} %pad_maximum_fusion.3.v, f32[1024,128]{1,0:T(8,128)S(1)} %get-tuple-element.182.rest_0_, f32[1,128]{1,0:T(1,128)S(1)} %bitcast_divide_fusion.4.rest_1_), custom_call_target="tpu_custom_call" | custom-call | flops 805306368 | bytes 6291456 | tf_op jit(solution)/shard_map/pallas_call | solution.py:42
  185.5 6.5 %collective-permute-done.13.other_ref = bf16[1024,128]{1,0:T(8,128)(2,1)S(1)} collective-permute-done((bf16[1024,128]{1,0:T(8,128)(2,1)S(1)}, bf16[1024,128]{1,0:T(8,128)(2,1)S(1)}, u32[]{:S(2)}, u32[]{:S(2)}) %collective-permute-start.13) | collective-permute-done | bytes 262176 | tf_op jit(solution)/shard_map/ppermute | solution.py:23
  192.1 3.8 shard_map.64
  195.9 2.5 shard_map.65
  203.0 14.0 %all_to_all.69 = bf16[32,64,128]{2,1,0:T(8,128)(2,1)S(1)} all-to-all(bf16[32,64,128]{2,1,0:T(8,128)(2,1)S(1)} %pad_maximum_fusion.9), channel_id=1, replica_groups=mesh['rows_0'=2,'rows_1'=4,'rows_2'=4,'rows_3'=2,'cols'=2] {'rows_0','ro..., dimensions={0} | all-to-all | bytes 1048576 | tf_op jit(solution)/shard_map/all_to_all | solution.py:279
  217.2 13.3 %all_to_all.70 = bf16[32,48,128]{2,1,0:T(8,128)(2,1)S(1)} all-to-all(bf16[32,48,128]{2,1,0:T(8,128)(2,1)S(1)} %broadcast_in_dim.102), channel_id=1, replica_groups=mesh['rows_0'=2,'rows_1'=4,'rows_2'=4,'rows_3'=2,'cols'=2] {'rows_0','ro..., dimensions={0} | all-to-all | bytes 786432 | tf_op jit(solution)/shard_map/all_to_all | solution.py:279
  234.4 4.2 %shard_map.67 = (f32[1024,128]{1,0:T(8,128)S(1)}, bf16[1024,128]{1,0:T(8,128)(2,1)S(1)}) custom-call(bf16[2048,3072]{1,0:T(8,128)(2,1)} %d.57, bf16[3072,128]{1,0:T(8,128)(2,1)S(1)} %pad_maximum_fusion.4.v, f32[1024,128]{1,0:T(8,128)S(1)} %get-tuple-element.205.rest_0_, f32[1,128]{1,0:T(1,128)S(1)} %bitcast_divide_fusion.3.rest_1_), custom_call_target="tpu_custom_call" | custom-call | flops 805306368 | bytes 6291456 | tf_op jit(solution)/shard_map/pallas_call | solution.py:42
  242.3 4.2 %shard_map.68 = (f32[1024,128]{1,0:T(8,128)S(1)}, bf16[1024,128]{1,0:T(8,128)(2,1)S(1)}) custom-call(bf16[2048,3072]{1,0:T(8,128)(2,1)} %d.57, bf16[3072,128]{1,0:T(8,128)(2,1)S(1)} %pad_maximum_fusion.4.v, f32[1024,128]{1,0:T(8,128)S(1)} %get-tuple-element.209.rest_0_, f32[1,128]{1,0:T(1,128)S(1)} %bitcast_divide_fusion.3.rest_1_), custom_call_target="tpu_custom_call" | custom-call | flops 805306368 | bytes 6291456 | tf_op jit(solution)/shard_map/pallas_call | solution.py:42
  248.5 6.5 %collective-permute-done.18.other_ref = bf16[1024,128]{1,0:T(8,128)(2,1)S(1)} collective-permute-done((bf16[1024,128]{1,0:T(8,128)(2,1)S(1)}, bf16[1024,128]{1,0:T(8,128)(2,1)S(1)}, u32[]{:S(2)}, u32[]{:S(2)}) %collective-permute-start.18) | collective-permute-done | bytes 262176 | tf_op jit(solution)/shard_map/ppermute | solution.py:23
  255.0 3.8 shard_map.69
  258.8 2.5 shard_map.70
  266.0 13.9 %all_to_all.71 = bf16[32,64,128]{2,1,0:T(8,128)(2,1)S(1)} all-to-all(bf16[32,64,128]{2,1,0:T(8,128)(2,1)S(1)} %pad_maximum_fusion.10), channel_id=1, replica_groups=mesh['rows_0'=2,'rows_1'=4,'rows_2'=4,'rows_3'=2,'cols'=2] {'rows_0','ro..., dimensions={0} | all-to-all | bytes 1048576 | tf_op jit(solution)/shard_map/all_to_all | solution.py:279
  280.1 13.3 %all_to_all.72 = bf16[32,48,128]{2,1,0:T(8,128)(2,1)S(1)} all-to-all(bf16[32,48,128]{2,1,0:T(8,128)(2,1)S(1)} %broadcast_in_dim.107), channel_id=1, replica_groups=mesh['rows_0'=2,'rows_1'=4,'rows_2'=4,'rows_3'=2,'cols'=2] {'rows_0','ro..., dimensions={0} | all-to-all | bytes 786432 | tf_op jit(solution)/shard_map/all_to_all | solution.py:279
  297.4 4.1 %shard_map.72 = (f32[1024,128]{1,0:T(8,128)S(1)}, bf16[1024,128]{1,0:T(8,128)(2,1)S(1)}) custom-call(bf16[2048,3072]{1,0:T(8,128)(2,1)} %d.57, bf16[3072,128]{1,0:T(8,128)(2,1)S(1)} %pad_maximum_fusion.5.v, f32[1024,128]{1,0:T(8,128)S(1)} %get-tuple-element.232.rest_0_, f32[1,128]{1,0:T(1,128)S(1)} %bitcast_divide_fusion.2.rest_1_), custom_call_target="tpu_custom_call" | custom-call | flops 805306368 | bytes 6291456 | tf_op jit(solution)/shard_map/pallas_call | solution.py:42
  305.1 4.1 %shard_map.73 = (f32[1024,128]{1,0:T(8,128)S(1)}, bf16[1024,128]{1,0:T(8,128)(2,1)S(1)}) custom-call(bf16[2048,3072]{1,0:T(8,128)(2,1)} %d.57, bf16[3072,128]{1,0:T(8,128)(2,1)S(1)} %pad_maximum_fusion.5.v, f32[1024,128]{1,0:T(8,128)S(1)} %get-tuple-element.236.rest_0_, f32[1,128]{1,0:T(1,128)S(1)} %bitcast_divide_fusion.2.rest_1_), custom_call_target="tpu_custom_call" | custom-call | flops 805306368 | bytes 6291456 | tf_op jit(solution)/shard_map/pallas_call | solution.py:42
  311.2 6.5 %collective-permute-done.23.other_ref = bf16[1024,128]{1,0:T(8,128)(2,1)S(1)} collective-permute-done((bf16[1024,128]{1,0:T(8,128)(2,1)S(1)}, bf16[1024,128]{1,0:T(8,128)(2,1)S(1)}, u32[]{:S(2)}, u32[]{:S(2)}) %collective-permute-start.23) | collective-permute-done | bytes 262176 | tf_op jit(solution)/shard_map/ppermute | solution.py:23
  317.7 3.8 shard_map.74
  321.5 2.5 shard_map.75
  328.7 14.0 %all_to_all.73 = bf16[32,64,128]{2,1,0:T(8,128)(2,1)S(1)} all-to-all(bf16[32,64,128]{2,1,0:T(8,128)(2,1)S(1)} %pad_maximum_fusion.11), channel_id=1, replica_groups=mesh['rows_0'=2,'rows_1'=4,'rows_2'=4,'rows_3'=2,'cols'=2] {'rows_0','ro..., dimensions={0} | all-to-all | bytes 1048576 | tf_op jit(solution)/shard_map/all_to_all | solution.py:279
  342.9 13.2 %all_to_all.74 = bf16[32,48,128]{2,1,0:T(8,128)(2,1)S(1)} all-to-all(bf16[32,48,128]{2,1,0:T(8,128)(2,1)S(1)} %broadcast_in_dim.112), channel_id=1, replica_groups=mesh['rows_0'=2,'rows_1'=4,'rows_2'=4,'rows_3'=2,'cols'=2] {'rows_0','ro..., dimensions={0} | all-to-all | bytes 786432 | tf_op jit(solution)/shard_map/all_to_all | solution.py:279
  360.1 5.0 %shard_map.77 = (f32[1024,128]{1,0:T(8,128)}, bf16[1024,128]{1,0:T(8,128)(2,1)S(1)}) custom-call(bf16[2048,3072]{1,0:T(8,128)(2,1)} %d.57, bf16[3072,128]{1,0:T(8,128)(2,1)S(1)} %pad_maximum_fusion.6.v, f32[1024,128]{1,0:T(8,128)S(1)} %get-tuple-element.259.rest_0_, f32[1,128]{1,0:T(1,128)S(1)} %bitcast_divide_fusion.1.rest_1_), custom_call_target="tpu_custom_call" | custom-call | flops 805306368 | bytes 6291456 | tf_op jit(solution)/shard_map/pallas_call | solution.py:42
  368.8 5.0 %shard_map.78 = (f32[1024,128]{1,0:T(8,128)}, bf16[1024,128]{1,0:T(8,128)(2,1)S(1)}) custom-call(bf16[2048,3072]{1,0:T(8,128)(2,1)} %d.57, bf16[3072,128]{1,0:T(8,128)(2,1)S(1)} %pad_maximum_fusion.6.v, f32[1024,128]{1,0:T(8,128)S(1)} %get-tuple-element.263.rest_0_, f32[1,128]{1,0:T(1,128)S(1)} %bitcast_divide_fusion.1.rest_1_), custom_call_target="tpu_custom_call" | custom-call | flops 805306368 | bytes 6291456 | tf_op jit(solution)/shard_map/pallas_call | solution.py:42
  375.7 6.5 %collective-permute-done.28 = bf16[1024,128]{1,0:T(8,128)(2,1)S(1)} collective-permute-done((bf16[1024,128]{1,0:T(8,128)(2,1)S(1)}, bf16[1024,128]{1,0:T(8,128)(2,1)S(1)}, u32[]{:S(2)}, u32[]{:S(2)}) %collective-permute-start.28) | collective-permute-done | bytes 262176 | tf_op jit(solution)/shard_map/ppermute | solution.py:23
  382.6 13.7 %all_to_all.75 = f32[64,1,128]{2,1,0:T(1,128)S(1)} all-to-all(f32[64,1,128]{2,1,0:T(1,128)S(1)} %broadcast_in_dim.114), channel_id=1, replica_groups=mesh['rows_0'=2,'rows_1'=4,'rows_2'=4,'rows_3'=2,'cols'=2] {'rows_0','ro..., dimensions={0} | all-to-all | bytes 65536 | tf_op jit(solution)/shard_map/all_to_all | solution.py:393
  (183 shorter events, 83.9 us)
Async XLA Ops:
  0.6 1.0 copy-start
  1.7 5.1 %copy-start.1 = (bf16[2048,128]{1,0:T(8,128)(2,1)S(1)}, bf16[2048,128]{1,0:T(8,128)(2,1)}, u32[]{:S(2)}) copy-start(bf16[2048,128]{1,0:T(8,128)(2,1)} %v.3) | copy-start | bytes 1572868
  5.3 5.1 %collective-permute-start = (bf16[1536,128]{1,0:T(8,128)(2,1)S(1)}, bf16[1536,128]{1,0:T(8,128)(2,1)S(1)}, u32[]{:S(2)}, u32[]{:S(2)}) collective-permute-start(bf16[1536,128]{1,0:T(8,128)(2,1)S(1)} %shard_map.51), channel_id=1, source_target_pairs={{0,2},{2,0},{1,3},{3,1},{4,6},{6,4},{5,7},{7,5},{8,10},{10,8},{9,1... | collective-permute-start | bytes 1179656 | tf_op jit(solution)/shard_map/ppermute | solution.py:23
  10.4 10.0 %copy-start.3 = (f32[3072]{0:T(1024)S(1)}, f32[3072]{0:T(1024)}, u32[]{:S(2)}) copy-start(f32[3072]{0:T(1024)} %param.5) | copy-start | bytes 36868
  11.2 18.3 %all-to-all-start = ((bf16[32,48,128]{2,1,0:T(8,128)(2,1)}), bf16[32,48,128]{2,1,0:T(8,128)(2,1)S(1)}, u32[]{:S(2)}, u32[]{:S(2)}) async-start(bf16[32,48,128]{2,1,0:T(8,128)(2,1)} %bitcast.1), calls=%async_computation | async-start | bytes 786432 | tf_op jit(solution)/shard_map/all_to_all | solution.py:279
  42.5 4.1 %collective-permute-start.1 = (bf16[1536,128]{1,0:T(8,128)(2,1)S(1)}, bf16[1536,128]{1,0:T(8,128)(2,1)S(1)}, u32[]{:S(2)}, u32[]{:S(2)}) collective-permute-start(bf16[1536,128]{1,0:T(8,128)(2,1)S(1)} %bitcast.134), channel_id=1, source_target_pairs={{0,2},{2,0},{1,3},{3,1},{4,6},{6,4},{5,7},{7,5},{8,10},{10,8},{9,1... | collective-permute-start | bytes 1179656 | tf_op jit(solution)/shard_map/ppermute | solution.py:23
  52.1 9.1 %collective-permute-start.4 = (bf16[1024,128]{1,0:T(8,128)(2,1)S(1)}, bf16[1024,128]{1,0:T(8,128)(2,1)S(1)}, u32[]{:S(2)}, u32[]{:S(2)}) collective-permute-start(bf16[1024,128]{1,0:T(8,128)(2,1)S(1)} %get-tuple-element.146.own_ref), channel_id=1, source_target_pairs={{0,1},{1,0},{2,3},{3,2},{4,5},{5,4},{6,7},{7,6},{8,9},{9,8},{10,11... | collective-permute-start | bytes 786440 | tf_op jit(solution)/shard_map/ppermute | solution.py:23
  59.2 8.8 %collective-permute-start.3 = (bf16[1024,128]{1,0:T(8,128)(2,1)S(1)}, bf16[1024,128]{1,0:T(8,128)(2,1)S(1)}, u32[]{:S(2)}, u32[]{:S(2)}) collective-permute-start(bf16[1024,128]{1,0:T(8,128)(2,1)S(1)} %get-tuple-element.145.own_ref), channel_id=1, source_target_pairs={{0,1},{1,0},{2,3},{3,2},{4,5},{5,4},{6,7},{7,6},{8,9},{9,8},{10,11... | collective-permute-start | bytes 786440 | tf_op jit(solution)/shard_map/ppermute | solution.py:23
  70.5 4.1 %collective-permute-start.5 = (bf16[1552,128]{1,0:T(8,128)(2,1)S(1)}, bf16[1552,128]{1,0:T(8,128)(2,1)S(1)}, u32[]{:S(2)}, u32[]{:S(2)}) collective-permute-start(bf16[1552,128]{1,0:T(8,128)(2,1)S(1)} %get-tuple-element.150), channel_id=1, source_target_pairs={{0,2},{2,0},{1,3},{3,1},{4,6},{6,4},{5,7},{7,5},{8,10},{10,8},{9,1... | collective-permute-start | bytes 1191944 | tf_op jit(solution)/shard_map/ppermute | solution.py:23
  89.6 13.5 %all-to-all-start.3 = ((bf16[32,48,128]{2,1,0:T(8,128)(2,1)}), bf16[32,48,128]{2,1,0:T(8,128)(2,1)}, u32[]{:S(2)}, u32[]{:S(2)}) async-start(bf16[32,48,128]{2,1,0:T(8,128)(2,1)} %broadcast_in_dim.92), calls=%async_computation.3 | async-start | bytes 786432 | tf_op jit(solution)/shard_map/all_to_all | solution.py:279
  94.5 11.4 %collective-permute-start.2 = (f32[1,128]{1,0:T(1,128)S(1)}, f32[1,128]{1,0:T(1,128)S(1)}, u32[]{:S(2)}, u32[]{:S(2)}) collective-permute-start(f32[1,128]{1,0:T(1,128)S(1)} %bitcast.153), channel_id=1, source_target_pairs={{0,1},{1,0},{2,3},{3,2},{4,5},{5,4},{6,7},{7,6},{8,9},{9,8},{10,11... | collective-permute-start | bytes 1544 | tf_op jit(solution)/shard_map/ppermute | solution.py:23
  103.2 4.3 %collective-permute-start.6 = (bf16[1536,128]{1,0:T(8,128)(2,1)}, bf16[1536,128]{1,0:T(8,128)(2,1)S(1)}, u32[]{:S(2)}, u32[]{:S(2)}) collective-permute-start(bf16[1536,128]{1,0:T(8,128)(2,1)} %bitcast.8), channel_id=1, source_target_pairs={{0,2},{2,0},{1,3},{3,1},{4,6},{6,4},{5,7},{7,5},{8,10},{10,8},{9,1... | collective-permute-start | bytes 1179656 | tf_op jit(solution)/shard_map/ppermute | solution.py:23
  108.6 5.6 %copy-start.2 = (f32[3072,128]{1,0:T(8,128)S(1)}, f32[3072,128]{1,0:T(8,128)}, u32[]{:S(2)}) copy-start(f32[3072,128]{1,0:T(8,128)} %get-tuple-element.154) | copy-start | bytes 4718596
  112.8 16.2 %collective-permute-start.9 = (bf16[1024,128]{1,0:T(8,128)(2,1)S(1)}, bf16[1024,128]{1,0:T(8,128)(2,1)S(1)}, u32[]{:S(2)}, u32[]{:S(2)}) collective-permute-start(bf16[1024,128]{1,0:T(8,128)(2,1)S(1)} %get-tuple-element.169.own_ref), channel_id=1, source_target_pairs={{0,1},{1,0},{2,3},{3,2},{4,5},{5,4},{6,7},{7,6},{8,9},{9,8},{10,11... | collective-permute-start | bytes 786440 | tf_op jit(solution)/shard_map/ppermute | solution.py:23
  114.6 7.3 %collective-permute-start.7 = (f32[1,128]{1,0:T(1,128)S(1)}, f32[1,128]{1,0:T(1,128)S(1)}, u32[]{:S(2)}, u32[]{:S(2)}) collective-permute-start(f32[1,128]{1,0:T(1,128)S(1)} %bitcast.151), channel_id=1, source_target_pairs={{0,1},{1,0},{2,3},{3,2},{4,5},{5,4},{6,7},{7,6},{8,9},{9,8},{10,11... | collective-permute-start | bytes 1544 | tf_op jit(solution)/shard_map/ppermute | solution.py:23
  120.5 8.5 %collective-permute-start.8 = (bf16[1024,128]{1,0:T(8,128)(2,1)S(1)}, bf16[1024,128]{1,0:T(8,128)(2,1)S(1)}, u32[]{:S(2)}, u32[]{:S(2)}) collective-permute-start(bf16[1024,128]{1,0:T(8,128)(2,1)S(1)} %get-tuple-element.167.own_ref), channel_id=1, source_target_pairs={{0,1},{1,0},{2,3},{3,2},{4,5},{5,4},{6,7},{7,6},{8,9},{9,8},{10,11... | collective-permute-start | bytes 786440 | tf_op jit(solution)/shard_map/ppermute | solution.py:23
  135.4 4.6 %collective-permute-start.10 = (bf16[1552,128]{1,0:T(8,128)(2,1)S(1)}, bf16[1552,128]{1,0:T(8,128)(2,1)S(1)}, u32[]{:S(2)}, u32[]{:S(2)}) collective-permute-start(bf16[1552,128]{1,0:T(8,128)(2,1)S(1)} %get-tuple-element.173), channel_id=1, source_target_pairs={{0,2},{2,0},{1,3},{3,1},{4,6},{6,4},{5,7},{7,5},{8,10},{10,8},{9,1... | collective-permute-start | bytes 1191944 | tf_op jit(solution)/shard_map/ppermute | solution.py:23
  167.5 3.9 collective-permute-start.11
  175.7 16.4 %collective-permute-start.14 = (bf16[1024,128]{1,0:T(8,128)(2,1)S(1)}, bf16[1024,128]{1,0:T(8,128)(2,1)S(1)}, u32[]{:S(2)}, u32[]{:S(2)}) collective-permute-start(bf16[1024,128]{1,0:T(8,128)(2,1)S(1)} %get-tuple-element.196.own_ref), channel_id=1, source_target_pairs={{0,1},{1,0},{2,3},{3,2},{4,5},{5,4},{6,7},{7,6},{8,9},{9,8},{10,11... | collective-permute-start | bytes 786440 | tf_op jit(solution)/shard_map/ppermute | solution.py:23
  177.6 7.8 %collective-permute-start.12 = (f32[1,128]{1,0:T(1,128)S(1)}, f32[1,128]{1,0:T(1,128)S(1)}, u32[]{:S(2)}, u32[]{:S(2)}) collective-permute-start(f32[1,128]{1,0:T(1,128)S(1)} %bitcast.145), channel_id=1, source_target_pairs={{0,1},{1,0},{2,3},{3,2},{4,5},{5,4},{6,7},{7,6},{8,9},{9,8},{10,11... | collective-permute-start | bytes 1544 | tf_op jit(solution)/shard_map/ppermute | solution.py:23
  183.6 8.5 %collective-permute-start.13 = (bf16[1024,128]{1,0:T(8,128)(2,1)S(1)}, bf16[1024,128]{1,0:T(8,128)(2,1)S(1)}, u32[]{:S(2)}, u32[]{:S(2)}) collective-permute-start(bf16[1024,128]{1,0:T(8,128)(2,1)S(1)} %get-tuple-element.194.own_ref), channel_id=1, source_target_pairs={{0,1},{1,0},{2,3},{3,2},{4,5},{5,4},{6,7},{7,6},{8,9},{9,8},{10,11... | collective-permute-start | bytes 786440 | tf_op jit(solution)/shard_map/ppermute | solution.py:23
  198.4 4.4 %collective-permute-start.15 = (bf16[1552,128]{1,0:T(8,128)(2,1)S(1)}, bf16[1552,128]{1,0:T(8,128)(2,1)S(1)}, u32[]{:S(2)}, u32[]{:S(2)}) collective-permute-start(bf16[1552,128]{1,0:T(8,128)(2,1)S(1)} %get-tuple-element.200), channel_id=1, source_target_pairs={{0,2},{2,0},{1,3},{3,1},{4,6},{6,4},{5,7},{7,5},{8,10},{10,8},{9,1... | collective-permute-start | bytes 1191944 | tf_op jit(solution)/shard_map/ppermute | solution.py:23
  230.4 3.9 collective-permute-start.16
  238.7 16.4 %collective-permute-start.19 = (bf16[1024,128]{1,0:T(8,128)(2,1)S(1)}, bf16[1024,128]{1,0:T(8,128)(2,1)S(1)}, u32[]{:S(2)}, u32[]{:S(2)}) collective-permute-start(bf16[1024,128]{1,0:T(8,128)(2,1)S(1)} %get-tuple-element.223.own_ref), channel_id=1, source_target_pairs={{0,1},{1,0},{2,3},{3,2},{4,5},{5,4},{6,7},{7,6},{8,9},{9,8},{10,11... | collective-permute-start | bytes 786440 | tf_op jit(solution)/shard_map/ppermute | solution.py:23
  240.5 7.8 %collective-permute-start.17 = (f32[1,128]{1,0:T(1,128)S(1)}, f32[1,128]{1,0:T(1,128)S(1)}, u32[]{:S(2)}, u32[]{:S(2)}) collective-permute-start(f32[1,128]{1,0:T(1,128)S(1)} %bitcast.147), channel_id=1, source_target_pairs={{0,1},{1,0},{2,3},{3,2},{4,5},{5,4},{6,7},{7,6},{8,9},{9,8},{10,11... | collective-permute-start | bytes 1544 | tf_op jit(solution)/shard_map/ppermute | solution.py:23
  246.5 8.5 %collective-permute-start.18 = (bf16[1024,128]{1,0:T(8,128)(2,1)S(1)}, bf16[1024,128]{1,0:T(8,128)(2,1)S(1)}, u32[]{:S(2)}, u32[]{:S(2)}) collective-permute-start(bf16[1024,128]{1,0:T(8,128)(2,1)S(1)} %get-tuple-element.221.own_ref), channel_id=1, source_target_pairs={{0,1},{1,0},{2,3},{3,2},{4,5},{5,4},{6,7},{7,6},{8,9},{9,8},{10,11... | collective-permute-start | bytes 786440 | tf_op jit(solution)/shard_map/ppermute | solution.py:23
  261.3 4.4 %collective-permute-start.20 = (bf16[1552,128]{1,0:T(8,128)(2,1)S(1)}, bf16[1552,128]{1,0:T(8,128)(2,1)S(1)}, u32[]{:S(2)}, u32[]{:S(2)}) collective-permute-start(bf16[1552,128]{1,0:T(8,128)(2,1)S(1)} %get-tuple-element.227), channel_id=1, source_target_pairs={{0,2},{2,0},{1,3},{3,1},{4,6},{6,4},{5,7},{7,5},{8,10},{10,8},{9,1... | collective-permute-start | bytes 1191944 | tf_op jit(solution)/shard_map/ppermute | solution.py:23
  293.4 3.9 collective-permute-start.21
  301.5 16.2 %collective-permute-start.24 = (bf16[1024,128]{1,0:T(8,128)(2,1)S(1)}, bf16[1024,128]{1,0:T(8,128)(2,1)S(1)}, u32[]{:S(2)}, u32[]{:S(2)}) collective-permute-start(bf16[1024,128]{1,0:T(8,128)(2,1)S(1)} %get-tuple-element.250.own_ref), channel_id=1, source_target_pairs={{0,1},{1,0},{2,3},{3,2},{4,5},{5,4},{6,7},{7,6},{8,9},{9,8},{10,11... | collective-permute-start | bytes 786440 | tf_op jit(solution)/shard_map/ppermute | solution.py:23
  303.3 7.7 %collective-permute-start.22 = (f32[1,128]{1,0:T(1,128)S(1)}, f32[1,128]{1,0:T(1,128)S(1)}, u32[]{:S(2)}, u32[]{:S(2)}) collective-permute-start(f32[1,128]{1,0:T(1,128)S(1)} %bitcast.149), channel_id=1, source_target_pairs={{0,1},{1,0},{2,3},{3,2},{4,5},{5,4},{6,7},{7,6},{8,9},{9,8},{10,11... | collective-permute-start | bytes 1544 | tf_op jit(solution)/shard_map/ppermute | solution.py:23
  309.2 8.5 %collective-permute-start.23 = (bf16[1024,128]{1,0:T(8,128)(2,1)S(1)}, bf16[1024,128]{1,0:T(8,128)(2,1)S(1)}, u32[]{:S(2)}, u32[]{:S(2)}) collective-permute-start(bf16[1024,128]{1,0:T(8,128)(2,1)S(1)} %get-tuple-element.248.own_ref), channel_id=1, source_target_pairs={{0,1},{1,0},{2,3},{3,2},{4,5},{5,4},{6,7},{7,6},{8,9},{9,8},{10,11... | collective-permute-start | bytes 786440 | tf_op jit(solution)/shard_map/ppermute | solution.py:23
  324.0 4.4 %collective-permute-start.25 = (bf16[1552,128]{1,0:T(8,128)(2,1)S(1)}, bf16[1552,128]{1,0:T(8,128)(2,1)S(1)}, u32[]{:S(2)}, u32[]{:S(2)}) collective-permute-start(bf16[1552,128]{1,0:T(8,128)(2,1)S(1)} %get-tuple-element.254), channel_id=1, source_target_pairs={{0,2},{2,0},{1,3},{3,1},{4,6},{6,4},{5,7},{7,5},{8,10},{10,8},{9,1... | collective-permute-start | bytes 1191944 | tf_op jit(solution)/shard_map/ppermute | solution.py:23
  356.1 3.9 collective-permute-start.26
  365.1 17.2 %collective-permute-start.29 = (bf16[1024,128]{1,0:T(8,128)(2,1)S(1)}, bf16[1024,128]{1,0:T(8,128)(2,1)S(1)}, u32[]{:S(2)}, u32[]{:S(2)}) collective-permute-start(bf16[1024,128]{1,0:T(8,128)(2,1)S(1)} %get-tuple-element.274), channel_id=1, source_target_pairs={{0,1},{1,0},{2,3},{3,2},{4,5},{5,4},{6,7},{7,6},{8,9},{9,8},{10,11... | collective-permute-start | bytes 786440 | tf_op jit(solution)/shard_map/ppermute | solution.py:23
  366.9 8.6 %collective-permute-start.27 = (f32[1,128]{1,0:T(1,128)S(1)}, f32[1,128]{1,0:T(1,128)S(1)}, u32[]{:S(2)}, u32[]{:S(2)}) collective-permute-start(f32[1,128]{1,0:T(1,128)S(1)} %bitcast.143), channel_id=1, source_target_pairs={{0,1},{1,0},{2,3},{3,2},{4,5},{5,4},{6,7},{7,6},{8,9},{9,8},{10,11... | collective-permute-start | bytes 1544 | tf_op jit(solution)/shard_map/ppermute | solution.py:23
  373.7 8.5 %collective-permute-start.28 = (bf16[1024,128]{1,0:T(8,128)(2,1)S(1)}, bf16[1024,128]{1,0:T(8,128)(2,1)S(1)}, u32[]{:S(2)}, u32[]{:S(2)}) collective-permute-start(bf16[1024,128]{1,0:T(8,128)(2,1)S(1)} %get-tuple-element.275), channel_id=1, source_target_pairs={{0,1},{1,0},{2,3},{3,2},{4,5},{5,4},{6,7},{7,6},{8,9},{9,8},{10,11... | collective-permute-start | bytes 786440 | tf_op jit(solution)/shard_map/ppermute | solution.py:23

commit v4 on v3

--- a/solution.py
+++ b/solution.py
@@ -13,18 +13,20 @@
 COLS = "cols"
 BF16 = jnp.bfloat16
 F32 = jnp.float32
-EXTRA = 16
+EXTRA = 8
 ROW_BLOCK = 128
 COL_BLOCK = 512
-VMEM = 48 * 1024 * 1024
+START_BLOCK = 256
+FAR_VMEM = 43 * 1024 * 1024
+NEAR_VMEM = 8 * 1024 * 1024
 
 
 def swapped(array, axis):
     return lax.ppermute(array, axis, ((0, 1), (1, 0)))
 
 
-def settings():
-    return pltpu.CompilerParams(vmem_limit_bytes=VMEM)
+def settings(near):
+    return pltpu.CompilerParams(vmem_limit_bytes=NEAR_VMEM if near else FAR_VMEM)
 
 
 def price(rows, cols, fits):
@@ -38,26 +40,32 @@
 SCALAR = pl.BlockSpec(memory_space=pltpu.SMEM)
 
 
-def called(kernel, ins, specs, outs, held, steps, cost, extra=()):
+def called(kernel, ins, specs, outs, cost, scratch=(), near=True):
     return pl.pallas_call(
         kernel,
         in_specs=specs,
         out_specs=[NEAR] * len(outs),
         out_shape=[jax.ShapeDtypeStruct(shape, dtype) for shape, dtype in outs],
-        scratch_shapes=[
-            pltpu.VMEM(held, BF16),
-            pltpu.SemaphoreType.DMA((steps,)),
-            *extra,
-        ],
-        compiler_params=settings(),
+        scratch_shapes=list(scratch),
+        compiler_params=settings(near),
         cost_estimate=cost,
     )(*ins)
 
 
-def started(fetch, steps):
+def streamed(fetch, steps, work):
     @pl.loop(0, steps)
     def _(i):
         fetch(i).start()
+
+    def ready(i):
+        fetch(i).wait()
+        work(i)
+
+    pl.loop(0, steps)(ready)
+
+
+def aligned(start, size):
+    return pl.ds(pl.multiple_of(start, size), size)
 
 
 def image_step(design, vector, chunk, moved=None, alpha=None):
@@ -67,29 +75,25 @@
 
     def kernel(d, v, *rest):
         if moved is not None:
-            u, a, out, short, held, sems = rest
+            u, a, out, short, close, sems = rest
         else:
-            out, short, held, sems = rest
+            out, short, close, sems = rest
 
         def fetch(i):
-            return pltpu.make_async_copy(
-                d.at[pl.ds(chunk * rows + i * ROW_BLOCK, ROW_BLOCK), :],
-                held.at[i],
-                sems.at[i],
-            )
-
-        started(fetch, steps)
-
-        @pl.loop(0, steps)
-        def _(i):
-            fetch(i).wait()
-            where = pl.ds(pl.multiple_of(i * ROW_BLOCK, ROW_BLOCK), ROW_BLOCK)
-            product = jnp.dot(held[i], v[...], preferred_element_type=F32)
+            where = aligned(i * ROW_BLOCK, ROW_BLOCK)
+            source = aligned(chunk * rows + i * ROW_BLOCK, ROW_BLOCK)
+            return pltpu.make_async_copy(d.at[source, :], close.at[where, :], sems.at[i])
+
+        def work(i):
+            where = aligned(i * ROW_BLOCK, ROW_BLOCK)
+            product = jnp.dot(close[where, :], v[...], preferred_element_type=F32)
             if moved is not None:
                 product = u[where, :] - a[...] * product
             out[where, :] = product
             short[where, :] = product.astype(BF16)
 
+        streamed(fetch, steps, work)
+
     args, specs = [design, vector], [ANYWHERE, NEAR]
     if moved is not None:
         args, specs = args + [moved, alpha], specs + [NEAR, NEAR]
@@ -97,53 +101,45 @@
         kernel,
         args,
         specs,
-        [((rows, fits), F32), ((rows, fits), BF16)],
-        (steps, ROW_BLOCK, width),
-        steps,
+        [((rows, fits), F32), ((rows, fits), BF16), ((rows, width), BF16)],
         price(rows, width, fits),
-    )
-
-
-def fetcher(d, held, sems, first_row, rows, first_col, block):
-    def fetch(i):
-        return pltpu.make_async_copy(
-            d.at[
-                pl.ds(first_row, rows),
-                pl.ds(pl.multiple_of(first_col + i * block, block), block),
-            ],
-            held.at[i],
-            sems.at[i],
-        )
-
-    return fetch
+        [pltpu.SemaphoreType.DMA((steps,))],
+        False,
+    )
 
 
 def start_back(side, design, vectors):
     rows, width = design.shape
     fits = vectors.shape[1]
-    half, block = width // 2, COL_BLOCK // 2
+    half, block = width // 2, START_BLOCK
     steps = half // block
 
-    def kernel(s, d, v, out, held, sems, turned):
-        fetch = fetcher(d, held, sems, 0, rows, s[0] * half, block)
-        started(fetch, steps)
+    def kernel(s, d, v, out, turned, held, sems):
+        def fetch(i):
+            return pltpu.make_async_copy(
+                d.at[:, aligned(s[0] * half + i * block, block)], held.at[i], sems.at[i]
+            )
+
         turned[...] = v[...].T
 
-        @pl.loop(0, steps)
-        def _(i):
-            fetch(i).wait()
+        def work(i):
             product = jnp.dot(turned[...], held[i], preferred_element_type=F32)
-            out[pl.ds(pl.multiple_of(i * block, block), block), :] = product.T.astype(BF16)
+            out[aligned(i * block, block), :] = product.T.astype(BF16)
+
+        streamed(fetch, steps, work)
 
     return called(
         kernel,
         [side, design, vectors],
         [SCALAR, ANYWHERE, NEAR],
         [((half, fits), BF16)],
-        (steps, rows, block),
-        steps,
         price(rows, half, fits),
-        [pltpu.VMEM((fits, rows), BF16)],
+        [
+            pltpu.VMEM((fits, rows), BF16),
+            pltpu.VMEM((steps, rows, block), BF16),
+            pltpu.SemaphoreType.DMA((steps,)),
+        ],
+        False,
     )[0]
 
 
@@ -157,28 +153,26 @@
 def back_first(design, own, other, prior, ratio):
     rows, width = own.shape[0], design.shape[1]
     fits = own.shape[1]
-    steps = width // COL_BLOCK
     follow = prior is not None
 
     def kernel(d, own_ref, other_ref, *rest):
         prior_ref = ratio_ref = None
         if follow:
             prior_ref, ratio_ref, *rest = rest
-        out, image, norm, held, sems, turned = rest
-        fetch = fetcher(d, held, sems, 0, rows, 0, COL_BLOCK)
-        started(fetch, steps)
+        out, image, norm, turned = rest
         total = joined(own_ref, other_ref, prior_ref, ratio_ref)
         image[...] = total
         norm[...] = jnp.sum(total * total, axis=0, keepdims=True)
         turned[...] = total.astype(BF16).T
 
-        @pl.loop(0, steps)
+        @pl.loop(0, width // COL_BLOCK)
         def _(i):
-            fetch(i).wait()
-            product = jnp.dot(turned[...], held[i], preferred_element_type=F32)
-            out[pl.ds(pl.multiple_of(i * COL_BLOCK, COL_BLOCK), COL_BLOCK), :] = product.T
-
-    args, specs = [design, own, other], [ANYWHERE, NEAR, NEAR]
+            where = aligned(i * COL_BLOCK, COL_BLOCK)
+            block = d[:, where]
+            product = jnp.dot(turned[...], block, preferred_element_type=F32)
+            out[where, :] = product.T
+
+    args, specs = [design, own, other], [NEAR, NEAR, NEAR]
     if follow:
         args, specs = args + [prior, ratio], specs + [NEAR, NEAR]
     return called(
@@ -186,8 +180,6 @@
         args,
         specs,
         [((width, fits), F32), ((rows, fits), F32), ((1, fits), F32)],
-        (steps, rows, COL_BLOCK),
-        steps,
         price(rows, width, fits),
         [pltpu.VMEM((fits, rows), BF16)],
     )
@@ -197,16 +189,13 @@
     rows, width = own.shape[0], design.shape[1]
     fits = own.shape[1]
     half = width // 2
-    steps = half // COL_BLOCK
     follow = prior is not None
 
     def kernel(s, d, own_ref, other_ref, begun_ref, norm_ref, *rest):
         prior_ref = ratio_ref = None
         if follow:
             prior_ref, ratio_ref, *rest = rest
-        out, image, turned, norm, held, sems = rest
-        fetch = fetcher(d, held, sems, rows, rows, s[0] * half, COL_BLOCK)
-        started(fetch, steps)
+        out, image, turned, norm = rest
         total = joined(own_ref, other_ref, prior_ref, ratio_ref)
         image[...] = total
         turned[...] = total.astype(BF16).T
@@ -219,16 +208,16 @@
         below = jnp.where(row == 0, high, jnp.where(row == 1, middle, low))
         out[pl.ds(half, EXTRA), :] = jnp.where(row < 3, below, 0.0).astype(BF16)
 
-        @pl.loop(0, steps)
+        @pl.loop(0, half // COL_BLOCK)
         def _(i):
-            fetch(i).wait()
-            where = pl.multiple_of(s[0] * half + i * COL_BLOCK, COL_BLOCK)
-            product = jnp.dot(turned[...], held[i], preferred_element_type=F32).T
-            product = product + begun_ref[pl.ds(where, COL_BLOCK), :]
-            out[pl.ds(pl.multiple_of(i * COL_BLOCK, COL_BLOCK), COL_BLOCK), :] = product.astype(BF16)
+            where = aligned(s[0] * half + i * COL_BLOCK, COL_BLOCK)
+            block = d[:, where]
+            product = jnp.dot(turned[...], block, preferred_element_type=F32).T
+            product = product + begun_ref[where, :]
+            out[aligned(i * COL_BLOCK, COL_BLOCK), :] = product.astype(BF16)
 
     args = [side, design, own, other, begun, norm_first]
-    specs = [SCALAR, ANYWHERE, NEAR, NEAR, NEAR, NEAR]
+    specs = [SCALAR, NEAR, NEAR, NEAR, NEAR, NEAR]
     if follow:
         args, specs = args + [prior, ratio], specs + [NEAR, NEAR]
     return called(
@@ -241,8 +230,6 @@
             ((fits, rows), BF16),
             ((1, fits), F32),
         ],
-        (steps, rows, COL_BLOCK),
-        steps,
         price(rows, half, fits),
     )
 
@@ -250,27 +237,20 @@
 def back_kept(side, design, turned, begun):
     fits, rows = turned.shape
     half = design.shape[1] // 2
-    steps = half // COL_BLOCK
-
-    def kernel(s, d, t, begun_ref, out, held, sems):
-        fetch = fetcher(d, held, sems, rows, rows, s[0] * half, COL_BLOCK)
-        started(fetch, steps)
-
-        @pl.loop(0, steps)
+
+    def kernel(s, d, t, begun_ref, out):
+        @pl.loop(0, half // COL_BLOCK)
         def _(i):
-            fetch(i).wait()
-            where = pl.multiple_of(s[0] * half + i * COL_BLOCK, COL_BLOCK)
-            product = jnp.dot(t[...], held[i], preferred_element_type=F32).T
-            product = product + begun_ref[pl.ds(where, COL_BLOCK), :]
-            out[pl.ds(pl.multiple_of(i * COL_BLOCK, COL_BLOCK), COL_BLOCK), :] = product
+            where = aligned(s[0] * half + i * COL_BLOCK, COL_BLOCK)
+            block = d[:, where]
+            product = jnp.dot(t[...], block, preferred_element_type=F32).T
+            out[aligned(i * COL_BLOCK, COL_BLOCK), :] = product + begun_ref[where, :]
 
     return called(
         kernel,
         [side, design, turned, begun],
-        [SCALAR, ANYWHERE, NEAR, NEAR],
+        [SCALAR, NEAR, NEAR, NEAR],
         [((half, fits), F32)],
-        (steps, rows, COL_BLOCK),
-        steps,
         price(rows, half, fits),
     )[0]
 
@@ -325,6 +305,7 @@
     arrived = swapped(given, CORE)
     kept = start_back(mine, design, targets)
     both = (kept.astype(F32) + arrived.astype(F32)).astype(BF16)
+    both, square, weight = lax.optimization_barrier((both, square, weight))
     share = exchanged(both.reshape(chips, rows, fits)).astype(F32).sum(axis=0)
     back = whole_half(share, square)
     gradient = back.astype(F32)
@@ -335,7 +316,9 @@
     alpha = ratio = gamma = None
     moved, image = [None, None], [None, None]
     for step in range(ITERS):
-        moved_first, short_first = image_step(design, back, 0, moved[0], alpha)
+        moved_first, short_first, rows_first = image_step(
+            design, back, 0, moved[0], alpha
+        )
         other_first = swapped(short_first, COLS)
         short_first, back = lax.optimization_barrier((short_first, back))
         if step:
@@ -343,7 +326,7 @@
         part = weighed(gradient)
         part, back, gradient = lax.optimization_barrier((part, back, gradient))
         gamma_new = part + swapped(part, COLS)
-        moved_second, short_second = image_step(design, back, 1, moved[1], alpha)
+        moved_second, short_second, rows_second = image_step(design, back, 1, moved[1], alpha)
         other_second = swapped(short_second, COLS)
         moved = [moved_first, moved_second]
         if step:
@@ -363,12 +346,14 @@
             )
         gamma = gamma_new
         if step + 1 < ITERS:
-            begun, image_first, norm = back_first(design, short_first, other_first, image[0], ratio)
+            begun, image_first, norm = back_first(
+                rows_first, short_first, other_first, image[0], ratio
+            )
             given, image_second, turned, norm = back_given(
-                theirs, design, short_second, other_second, image[1], ratio, begun, norm
+                theirs, rows_second, short_second, other_second, image[1], ratio, begun, norm
             )
             arrived = swapped(given, CORE)
-            kept = back_kept(mine, design, turned, begun)
+            kept = back_kept(mine, rows_second, turned, begun)
             image = [image_first, image_second]
             both = (kept + arrived[:half].astype(F32)).astype(BF16)
             norms = norm + jnp.sum(arrived[half:].astype(F32), axis=0, keepdims=True)

time: 399 us -> 382 us (0.957)
  waiting for transfers between devices: 61.2 us -> 45.6 us
  Pallas kernels: 103 us -> 89.6 us
  blocking collectives: 149 us -> 161 us
  starting transfers between devices: 66.8 us -> 61.4 us
  other arithmetic: 12.2 us -> 17.3 us
    pallas_call x29, Pallas kernels: 103 us -> 89.6 us  [called(): pl.pallas_call(kernel, in_specs=specs, out_specs=[NEAR] * len(outs), out_...]
    all_to_all x10 -> x11, blocking collectives: 135 us -> 147 us  [exchanged(): lax.all_to_all(pieces, CHIPS, split_axis=0, concat_axis=0, tiled=True)]
    all_to_all x2 -> x1, starting transfers between devices: 13.9 us -> 4.59 us  [exchanged(): lax.all_to_all(pieces, CHIPS, split_axis=0, concat_axis=0, tiled=True)]
    all_to_all x2 -> x1, waiting for transfers between devices: 16.1 us -> 6.82 us  [exchanged(): lax.all_to_all(pieces, CHIPS, split_axis=0, concat_axis=0, tiled=True)]
    ppermute x30, waiting for transfers between devices: 45.1 us -> 38.8 us  [swapped(): return lax.ppermute(array, axis, ((0, 1), (1, 0)))]
  transfers between devices with their start and end apart: 32 -> 31, of which waited for: 15 -> 19; matrix products, arithmetic and copies ran while one was open for 2% -> 3% of each run, Pallas kernels for 11% -> 10%
where the time goes in v4:
time: 382 us
  blocking collectives  161 us (42%)
  Pallas kernels  89.6 us (23%)
  starting transfers between devices  61.4 us (16%)
  waiting for transfers between devices  45.6 us (12%)
  other arithmetic  17.3 us (5%)
    all_to_all x11, blocking collectives, exchanged(): lax.all_to_all(pieces, CHIPS, split_axis=0, concat_axis=0, tiled=True)  147 us
    pallas_call x29, Pallas kernels, called(): pl.pallas_call(kernel, in_specs=specs, out_specs=[NEAR] * len(outs), out_...  89.6 us
    ppermute x30, starting transfers between devices, swapped(): return lax.ppermute(array, axis, ((0, 1), (1, 0)))  56.8 us
    ppermute x30, waiting for transfers between devices, swapped(): return lax.ppermute(array, axis, ((0, 1), (1, 0)))  38.8 us
    all_to_all x1, blocking collectives, per_device(): lax.all_to_all(copies, ROWS, split_axis=0, concat_axis=0, tiled=True)  13.3 us
  transfers between devices with their start and end apart: 31, of which 19 were waited for; matrix products, arithmetic and copies ran while one was open for 3% of the time, Pallas kernels for 10%

profile of v4, /device:TPU:1, one launch (start us, length us, event | category | flops | bytes accessed | tf_op | source)
XLA Modules:
  0.0 381.6 jit_solution(18033311477401558706)
XLA Ops:
  1.7 3.8 shard_map.51
  6.9 3.8 shard_map.50
  10.9 18.1 %all_to_all.65 = bf16[32,48,128]{2,1,0:T(8,128)(2,1)S(1)} all-to-all(bf16[32,48,128]{2,1,0:T(8,128)(2,1)S(1)} %bitcast.145), channel_id=1, replica_groups=mesh['rows_0'=2,'rows_1'=4,'rows_2'=4,'rows_3'=2,'cols'=2] {'rows_0','ro..., dimensions={0} | all-to-all | bytes 786432 | tf_op jit(solution)/shard_map/all_to_all | solution.py:259
  29.2 12.7 %all_to_all.66 = bf16[32,48,128]{2,1,0:T(8,128)(2,1)S(1)} all-to-all(bf16[32,48,128]{2,1,0:T(8,128)(2,1)S(1)} %broadcast_in_dim.87), channel_id=1, replica_groups=mesh['rows_0'=2,'rows_1'=4,'rows_2'=4,'rows_3'=2,'cols'=2] {'rows_0','ro..., dimensions={0} | all-to-all | bytes 786432 | tf_op jit(solution)/shard_map/all_to_all | solution.py:259
  42.0 2.7 collective-permute-start.1
  47.5 4.1 %shard_map.52 = (f32[1024,128]{1,0:T(8,128)S(1)}, bf16[1024,128]{1,0:T(8,128)(2,1)S(1)}, bf16[1024,3072]{1,0:T(8,128)(2,1)S(1)}) custom-call(bf16[2048,3072]{1,0:T(8,128)(2,1)} %d.27, bf16[3072,128]{1,0:T(8,128)(2,1)S(1)} %get-tuple-element.160.v), custom_call_target="tpu_custom_call" | custom-call | flops 805306368 | bytes 6291456 | tf_op jit(solution)/shard_map/pallas_call | solution.py:44
  51.5 2.5 collective-permute-start.4
  54.5 4.1 %shard_map.53 = (f32[1024,128]{1,0:T(8,128)S(1)}, bf16[1024,128]{1,0:T(8,128)(2,1)S(1)}, bf16[1024,3072]{1,0:T(8,128)(2,1)S(1)}) custom-call(bf16[2048,3072]{1,0:T(8,128)(2,1)} %d.27, bf16[3072,128]{1,0:T(8,128)(2,1)S(1)} %get-tuple-element.160.v), custom_call_target="tpu_custom_call" | custom-call | flops 805306368 | bytes 6291456 | tf_op jit(solution)/shard_map/pallas_call | solution.py:44
  60.6 2.7 shard_map.54
  63.3 4.1 %collective-permute-done.3.other_ref = bf16[1024,128]{1,0:T(8,128)(2,1)S(1)} collective-permute-done((bf16[1024,128]{1,0:T(8,128)(2,1)S(1)}, bf16[1024,128]{1,0:T(8,128)(2,1)S(1)}, u32[]{:S(2)}, u32[]{:S(2)}) %collective-permute-start.3) | collective-permute-done | bytes 262176 | tf_op jit(solution)/shard_map/ppermute | solution.py:25
  72.0 13.0 %all_to_all.67 = bf16[32,56,128]{2,1,0:T(8,128)(2,1)S(1)} all-to-all(bf16[32,56,128]{2,1,0:T(8,128)(2,1)S(1)} %pad_maximum_fusion.7), channel_id=1, replica_groups=mesh['rows_0'=2,'rows_1'=4,'rows_2'=4,'rows_3'=2,'cols'=2] {'rows_0','ro..., dimensions={0} | all-to-all | bytes 917504 | tf_op jit(solution)/shard_map/all_to_all | solution.py:259
  86.0 4.6 %all-to-all-start.3 = ((bf16[32,48,128]{2,1,0:T(8,128)(2,1)}), bf16[32,48,128]{2,1,0:T(8,128)(2,1)}, u32[]{:S(2)}, u32[]{:S(2)}) async-start(bf16[32,48,128]{2,1,0:T(8,128)(2,1)} %broadcast_in_dim.92), calls=%async_computation.3 | async-start | bytes 786432 | tf_op jit(solution)/shard_map/all_to_all | solution.py:259
  92.3 6.8 %all-to-all-done.3 = bf16[32,48,128]{2,1,0:T(8,128)(2,1)} async-done(((bf16[32,48,128]{2,1,0:T(8,128)(2,1)}), bf16[32,48,128]{2,1,0:T(8,128)(2,1)}, u32[]{:S(2)}, u32[]{:S(2)}) %all-to-all-start.3) | async-done | bytes 393248 | tf_op jit(solution)/shard_map/all_to_all | solution.py:259
  99.1 3.3 collective-permute-start.6
  105.1 4.2 %shard_map.57 = (f32[1024,128]{1,0:T(8,128)S(1)}, bf16[1024,128]{1,0:T(8,128)(2,1)S(1)}, bf16[1024,3072]{1,0:T(8,128)(2,1)S(1)}) custom-call(bf16[2048,3072]{1,0:T(8,128)(2,1)} %d.27, bf16[3072,128]{1,0:T(8,128)(2,1)S(1)} %pad_maximum_fusion.2.v, f32[1024,128]{1,0:T(8,128)S(1)} %get-tuple-element.173.rest_0_, f32[1,128]{1,0:T(1,128)S(1)} %get-tuple-element.336.rest_1_), custom_call_target="tpu_custom_call" | custom-call | flops 805306368 | bytes 6291456 | tf_op jit(solution)/shard_map/pallas_call | solution.py:44
  112.3 4.1 %shard_map.58 = (f32[1024,128]{1,0:T(8,128)S(1)}, bf16[1024,128]{1,0:T(8,128)(2,1)S(1)}, bf16[1024,3072]{1,0:T(8,128)(2,1)S(1)}) custom-call(bf16[2048,3072]{1,0:T(8,128)(2,1)} %d.27, bf16[3072,128]{1,0:T(8,128)(2,1)S(1)} %pad_maximum_fusion.2.v, f32[1024,128]{1,0:T(8,128)S(1)} %get-tuple-element.177.rest_0_, f32[1,128]{1,0:T(1,128)S(1)} %get-tuple-element.336.rest_1_), custom_call_target="tpu_custom_call" | custom-call | flops 805306368 | bytes 6291456 | tf_op jit(solution)/shard_map/pallas_call | solution.py:44
  120.4 4.9 %collective-permute-done.7 = f32[1,128]{1,0:T(1,128)S(1)} collective-permute-done((f32[1,128]{1,0:T(1,128)S(1)}, f32[1,128]{1,0:T(1,128)S(1)}, u32[]{:S(2)}, u32[]{:S(2)}) %collective-permute-start.7) | collective-permute-done | bytes 544 | tf_op jit(solution)/shard_map/ppermute | solution.py:25
  126.3 2.7 shard_map.59
  133.9 13.0 %all_to_all.68 = bf16[32,56,128]{2,1,0:T(8,128)(2,1)S(1)} all-to-all(bf16[32,56,128]{2,1,0:T(8,128)(2,1)S(1)} %pad_maximum_fusion.8), channel_id=1, replica_groups=mesh['rows_0'=2,'rows_1'=4,'rows_2'=4,'rows_3'=2,'cols'=2] {'rows_0','ro..., dimensions={0} | all-to-all | bytes 917504 | tf_op jit(solution)/shard_map/all_to_all | solution.py:259
  147.1 12.8 %all_to_all.69 = bf16[32,48,128]{2,1,0:T(8,128)(2,1)S(1)} all-to-all(bf16[32,48,128]{2,1,0:T(8,128)(2,1)S(1)} %broadcast_in_dim.97), channel_id=1, replica_groups=mesh['rows_0'=2,'rows_1'=4,'rows_2'=4,'rows_3'=2,'cols'=2] {'rows_0','ro..., dimensions={0} | all-to-all | bytes 786432 | tf_op jit(solution)/shard_map/all_to_all | solution.py:259
  159.9 3.0 collective-permute-start.11
  164.4 4.2 %shard_map.62 = (f32[1024,128]{1,0:T(8,128)S(1)}, bf16[1024,128]{1,0:T(8,128)(2,1)S(1)}, bf16[1024,3072]{1,0:T(8,128)(2,1)S(1)}) custom-call(bf16[2048,3072]{1,0:T(8,128)(2,1)} %d.27, bf16[3072,128]{1,0:T(8,128)(2,1)S(1)} %pad_maximum_fusion.3.v, f32[1024,128]{1,0:T(8,128)S(1)} %get-tuple-element.198.rest_0_, f32[1,128]{1,0:T(1,128)S(1)} %bitcast_divide_fusion.4.rest_1_), custom_call_target="tpu_custom_call" | custom-call | flops 805306368 | bytes 6291456 | tf_op jit(solution)/shard_map/pallas_call | solution.py:44
  168.7 2.4 collective-permute-start.14
  171.6 4.2 %shard_map.63 = (f32[1024,128]{1,0:T(8,128)S(1)}, bf16[1024,128]{1,0:T(8,128)(2,1)S(1)}, bf16[1024,3072]{1,0:T(8,128)(2,1)S(1)}) custom-call(bf16[2048,3072]{1,0:T(8,128)(2,1)} %d.27, bf16[3072,128]{1,0:T(8,128)(2,1)S(1)} %pad_maximum_fusion.3.v, f32[1024,128]{1,0:T(8,128)S(1)} %get-tuple-element.202.rest_0_, f32[1,128]{1,0:T(1,128)S(1)} %bitcast_divide_fusion.4.rest_1_), custom_call_target="tpu_custom_call" | custom-call | flops 805306368 | bytes 6291456 | tf_op jit(solution)/shard_map/pallas_call | solution.py:44
  179.4 5.2 %collective-permute-done.12 = f32[1,128]{1,0:T(1,128)S(1)} collective-permute-done((f32[1,128]{1,0:T(1,128)S(1)}, f32[1,128]{1,0:T(1,128)S(1)}, u32[]{:S(2)}, u32[]{:S(2)}) %collective-permute-start.12) | collective-permute-done | bytes 544 | tf_op jit(solution)/shard_map/ppermute | solution.py:25
  184.8 2.7 shard_map.64
  192.2 13.0 %all_to_all.70 = bf16[32,56,128]{2,1,0:T(8,128)(2,1)S(1)} all-to-all(bf16[32,56,128]{2,1,0:T(8,128)(2,1)S(1)} %pad_maximum_fusion.9), channel_id=1, replica_groups=mesh['rows_0'=2,'rows_1'=4,'rows_2'=4,'rows_3'=2,'cols'=2] {'rows_0','ro..., dimensions={0} | all-to-all | bytes 917504 | tf_op jit(solution)/shard_map/all_to_all | solution.py:259
  205.5 12.8 %all_to_all.71 = bf16[32,48,128]{2,1,0:T(8,128)(2,1)S(1)} all-to-all(bf16[32,48,128]{2,1,0:T(8,128)(2,1)S(1)} %broadcast_in_dim.102), channel_id=1, replica_groups=mesh['rows_0'=2,'rows_1'=4,'rows_2'=4,'rows_3'=2,'cols'=2] {'rows_0','ro..., dimensions={0} | all-to-all | bytes 786432 | tf_op jit(solution)/shard_map/all_to_all | solution.py:259
  218.2 3.0 collective-permute-start.16
  222.8 4.1 %shard_map.67 = (f32[1024,128]{1,0:T(8,128)S(1)}, bf16[1024,128]{1,0:T(8,128)(2,1)S(1)}, bf16[1024,3072]{1,0:T(8,128)(2,1)S(1)}) custom-call(bf16[2048,3072]{1,0:T(8,128)(2,1)} %d.27, bf16[3072,128]{1,0:T(8,128)(2,1)S(1)} %pad_maximum_fusion.4.v, f32[1024,128]{1,0:T(8,128)S(1)} %get-tuple-element.227.rest_0_, f32[1,128]{1,0:T(1,128)S(1)} %bitcast_divide_fusion.3.rest_1_), custom_call_target="tpu_custom_call" | custom-call | flops 805306368 | bytes 6291456 | tf_op jit(solution)/shard_map/pallas_call | solution.py:44
  228.8 4.1 %shard_map.68 = (f32[1024,128]{1,0:T(8,128)S(1)}, bf16[1024,128]{1,0:T(8,128)(2,1)S(1)}, bf16[1024,3072]{1,0:T(8,128)(2,1)S(1)}) custom-call(bf16[2048,3072]{1,0:T(8,128)(2,1)} %d.27, bf16[3072,128]{1,0:T(8,128)(2,1)S(1)} %pad_maximum_fusion.4.v, f32[1024,128]{1,0:T(8,128)S(1)} %get-tuple-element.231.rest_0_, f32[1,128]{1,0:T(1,128)S(1)} %bitcast_divide_fusion.3.rest_1_), custom_call_target="tpu_custom_call" | custom-call | flops 805306368 | bytes 6291456 | tf_op jit(solution)/shard_map/pallas_call | solution.py:44
  236.5 5.2 %collective-permute-done.17 = f32[1,128]{1,0:T(1,128)S(1)} collective-permute-done((f32[1,128]{1,0:T(1,128)S(1)}, f32[1,128]{1,0:T(1,128)S(1)}, u32[]{:S(2)}, u32[]{:S(2)}) %collective-permute-start.17) | collective-permute-done | bytes 544 | tf_op jit(solution)/shard_map/ppermute | solution.py:25
  241.9 2.7 shard_map.69
  249.3 13.0 %all_to_all.72 = bf16[32,56,128]{2,1,0:T(8,128)(2,1)S(1)} all-to-all(bf16[32,56,128]{2,1,0:T(8,128)(2,1)S(1)} %pad_maximum_fusion.10), channel_id=1, replica_groups=mesh['rows_0'=2,'rows_1'=4,'rows_2'=4,'rows_3'=2,'cols'=2] {'rows_0','ro..., dimensions={0} | all-to-all | bytes 917504 | tf_op jit(solution)/shard_map/all_to_all | solution.py:259
  262.6 13.0 %all_to_all.73 = bf16[32,48,128]{2,1,0:T(8,128)(2,1)S(1)} all-to-all(bf16[32,48,128]{2,1,0:T(8,128)(2,1)S(1)} %broadcast_in_dim.107), channel_id=1, replica_groups=mesh['rows_0'=2,'rows_1'=4,'rows_2'=4,'rows_3'=2,'cols'=2] {'rows_0','ro..., dimensions={0} | all-to-all | bytes 786432 | tf_op jit(solution)/shard_map/all_to_all | solution.py:259
  275.6 3.0 collective-permute-start.21
  280.1 4.1 %shard_map.72 = (f32[1024,128]{1,0:T(8,128)S(1)}, bf16[1024,128]{1,0:T(8,128)(2,1)S(1)}, bf16[1024,3072]{1,0:T(8,128)(2,1)S(1)}) custom-call(bf16[2048,3072]{1,0:T(8,128)(2,1)} %d.27, bf16[3072,128]{1,0:T(8,128)(2,1)S(1)} %pad_maximum_fusion.5.v, f32[1024,128]{1,0:T(8,128)S(1)} %get-tuple-element.256.rest_0_, f32[1,128]{1,0:T(1,128)S(1)} %bitcast_divide_fusion.2.rest_1_), custom_call_target="tpu_custom_call" | custom-call | flops 805306368 | bytes 6291456 | tf_op jit(solution)/shard_map/pallas_call | solution.py:44
  284.2 2.4 collective-permute-start.24
  288.3 4.1 %shard_map.73 = (f32[1024,128]{1,0:T(8,128)S(1)}, bf16[1024,128]{1,0:T(8,128)(2,1)S(1)}, bf16[1024,3072]{1,0:T(8,128)(2,1)S(1)}) custom-call(bf16[2048,3072]{1,0:T(8,128)(2,1)} %d.27, bf16[3072,128]{1,0:T(8,128)(2,1)S(1)} %pad_maximum_fusion.5.v, f32[1024,128]{1,0:T(8,128)S(1)} %get-tuple-element.260.rest_0_, f32[1,128]{1,0:T(1,128)S(1)} %bitcast_divide_fusion.2.rest_1_), custom_call_target="tpu_custom_call" | custom-call | flops 805306368 | bytes 6291456 | tf_op jit(solution)/shard_map/pallas_call | solution.py:44
  296.8 4.4 %collective-permute-done.22 = f32[1,128]{1,0:T(1,128)S(1)} collective-permute-done((f32[1,128]{1,0:T(1,128)S(1)}, f32[1,128]{1,0:T(1,128)S(1)}, u32[]{:S(2)}, u32[]{:S(2)}) %collective-permute-start.22) | collective-permute-done | bytes 544 | tf_op jit(solution)/shard_map/ppermute | solution.py:25
  301.4 2.7 shard_map.74
  308.8 13.0 %all_to_all.74 = bf16[32,56,128]{2,1,0:T(8,128)(2,1)S(1)} all-to-all(bf16[32,56,128]{2,1,0:T(8,128)(2,1)S(1)} %pad_maximum_fusion.11), channel_id=1, replica_groups=mesh['rows_0'=2,'rows_1'=4,'rows_2'=4,'rows_3'=2,'cols'=2] {'rows_0','ro..., dimensions={0} | all-to-all | bytes 917504 | tf_op jit(solution)/shard_map/all_to_all | solution.py:259
  322.0 12.8 %all_to_all.75 = bf16[32,48,128]{2,1,0:T(8,128)(2,1)S(1)} all-to-all(bf16[32,48,128]{2,1,0:T(8,128)(2,1)S(1)} %broadcast_in_dim.112), channel_id=1, replica_groups=mesh['rows_0'=2,'rows_1'=4,'rows_2'=4,'rows_3'=2,'cols'=2] {'rows_0','ro..., dimensions={0} | all-to-all | bytes 786432 | tf_op jit(solution)/shard_map/all_to_all | solution.py:259
  334.8 3.0 collective-permute-start.26
  339.3 6.8 %shard_map.77 = (f32[1024,128]{1,0:T(8,128)}, bf16[1024,128]{1,0:T(8,128)(2,1)S(1)}, bf16[1024,3072]{1,0:T(8,128)(2,1)}) custom-call(bf16[2048,3072]{1,0:T(8,128)(2,1)} %d.27, bf16[3072,128]{1,0:T(8,128)(2,1)S(1)} %pad_maximum_fusion.6.v, f32[1024,128]{1,0:T(8,128)S(1)} %get-tuple-element.285.rest_0_, f32[1,128]{1,0:T(1,128)S(1)} %bitcast_divide_fusion.1.rest_1_), custom_call_target="tpu_custom_call" | custom-call | flops 805306368 | bytes 6291456 | tf_op jit(solution)/shard_map/pallas_call | solution.py:44
  348.1 6.8 %shard_map.78 = (f32[1024,128]{1,0:T(8,128)}, bf16[1024,128]{1,0:T(8,128)(2,1)S(1)}, bf16[1024,3072]{1,0:T(8,128)(2,1)}) custom-call(bf16[2048,3072]{1,0:T(8,128)(2,1)} %d.27, bf16[3072,128]{1,0:T(8,128)(2,1)S(1)} %pad_maximum_fusion.6.v, f32[1024,128]{1,0:T(8,128)S(1)} %get-tuple-element.289.rest_0_, f32[1,128]{1,0:T(1,128)S(1)} %bitcast_divide_fusion.1.rest_1_), custom_call_target="tpu_custom_call" | custom-call | flops 805306368 | bytes 6291456 | tf_op jit(solution)/shard_map/pallas_call | solution.py:44
  358.4 5.4 %collective-permute-done.27 = f32[1,128]{1,0:T(1,128)S(1)} collective-permute-done((f32[1,128]{1,0:T(1,128)S(1)}, f32[1,128]{1,0:T(1,128)S(1)}, u32[]{:S(2)}, u32[]{:S(2)}) %collective-permute-start.27) | collective-permute-done | bytes 544 | tf_op jit(solution)/shard_map/ppermute | solution.py:25
  365.2 13.3 %all_to_all.76 = f32[64,1,128]{2,1,0:T(1,128)S(1)} all-to-all(f32[64,1,128]{2,1,0:T(1,128)S(1)} %broadcast_in_dim.114), channel_id=1, replica_groups=mesh['rows_0'=2,'rows_1'=4,'rows_2'=4,'rows_3'=2,'cols'=2] {'rows_0','ro..., dimensions={0} | all-to-all | bytes 65536 | tf_op jit(solution)/shard_map/all_to_all | solution.py:378
  (204 shorter events, 77.4 us)
Async XLA Ops:
  0.6 1.0 copy-start
  1.7 5.2 %copy-start.1 = (bf16[2048,128]{1,0:T(8,128)(2,1)S(1)}, bf16[2048,128]{1,0:T(8,128)(2,1)}, u32[]{:S(2)}) copy-start(bf16[2048,128]{1,0:T(8,128)(2,1)} %v.3) | copy-start | bytes 1572868
  5.5 5.3 %collective-permute-start = (bf16[1536,128]{1,0:T(8,128)(2,1)S(1)}, bf16[1536,128]{1,0:T(8,128)(2,1)S(1)}, u32[]{:S(2)}, u32[]{:S(2)}) collective-permute-start(bf16[1536,128]{1,0:T(8,128)(2,1)S(1)} %shard_map.51), channel_id=1, source_target_pairs={{0,2},{2,0},{1,3},{3,1},{4,6},{6,4},{5,7},{7,5},{8,10},{10,8},{9,1... | collective-permute-start | bytes 1179656 | tf_op jit(solution)/shard_map/ppermute | solution.py:25
  6.9 3.8 copy-start.8
  10.8 136.2 %copy-start.9 = (f32[48,1]{0,1:T(1,128)}, f32[48,1]{0,1:T(1,128)S(1)}, u32[]{:S(2)}) copy-start(f32[48,1]{0,1:T(1,128)S(1)} %multiply_bitcast_fusion) | copy-start | bytes 580
  42.0 4.1 %collective-permute-start.1 = (bf16[1536,128]{1,0:T(8,128)(2,1)S(1)}, bf16[1536,128]{1,0:T(8,128)(2,1)S(1)}, u32[]{:S(2)}, u32[]{:S(2)}) collective-permute-start(bf16[1536,128]{1,0:T(8,128)(2,1)S(1)} %bitcast.144), channel_id=1, source_target_pairs={{0,2},{2,0},{1,3},{3,1},{4,6},{6,4},{5,7},{7,5},{8,10},{10,8},{9,1... | collective-permute-start | bytes 1179656 | tf_op jit(solution)/shard_map/ppermute | solution.py:25
  51.5 9.1 %collective-permute-start.4 = (bf16[1024,128]{1,0:T(8,128)(2,1)S(1)}, bf16[1024,128]{1,0:T(8,128)(2,1)S(1)}, u32[]{:S(2)}, u32[]{:S(2)}) collective-permute-start(bf16[1024,128]{1,0:T(8,128)(2,1)S(1)} %get-tuple-element.164.own_ref), channel_id=1, source_target_pairs={{0,1},{1,0},{2,3},{3,2},{4,5},{5,4},{6,7},{7,6},{8,9},{9,8},{10,11... | collective-permute-start | bytes 786440 | tf_op jit(solution)/shard_map/ppermute | solution.py:25
  58.6 8.8 %collective-permute-start.3 = (bf16[1024,128]{1,0:T(8,128)(2,1)S(1)}, bf16[1024,128]{1,0:T(8,128)(2,1)S(1)}, u32[]{:S(2)}, u32[]{:S(2)}) collective-permute-start(bf16[1024,128]{1,0:T(8,128)(2,1)S(1)} %get-tuple-element.162.own_ref), channel_id=1, source_target_pairs={{0,1},{1,0},{2,3},{3,2},{4,5},{5,4},{6,7},{7,6},{8,9},{9,8},{10,11... | collective-permute-start | bytes 786440 | tf_op jit(solution)/shard_map/ppermute | solution.py:25
  68.9 2.9 collective-permute-start.5
  86.0 13.1 %all-to-all-start.3 = ((bf16[32,48,128]{2,1,0:T(8,128)(2,1)}), bf16[32,48,128]{2,1,0:T(8,128)(2,1)}, u32[]{:S(2)}, u32[]{:S(2)}) async-start(bf16[32,48,128]{2,1,0:T(8,128)(2,1)} %broadcast_in_dim.92), calls=%async_computation.3 | async-start | bytes 786432 | tf_op jit(solution)/shard_map/all_to_all | solution.py:259
  90.6 88.4 %copy-start.11 = (s32[2]{0:T(128)}, s32[2]{0:T(128)S(1)}, u32[]{:S(2)}) copy-start(s32[2]{0:T(128)S(1)} %iota_add_fusion) | copy-start | bytes 28
  90.6 11.8 %collective-permute-start.2 = (f32[1,128]{1,0:T(1,128)S(1)}, f32[1,128]{1,0:T(1,128)S(1)}, u32[]{:S(2)}, u32[]{:S(2)}) collective-permute-start(f32[1,128]{1,0:T(1,128)S(1)} %bitcast.165), channel_id=1, source_target_pairs={{0,1},{1,0},{2,3},{3,2},{4,5},{5,4},{6,7},{7,6},{8,9},{9,8},{10,11... | collective-permute-start | bytes 1544 | tf_op jit(solution)/shard_map/ppermute | solution.py:25
  99.1 4.9 %collective-permute-start.6 = (bf16[1536,128]{1,0:T(8,128)(2,1)}, bf16[1536,128]{1,0:T(8,128)(2,1)S(1)}, u32[]{:S(2)}, u32[]{:S(2)}) collective-permute-start(bf16[1536,128]{1,0:T(8,128)(2,1)} %bitcast.12), channel_id=1, source_target_pairs={{0,2},{2,0},{1,3},{3,1},{4,6},{6,4},{5,7},{7,5},{8,10},{10,8},{9,1... | collective-permute-start | bytes 1179656 | tf_op jit(solution)/shard_map/ppermute | solution.py:25
  105.1 5.6 %copy-start.3 = (f32[3072,128]{1,0:T(8,128)S(1)}, f32[3072,128]{1,0:T(8,128)}, u32[]{:S(2)}) copy-start(f32[3072,128]{1,0:T(8,128)} %get-tuple-element.172) | copy-start | bytes 4718596
  109.4 16.9 %collective-permute-start.9 = (bf16[1024,128]{1,0:T(8,128)(2,1)S(1)}, bf16[1024,128]{1,0:T(8,128)(2,1)S(1)}, u32[]{:S(2)}, u32[]{:S(2)}) collective-permute-start(bf16[1024,128]{1,0:T(8,128)(2,1)S(1)} %get-tuple-element.189.own_ref), channel_id=1, source_target_pairs={{0,1},{1,0},{2,3},{3,2},{4,5},{5,4},{6,7},{7,6},{8,9},{9,8},{10,11... | collective-permute-start | bytes 786440 | tf_op jit(solution)/shard_map/ppermute | solution.py:25
  116.4 9.9 %collective-permute-start.8 = (bf16[1024,128]{1,0:T(8,128)(2,1)S(1)}, bf16[1024,128]{1,0:T(8,128)(2,1)S(1)}, u32[]{:S(2)}, u32[]{:S(2)}) collective-permute-start(bf16[1024,128]{1,0:T(8,128)(2,1)S(1)} %get-tuple-element.186.own_ref), channel_id=1, source_target_pairs={{0,1},{1,0},{2,3},{3,2},{4,5},{5,4},{6,7},{7,6},{8,9},{9,8},{10,11... | collective-permute-start | bytes 786440 | tf_op jit(solution)/shard_map/ppermute | solution.py:25
  118.2 7.0 %collective-permute-start.7 = (f32[1,128]{1,0:T(1,128)S(1)}, f32[1,128]{1,0:T(1,128)S(1)}, u32[]{:S(2)}, u32[]{:S(2)}) collective-permute-start(f32[1,128]{1,0:T(1,128)S(1)} %bitcast.163), channel_id=1, source_target_pairs={{0,1},{1,0},{2,3},{3,2},{4,5},{5,4},{6,7},{7,6},{8,9},{9,8},{10,11... | collective-permute-start | bytes 1544 | tf_op jit(solution)/shard_map/ppermute | solution.py:25
  130.5 3.2 collective-permute-start.10
  159.9 4.4 %collective-permute-start.11 = (bf16[1536,128]{1,0:T(8,128)(2,1)S(1)}, bf16[1536,128]{1,0:T(8,128)(2,1)S(1)}, u32[]{:S(2)}, u32[]{:S(2)}) collective-permute-start(bf16[1536,128]{1,0:T(8,128)(2,1)S(1)} %bitcast.141), channel_id=1, source_target_pairs={{0,2},{2,0},{1,3},{3,1},{4,6},{6,4},{5,7},{7,5},{8,10},{10,8},{9,1... | collective-permute-start | bytes 1179656 | tf_op jit(solution)/shard_map/ppermute | solution.py:25
  164.4 6.7 %copy-start.2 = (f32[3072,128]{1,0:T(8,128)S(1)}, f32[3072,128]{1,0:T(8,128)}, u32[]{:S(2)}) copy-start(f32[3072,128]{1,0:T(8,128)} %get-tuple-element.197) | copy-start | bytes 4718596
  168.7 16.1 %collective-permute-start.14 = (bf16[1024,128]{1,0:T(8,128)(2,1)S(1)}, bf16[1024,128]{1,0:T(8,128)(2,1)S(1)}, u32[]{:S(2)}, u32[]{:S(2)}) collective-permute-start(bf16[1024,128]{1,0:T(8,128)(2,1)S(1)} %get-tuple-element.218.own_ref), channel_id=1, source_target_pairs={{0,1},{1,0},{2,3},{3,2},{4,5},{5,4},{6,7},{7,6},{8,9},{9,8},{10,11... | collective-permute-start | bytes 786440 | tf_op jit(solution)/shard_map/ppermute | solution.py:25
  171.6 7.2 %copy-start.6 = (f32[1024,128]{1,0:T(8,128)S(1)}, f32[1024,128]{1,0:T(8,128)}, u32[]{:S(2)}) copy-start(f32[1024,128]{1,0:T(8,128)} %get-tuple-element.184) | copy-start | bytes 1572868
  175.8 9.0 %collective-permute-start.13 = (bf16[1024,128]{1,0:T(8,128)(2,1)S(1)}, bf16[1024,128]{1,0:T(8,128)(2,1)S(1)}, u32[]{:S(2)}, u32[]{:S(2)}) collective-permute-start(bf16[1024,128]{1,0:T(8,128)(2,1)S(1)} %get-tuple-element.215.own_ref), channel_id=1, source_target_pairs={{0,1},{1,0},{2,3},{3,2},{4,5},{5,4},{6,7},{7,6},{8,9},{9,8},{10,11... | collective-permute-start | bytes 786440 | tf_op jit(solution)/shard_map/ppermute | solution.py:25
  176.5 8.2 %copy-start.7 = (f32[2,3072]{1,0:T(2,128)S(1)}, f32[2,3072]{1,0:T(2,128)}, u32[]{:S(2)}) copy-start(f32[2,3072]{1,0:T(2,128)} %get-tuple-element.207) | copy-start | bytes 73732
  176.5 8.1 %collective-permute-start.12 = (f32[1,128]{1,0:T(1,128)S(1)}, f32[1,128]{1,0:T(1,128)S(1)}, u32[]{:S(2)}, u32[]{:S(2)}) collective-permute-start(f32[1,128]{1,0:T(1,128)S(1)} %bitcast.157), channel_id=1, source_target_pairs={{0,1},{1,0},{2,3},{3,2},{4,5},{5,4},{6,7},{7,6},{8,9},{9,8},{10,11... | collective-permute-start | bytes 1544 | tf_op jit(solution)/shard_map/ppermute | solution.py:25
  184.6 36.7 %copy-start.13 = (f32[1,128]{1,0:T(1,128)}, f32[1,128]{1,0:T(1,128)S(1)}, u32[]{:S(2)}) copy-start(f32[1,128]{1,0:T(1,128)S(1)} %get-tuple-element.329) | copy-start | bytes 1540
  189.0 3.0 collective-permute-start.15
  192.1 13.2 %copy-start.10 = (f32[48,1]{0,1:T(1,128)S(1)}, f32[48,1]{0,1:T(1,128)}, u32[]{:S(2)}) copy-start(f32[48,1]{0,1:T(1,128)} %copy-done.9) | copy-start | bytes 580
  218.2 4.4 %collective-permute-start.16 = (bf16[1536,128]{1,0:T(8,128)(2,1)S(1)}, bf16[1536,128]{1,0:T(8,128)(2,1)S(1)}, u32[]{:S(2)}, u32[]{:S(2)}) collective-permute-start(bf16[1536,128]{1,0:T(8,128)(2,1)S(1)} %bitcast.142), channel_id=1, source_target_pairs={{0,2},{2,0},{1,3},{3,1},{4,6},{6,4},{5,7},{7,5},{8,10},{10,8},{9,1... | collective-permute-start | bytes 1179656 | tf_op jit(solution)/shard_map/ppermute | solution.py:25
  226.9 15.0 %collective-permute-start.19 = (bf16[1024,128]{1,0:T(8,128)(2,1)S(1)}, bf16[1024,128]{1,0:T(8,128)(2,1)S(1)}, u32[]{:S(2)}, u32[]{:S(2)}) collective-permute-start(bf16[1024,128]{1,0:T(8,128)(2,1)S(1)} %get-tuple-element.247.own_ref), channel_id=1, source_target_pairs={{0,1},{1,0},{2,3},{3,2},{4,5},{5,4},{6,7},{7,6},{8,9},{9,8},{10,11... | collective-permute-start | bytes 786440 | tf_op jit(solution)/shard_map/ppermute | solution.py:25
  232.9 9.0 %collective-permute-start.18 = (bf16[1024,128]{1,0:T(8,128)(2,1)S(1)}, bf16[1024,128]{1,0:T(8,128)(2,1)S(1)}, u32[]{:S(2)}, u32[]{:S(2)}) collective-permute-start(bf16[1024,128]{1,0:T(8,128)(2,1)S(1)} %get-tuple-element.244.own_ref), channel_id=1, source_target_pairs={{0,1},{1,0},{2,3},{3,2},{4,5},{5,4},{6,7},{7,6},{8,9},{9,8},{10,11... | collective-permute-start | bytes 786440 | tf_op jit(solution)/shard_map/ppermute | solution.py:25
  234.6 1.5 copy-start.12
  234.6 7.1 %copy-start.14 = (f32[1,128]{1,0:T(1,128)S(1)}, f32[1,128]{1,0:T(1,128)}, u32[]{:S(2)}) copy-start(f32[1,128]{1,0:T(1,128)} %copy-done.13) | copy-start | bytes 1540
  234.6 7.1 %collective-permute-start.17 = (f32[1,128]{1,0:T(1,128)S(1)}, f32[1,128]{1,0:T(1,128)S(1)}, u32[]{:S(2)}, u32[]{:S(2)}) collective-permute-start(f32[1,128]{1,0:T(1,128)S(1)} %bitcast.159), channel_id=1, source_target_pairs={{0,1},{1,0},{2,3},{3,2},{4,5},{5,4},{6,7},{7,6},{8,9},{9,8},{10,11... | collective-permute-start | bytes 1544 | tf_op jit(solution)/shard_map/ppermute | solution.py:25
  246.1 3.0 collective-permute-start.20
  275.6 4.4 %collective-permute-start.21 = (bf16[1536,128]{1,0:T(8,128)(2,1)S(1)}, bf16[1536,128]{1,0:T(8,128)(2,1)S(1)}, u32[]{:S(2)}, u32[]{:S(2)}) collective-permute-start(bf16[1536,128]{1,0:T(8,128)(2,1)S(1)} %bitcast.143), channel_id=1, source_target_pairs={{0,2},{2,0},{1,3},{3,1},{4,6},{6,4},{5,7},{7,5},{8,10},{10,8},{9,1... | collective-permute-start | bytes 1179656 | tf_op jit(solution)/shard_map/ppermute | solution.py:25
  284.2 17.1 %collective-permute-start.24 = (bf16[1024,128]{1,0:T(8,128)(2,1)S(1)}, bf16[1024,128]{1,0:T(8,128)(2,1)S(1)}, u32[]{:S(2)}, u32[]{:S(2)}) collective-permute-start(bf16[1024,128]{1,0:T(8,128)(2,1)S(1)} %get-tuple-element.276.own_ref), channel_id=1, source_target_pairs={{0,1},{1,0},{2,3},{3,2},{4,5},{5,4},{6,7},{7,6},{8,9},{9,8},{10,11... | collective-permute-start | bytes 786440 | tf_op jit(solution)/shard_map/ppermute | solution.py:25
  292.4 9.0 %collective-permute-start.23 = (bf16[1024,128]{1,0:T(8,128)(2,1)S(1)}, bf16[1024,128]{1,0:T(8,128)(2,1)S(1)}, u32[]{:S(2)}, u32[]{:S(2)}) collective-permute-start(bf16[1024,128]{1,0:T(8,128)(2,1)S(1)} %get-tuple-element.273.own_ref), channel_id=1, source_target_pairs={{0,1},{1,0},{2,3},{3,2},{4,5},{5,4},{6,7},{7,6},{8,9},{9,8},{10,11... | collective-permute-start | bytes 786440 | tf_op jit(solution)/shard_map/ppermute | solution.py:25
  293.0 8.1 %collective-permute-start.22 = (f32[1,128]{1,0:T(1,128)S(1)}, f32[1,128]{1,0:T(1,128)S(1)}, u32[]{:S(2)}, u32[]{:S(2)}) collective-permute-start(f32[1,128]{1,0:T(1,128)S(1)} %bitcast.161), channel_id=1, source_target_pairs={{0,1},{1,0},{2,3},{3,2},{4,5},{5,4},{6,7},{7,6},{8,9},{9,8},{10,11... | collective-permute-start | bytes 1544 | tf_op jit(solution)/shard_map/ppermute | solution.py:25
  305.6 3.0 collective-permute-start.25
  334.8 4.4 %collective-permute-start.26 = (bf16[1536,128]{1,0:T(8,128)(2,1)S(1)}, bf16[1536,128]{1,0:T(8,128)(2,1)S(1)}, u32[]{:S(2)}, u32[]{:S(2)}) collective-permute-start(bf16[1536,128]{1,0:T(8,128)(2,1)S(1)} %bitcast.140), channel_id=1, source_target_pairs={{0,2},{2,0},{1,3},{3,1},{4,6},{6,4},{5,7},{7,5},{8,10},{10,8},{9,1... | collective-permute-start | bytes 1179656 | tf_op jit(solution)/shard_map/ppermute | solution.py:25
  339.3 8.3 %copy-start.4 = (f32[3072,128]{1,0:T(8,128)S(1)}, f32[3072,128]{1,0:T(8,128)}, u32[]{:S(2)}) copy-start(f32[3072,128]{1,0:T(8,128)} %get-tuple-element.284) | copy-start | bytes 4718596
  346.2 17.8 %collective-permute-start.29 = (bf16[1024,128]{1,0:T(8,128)(2,1)S(1)}, bf16[1024,128]{1,0:T(8,128)(2,1)S(1)}, u32[]{:S(2)}, u32[]{:S(2)}) collective-permute-start(bf16[1024,128]{1,0:T(8,128)(2,1)S(1)} %get-tuple-element.300), channel_id=1, source_target_pairs={{0,1},{1,0},{2,3},{3,2},{4,5},{5,4},{6,7},{7,6},{8,9},{9,8},{10,11... | collective-permute-start | bytes 786440 | tf_op jit(solution)/shard_map/ppermute | solution.py:25
  348.1 9.8 %copy-start.5 = (f32[1024,128]{1,0:T(8,128)S(1)}, f32[1024,128]{1,0:T(8,128)}, u32[]{:S(2)}) copy-start(f32[1024,128]{1,0:T(8,128)} %get-tuple-element.271) | copy-start | bytes 1572868
  354.9 9.1 %collective-permute-start.28 = (bf16[1024,128]{1,0:T(8,128)(2,1)S(1)}, bf16[1024,128]{1,0:T(8,128)(2,1)}, u32[]{:S(2)}, u32[]{:S(2)}) collective-permute-start(bf16[1024,128]{1,0:T(8,128)(2,1)S(1)} %get-tuple-element.301), channel_id=1, source_target_pairs={{0,1},{1,0},{2,3},{3,2},{4,5},{5,4},{6,7},{7,6},{8,9},{9,8},{10,11... | collective-permute-start | bytes 786440 | tf_op jit(solution)/shard_map/ppermute | solution.py:25
  356.6 7.2 %collective-permute-start.27 = (f32[1,128]{1,0:T(1,128)S(1)}, f32[1,128]{1,0:T(1,128)S(1)}, u32[]{:S(2)}, u32[]{:S(2)}) collective-permute-start(f32[1,128]{1,0:T(1,128)S(1)} %bitcast.155), channel_id=1, source_target_pairs={{0,1},{1,0},{2,3},{3,2},{4,5},{5,4},{6,7},{7,6},{8,9},{9,8},{10,11... | collective-permute-start | bytes 1544 | tf_op jit(solution)/shard_map/ppermute | solution.py:25

commit v5 on v4

--- a/solution.py
+++ b/solution.py
@@ -17,7 +17,7 @@
 ROW_BLOCK = 128
 COL_BLOCK = 512
 START_BLOCK = 256
-FAR_VMEM = 43 * 1024 * 1024
+FAR_VMEM = 42 * 1024 * 1024
 NEAR_VMEM = 8 * 1024 * 1024
 
 
@@ -68,9 +68,8 @@
     return pl.ds(pl.multiple_of(start, size), size)
 
 
-def image_step(design, vector, chunk, moved=None, alpha=None):
-    rows, width = design.shape[0] // 2, design.shape[1]
-    fits = vector.shape[1]
+def image_step(design, vector, begin, rows, keep, moved=None, alpha=None):
+    width, fits = design.shape[1], vector.shape[1]
     steps = rows // ROW_BLOCK
 
     def kernel(d, v, *rest):
@@ -81,7 +80,7 @@
 
         def fetch(i):
             where = aligned(i * ROW_BLOCK, ROW_BLOCK)
-            source = aligned(chunk * rows + i * ROW_BLOCK, ROW_BLOCK)
+            source = aligned(begin + i * ROW_BLOCK, ROW_BLOCK)
             return pltpu.make_async_copy(d.at[source, :], close.at[where, :], sems.at[i])
 
         def work(i):
@@ -97,15 +96,15 @@
     args, specs = [design, vector], [ANYWHERE, NEAR]
     if moved is not None:
         args, specs = args + [moved, alpha], specs + [NEAR, NEAR]
-    return called(
-        kernel,
-        args,
-        specs,
-        [((rows, fits), F32), ((rows, fits), BF16), ((rows, width), BF16)],
-        price(rows, width, fits),
-        [pltpu.SemaphoreType.DMA((steps,))],
-        False,
-    )
+    outs = [((rows, fits), F32), ((rows, fits), BF16)]
+    scratch = [pltpu.SemaphoreType.DMA((steps,))]
+    if keep:
+        outs.append(((rows, width), BF16))
+    else:
+        scratch.insert(0, pltpu.VMEM((rows, width), BF16))
+    cost = price(rows, width, fits)
+    made = called(kernel, args, specs, outs, cost, scratch, False)
+    return made if keep else [*made, None]
 
 
 def start_back(side, design, vectors):
@@ -275,7 +274,8 @@
     core = lax.axis_index(CORE)
     chips = lax.axis_size(CHIPS)
     width, fits = design.shape[1], targets.shape[1]
-    depth = targets.shape[0] // 2
+    total = targets.shape[0]
+    depth = total * 5 // 8
     half = width // 2
     mine = core.astype(jnp.int32).reshape(1)
     theirs = 1 - mine
@@ -308,7 +308,7 @@
     both, square, weight = lax.optimization_barrier((both, square, weight))
     share = exchanged(both.reshape(chips, rows, fits)).astype(F32).sum(axis=0)
     back = whole_half(share, square)
-    gradient = back.astype(F32)
+    gradient = None
     narrow = picked(back)
     narrow_dir = narrow
     narrow_fit = jnp.zeros_like(narrow)
@@ -316,17 +316,22 @@
     alpha = ratio = gamma = None
     moved, image = [None, None], [None, None]
     for step in range(ITERS):
+        keep = step + 1 < ITERS
         moved_first, short_first, rows_first = image_step(
-            design, back, 0, moved[0], alpha
+            design, back, 0, depth, keep, moved[0], alpha
         )
         other_first = swapped(short_first, COLS)
         short_first, back = lax.optimization_barrier((short_first, back))
         if step:
             gradient = gradient - alpha * back.astype(F32)
+        else:
+            gradient = back.astype(F32)
         part = weighed(gradient)
         part, back, gradient = lax.optimization_barrier((part, back, gradient))
         gamma_new = part + swapped(part, COLS)
-        moved_second, short_second, rows_second = image_step(design, back, 1, moved[1], alpha)
+        moved_second, short_second, rows_second = image_step(
+            design, back, depth, total - depth, keep, moved[1], alpha
+        )
         other_second = swapped(short_second, COLS)
         moved = [moved_first, moved_second]
         if step:

time: 382 us -> 372 us (0.974)
  waiting for transfers between devices: 45.6 us -> 40.4 us
  other arithmetic: 17.3 us -> 12.8 us
  Pallas kernels: 89.6 us -> 85.7 us
    pallas_call x29, Pallas kernels: 89.6 us -> 85.7 us  [called(): pl.pallas_call(kernel, in_specs=specs, out_specs=[NEAR] * len(outs), out_...]
  transfers between devices with their start and end apart: 31 -> 31, of which waited for: 19 -> 22; matrix products, arithmetic and copies ran while one was open for 3% -> 3% of each run, Pallas kernels for 10% -> 9%
where the time goes in v5:
time: 372 us; the launch traced here: 371 us
  blocking collectives  161 us (43%)
  Pallas kernels  85.7 us (23%)
  starting transfers between devices  63 us (17%)
  waiting for transfers between devices  40.4 us (11%)
  other arithmetic  12.8 us (3%)
  local copies, waits for them, and re-layouts  4.18 us (1%)
    all_to_all x11, blocking collectives, exchanged(): lax.all_to_all(pieces, CHIPS, split_axis=0, concat_axis=0, tiled=True)  148 us
    pallas_call x29, Pallas kernels, called(): pl.pallas_call(kernel, in_specs=specs, out_specs=[NEAR] * len(outs), out_...  85.7 us
    ppermute x30, starting transfers between devices, swapped(): return lax.ppermute(array, axis, ((0, 1), (1, 0)))  58.7 us
    ppermute x30, waiting for transfers between devices, swapped(): return lax.ppermute(array, axis, ((0, 1), (1, 0)))  35.2 us
    all_to_all x1, blocking collectives, per_device(): lax.all_to_all(copies, ROWS, split_axis=0, concat_axis=0, tiled=True)  13.2 us
  transfers between devices with their start and end apart: 31, of which 22 were waited for; matrix products, arithmetic and copies ran while one was open for 3% of the time, Pallas kernels for 9%

profile of v5, /device:TPU:1, one launch (start us, length us, event | category | flops | bytes accessed | tf_op | source)
XLA Modules:
  0.0 371.3 jit_solution(14544335450291898081)
XLA Ops:
  1.7 3.8 %shard_map.51 = bf16[1536,128]{1,0:T(8,128)(2,1)S(1)} custom-call(s32[1]{0:T(128)S(6)} %sub.104.s, bf16[2048,3072]{1,0:T(8,128)(2,1)} %d.27, bf16[2048,128]{1,0:T(8,128)(2,1)S(1)} %copy-done), custom_call_target="tpu_custom_call" | custom-call | flops 805306368 | bytes 6291456 | tf_op jit(solution)/shard_map/pallas_call | solution.py:44
  6.9 3.8 %shard_map.50 = bf16[1536,128]{1,0:T(8,128)(2,1)S(1)} custom-call(s32[1]{0:T(128)} %bitcast.s, bf16[2048,3072]{1,0:T(8,128)(2,1)} %d.27, bf16[2048,128]{1,0:T(8,128)(2,1)S(1)} %copy-done.1), custom_call_target="tpu_custom_call" | custom-call | flops 805306368 | bytes 6291456 | tf_op jit(solution)/shard_map/pallas_call | solution.py:44
  10.9 18.1 %all_to_all.65 = bf16[32,48,128]{2,1,0:T(8,128)(2,1)S(1)} all-to-all(bf16[32,48,128]{2,1,0:T(8,128)(2,1)S(1)} %bitcast.151), channel_id=1, replica_groups=mesh['rows_0'=2,'rows_1'=4,'rows_2'=4,'rows_3'=2,'cols'=2] {'rows_0','ro..., dimensions={0} | all-to-all | bytes 786432 | tf_op jit(solution)/shard_map/all_to_all | solution.py:258
  29.2 12.7 %all_to_all.66 = bf16[32,48,128]{2,1,0:T(8,128)(2,1)S(1)} all-to-all(bf16[32,48,128]{2,1,0:T(8,128)(2,1)S(1)} %broadcast_in_dim.87), channel_id=1, replica_groups=mesh['rows_0'=2,'rows_1'=4,'rows_2'=4,'rows_3'=2,'cols'=2] {'rows_0','ro..., dimensions={0} | all-to-all | bytes 786432 | tf_op jit(solution)/shard_map/all_to_all | solution.py:258
  42.0 2.7 collective-permute-start.1
  47.9 4.8 %shard_map.52 = (f32[1280,128]{1,0:T(8,128)S(1)}, bf16[1280,128]{1,0:T(8,128)(2,1)S(1)}, bf16[1280,3072]{1,0:T(8,128)(2,1)S(1)}) custom-call(bf16[2048,3072]{1,0:T(8,128)(2,1)} %d.27, bf16[3072,128]{1,0:T(8,128)(2,1)S(1)} %pad_maximum_fusion.1.v), custom_call_target="tpu_custom_call" | custom-call | flops 1006632960 | bytes 7864320 | tf_op jit(solution)/shard_map/pallas_call | solution.py:44
  52.7 2.5 collective-permute-start.4
  57.0 3.3 shard_map.53
  61.0 2.3 collective-permute-done.4.other_ref
  63.2 2.9 shard_map.54
  72.2 13.1 %all_to_all.67 = bf16[32,56,128]{2,1,0:T(8,128)(2,1)S(1)} all-to-all(bf16[32,56,128]{2,1,0:T(8,128)(2,1)S(1)} %pad_maximum_fusion.7), channel_id=1, replica_groups=mesh['rows_0'=2,'rows_1'=4,'rows_2'=4,'rows_3'=2,'cols'=2] {'rows_0','ro..., dimensions={0} | all-to-all | bytes 917504 | tf_op jit(solution)/shard_map/all_to_all | solution.py:258
  86.2 4.4 %all-to-all-start.3 = ((bf16[32,48,128]{2,1,0:T(8,128)(2,1)}), bf16[32,48,128]{2,1,0:T(8,128)(2,1)S(1)}, u32[]{:S(2)}, u32[]{:S(2)}) async-start(bf16[32,48,128]{2,1,0:T(8,128)(2,1)} %broadcast_in_dim.92), calls=%async_computation.3 | async-start | bytes 786432 | tf_op jit(solution)/shard_map/all_to_all | solution.py:258
  93.9 5.2 %all-to-all-done.3 = bf16[32,48,128]{2,1,0:T(8,128)(2,1)S(1)} async-done(((bf16[32,48,128]{2,1,0:T(8,128)(2,1)}), bf16[32,48,128]{2,1,0:T(8,128)(2,1)S(1)}, u32[]{:S(2)}, u32[]{:S(2)}) %all-to-all-start.3) | async-done | bytes 393248 | tf_op jit(solution)/shard_map/all_to_all | solution.py:258
  99.1 3.0 collective-permute-start.6
  103.7 5.0 %shard_map.57 = (f32[1280,128]{1,0:T(8,128)S(1)}, bf16[1280,128]{1,0:T(8,128)(2,1)S(1)}, bf16[1280,3072]{1,0:T(8,128)(2,1)S(1)}) custom-call(bf16[2048,3072]{1,0:T(8,128)(2,1)} %d.27, bf16[3072,128]{1,0:T(8,128)(2,1)S(1)} %pad_maximum_fusion.2.v, f32[1280,128]{1,0:T(8,128)S(1)} %get-tuple-element.173.rest_0_, f32[1,128]{1,0:T(1,128)S(1)} %get-tuple-element.334.rest_1_), custom_call_target="tpu_custom_call" | custom-call | flops 1006632960 | bytes 7864320 | tf_op jit(solution)/shard_map/pallas_call | solution.py:44
  112.3 3.3 shard_map.58
  115.6 2.0 collective-permute-start.8
  119.5 3.2 collective-permute-done.8.other_ref
  122.8 3.0 shard_map.59
  130.5 13.3 %all_to_all.68 = bf16[32,56,128]{2,1,0:T(8,128)(2,1)S(1)} all-to-all(bf16[32,56,128]{2,1,0:T(8,128)(2,1)S(1)} %pad_maximum_fusion.8), channel_id=1, replica_groups=mesh['rows_0'=2,'rows_1'=4,'rows_2'=4,'rows_3'=2,'cols'=2] {'rows_0','ro..., dimensions={0} | all-to-all | bytes 917504 | tf_op jit(solution)/shard_map/all_to_all | solution.py:258
  144.1 12.8 %all_to_all.69 = bf16[32,48,128]{2,1,0:T(8,128)(2,1)S(1)} all-to-all(bf16[32,48,128]{2,1,0:T(8,128)(2,1)S(1)} %broadcast_in_dim.97), channel_id=1, replica_groups=mesh['rows_0'=2,'rows_1'=4,'rows_2'=4,'rows_3'=2,'cols'=2] {'rows_0','ro..., dimensions={0} | all-to-all | bytes 786432 | tf_op jit(solution)/shard_map/all_to_all | solution.py:258
  156.8 3.0 collective-permute-start.11
  161.3 4.8 %shard_map.62 = (f32[1280,128]{1,0:T(8,128)S(1)}, bf16[1280,128]{1,0:T(8,128)(2,1)S(1)}, bf16[1280,3072]{1,0:T(8,128)(2,1)S(1)}) custom-call(bf16[2048,3072]{1,0:T(8,128)(2,1)} %d.27, bf16[3072,128]{1,0:T(8,128)(2,1)S(1)} %pad_maximum_fusion.3.v, f32[1280,128]{1,0:T(8,128)S(1)} %get-tuple-element.198.rest_0_, f32[1,128]{1,0:T(1,128)S(1)} %bitcast_divide_fusion.4.rest_1_), custom_call_target="tpu_custom_call" | custom-call | flops 1006632960 | bytes 7864320 | tf_op jit(solution)/shard_map/pallas_call | solution.py:44
  169.8 3.4 shard_map.63
  173.2 2.0 collective-permute-start.13
  176.9 3.5 collective-permute-done.13.other_ref
  180.4 3.0 shard_map.64
  188.1 13.2 %all_to_all.70 = bf16[32,56,128]{2,1,0:T(8,128)(2,1)S(1)} all-to-all(bf16[32,56,128]{2,1,0:T(8,128)(2,1)S(1)} %pad_maximum_fusion.9), channel_id=1, replica_groups=mesh['rows_0'=2,'rows_1'=4,'rows_2'=4,'rows_3'=2,'cols'=2] {'rows_0','ro..., dimensions={0} | all-to-all | bytes 917504 | tf_op jit(solution)/shard_map/all_to_all | solution.py:258
  201.5 12.8 %all_to_all.71 = bf16[32,48,128]{2,1,0:T(8,128)(2,1)S(1)} all-to-all(bf16[32,48,128]{2,1,0:T(8,128)(2,1)S(1)} %broadcast_in_dim.102), channel_id=1, replica_groups=mesh['rows_0'=2,'rows_1'=4,'rows_2'=4,'rows_3'=2,'cols'=2] {'rows_0','ro..., dimensions={0} | all-to-all | bytes 786432 | tf_op jit(solution)/shard_map/all_to_all | solution.py:258
  214.2 3.0 collective-permute-start.16
  218.7 4.8 %shard_map.67 = (f32[1280,128]{1,0:T(8,128)S(1)}, bf16[1280,128]{1,0:T(8,128)(2,1)S(1)}, bf16[1280,3072]{1,0:T(8,128)(2,1)S(1)}) custom-call(bf16[2048,3072]{1,0:T(8,128)(2,1)} %d.27, bf16[3072,128]{1,0:T(8,128)(2,1)S(1)} %pad_maximum_fusion.4.v, f32[1280,128]{1,0:T(8,128)S(1)} %get-tuple-element.227.rest_0_, f32[1,128]{1,0:T(1,128)S(1)} %bitcast_divide_fusion.3.rest_1_), custom_call_target="tpu_custom_call" | custom-call | flops 1006632960 | bytes 7864320 | tf_op jit(solution)/shard_map/pallas_call | solution.py:44
  227.2 3.4 shard_map.68
  234.3 3.5 collective-permute-done.18.other_ref
  237.7 3.0 shard_map.69
  245.4 13.1 %all_to_all.72 = bf16[32,56,128]{2,1,0:T(8,128)(2,1)S(1)} all-to-all(bf16[32,56,128]{2,1,0:T(8,128)(2,1)S(1)} %pad_maximum_fusion.10), channel_id=1, replica_groups=mesh['rows_0'=2,'rows_1'=4,'rows_2'=4,'rows_3'=2,'cols'=2] {'rows_0','ro..., dimensions={0} | all-to-all | bytes 917504 | tf_op jit(solution)/shard_map/all_to_all | solution.py:258
  258.8 12.8 %all_to_all.73 = bf16[32,48,128]{2,1,0:T(8,128)(2,1)S(1)} all-to-all(bf16[32,48,128]{2,1,0:T(8,128)(2,1)S(1)} %broadcast_in_dim.107), channel_id=1, replica_groups=mesh['rows_0'=2,'rows_1'=4,'rows_2'=4,'rows_3'=2,'cols'=2] {'rows_0','ro..., dimensions={0} | all-to-all | bytes 786432 | tf_op jit(solution)/shard_map/all_to_all | solution.py:258
  271.6 3.0 collective-permute-start.21
  276.1 4.8 %shard_map.72 = (f32[1280,128]{1,0:T(8,128)S(1)}, bf16[1280,128]{1,0:T(8,128)(2,1)S(1)}, bf16[1280,3072]{1,0:T(8,128)(2,1)S(1)}) custom-call(bf16[2048,3072]{1,0:T(8,128)(2,1)} %d.27, bf16[3072,128]{1,0:T(8,128)(2,1)S(1)} %pad_maximum_fusion.5.v, f32[1280,128]{1,0:T(8,128)S(1)} %get-tuple-element.256.rest_0_, f32[1,128]{1,0:T(1,128)S(1)} %bitcast_divide_fusion.2.rest_1_), custom_call_target="tpu_custom_call" | custom-call | flops 1006632960 | bytes 7864320 | tf_op jit(solution)/shard_map/pallas_call | solution.py:44
  283.5 3.4 shard_map.73
  290.3 5.3 %collective-permute-done.22 = f32[1,128]{1,0:T(1,128)S(1)} collective-permute-done((f32[1,128]{1,0:T(1,128)S(1)}, f32[1,128]{1,0:T(1,128)S(1)}, u32[]{:S(2)}, u32[]{:S(2)}) %collective-permute-start.22) | collective-permute-done | bytes 544 | tf_op jit(solution)/shard_map/ppermute | solution.py:25
  295.8 3.0 shard_map.74
  303.1 13.2 %all_to_all.74 = bf16[32,56,128]{2,1,0:T(8,128)(2,1)S(1)} all-to-all(bf16[32,56,128]{2,1,0:T(8,128)(2,1)S(1)} %pad_maximum_fusion.11), channel_id=1, replica_groups=mesh['rows_0'=2,'rows_1'=4,'rows_2'=4,'rows_3'=2,'cols'=2] {'rows_0','ro..., dimensions={0} | all-to-all | bytes 917504 | tf_op jit(solution)/shard_map/all_to_all | solution.py:258
  316.5 12.8 %all_to_all.75 = bf16[32,48,128]{2,1,0:T(8,128)(2,1)S(1)} all-to-all(bf16[32,48,128]{2,1,0:T(8,128)(2,1)S(1)} %broadcast_in_dim.112), channel_id=1, replica_groups=mesh['rows_0'=2,'rows_1'=4,'rows_2'=4,'rows_3'=2,'cols'=2] {'rows_0','ro..., dimensions={0} | all-to-all | bytes 786432 | tf_op jit(solution)/shard_map/all_to_all | solution.py:258
  329.2 3.0 collective-permute-start.26
  333.7 5.8 %shard_map.77 = (f32[1280,128]{1,0:T(8,128)}, bf16[1280,128]{1,0:T(8,128)(2,1)S(1)}) custom-call(bf16[2048,3072]{1,0:T(8,128)(2,1)} %d.27, bf16[3072,128]{1,0:T(8,128)(2,1)S(1)} %pad_maximum_fusion.6.v, f32[1280,128]{1,0:T(8,128)S(1)} %get-tuple-element.285.rest_0_, f32[1,128]{1,0:T(1,128)S(1)} %bitcast_divide_fusion.1.rest_1_), custom_call_target="tpu_custom_call" | custom-call | flops 1006632960 | bytes 7864320 | tf_op jit(solution)/shard_map/pallas_call | solution.py:44
  342.1 4.2 %shard_map.78 = (f32[768,128]{1,0:T(8,128)}, bf16[768,128]{1,0:T(8,128)(2,1)S(1)}) custom-call(bf16[2048,3072]{1,0:T(8,128)(2,1)} %d.27, bf16[3072,128]{1,0:T(8,128)(2,1)S(1)} %pad_maximum_fusion.6.v, f32[768,128]{1,0:T(8,128)S(1)} %get-tuple-element.289.rest_0_, f32[1,128]{1,0:T(1,128)S(1)} %bitcast_divide_fusion.1.rest_1_), custom_call_target="tpu_custom_call" | custom-call | flops 603979776 | bytes 4718592 | tf_op jit(solution)/shard_map/pallas_call | solution.py:44
  349.7 4.6 %collective-permute-done.27 = f32[1,128]{1,0:T(1,128)S(1)} collective-permute-done((f32[1,128]{1,0:T(1,128)S(1)}, f32[1,128]{1,0:T(1,128)S(1)}, u32[]{:S(2)}, u32[]{:S(2)}) %collective-permute-start.27) | collective-permute-done | bytes 544 | tf_op jit(solution)/shard_map/ppermute | solution.py:25
  355.2 13.2 %all_to_all.76 = f32[64,1,128]{2,1,0:T(1,128)S(1)} all-to-all(f32[64,1,128]{2,1,0:T(1,128)S(1)} %broadcast_in_dim.114), channel_id=1, replica_groups=mesh['rows_0'=2,'rows_1'=4,'rows_2'=4,'rows_3'=2,'cols'=2] {'rows_0','ro..., dimensions={0} | all-to-all | bytes 65536 | tf_op jit(solution)/shard_map/all_to_all | solution.py:383
  (195 shorter events, 79.1 us)
Async XLA Ops:
  0.6 1.0 copy-start
  1.7 5.2 %copy-start.1 = (bf16[2048,128]{1,0:T(8,128)(2,1)S(1)}, bf16[2048,128]{1,0:T(8,128)(2,1)}, u32[]{:S(2)}) copy-start(bf16[2048,128]{1,0:T(8,128)(2,1)} %v.3) | copy-start | bytes 1572868
  5.5 5.3 %collective-permute-start = (bf16[1536,128]{1,0:T(8,128)(2,1)S(1)}, bf16[1536,128]{1,0:T(8,128)(2,1)S(1)}, u32[]{:S(2)}, u32[]{:S(2)}) collective-permute-start(bf16[1536,128]{1,0:T(8,128)(2,1)S(1)} %shard_map.51), channel_id=1, source_target_pairs={{0,2},{2,0},{1,3},{3,1},{4,6},{6,4},{5,7},{7,5},{8,10},{10,8},{9,1... | collective-permute-start | bytes 1179656 | tf_op jit(solution)/shard_map/ppermute | solution.py:25
  6.9 3.8 %copy-start.6 = (f32[3072]{0:T(1024)S(1)}, f32[3072]{0:T(1024)}, u32[]{:S(2)}) copy-start(f32[3072]{0:T(1024)} %param.5) | copy-start | bytes 36868
  42.0 4.1 %collective-permute-start.1 = (bf16[1536,128]{1,0:T(8,128)(2,1)S(1)}, bf16[1536,128]{1,0:T(8,128)(2,1)S(1)}, u32[]{:S(2)}, u32[]{:S(2)}) collective-permute-start(bf16[1536,128]{1,0:T(8,128)(2,1)S(1)} %bitcast.150), channel_id=1, source_target_pairs={{0,2},{2,0},{1,3},{3,1},{4,6},{6,4},{5,7},{7,5},{8,10},{10,8},{9,1... | collective-permute-start | bytes 1179656 | tf_op jit(solution)/shard_map/ppermute | solution.py:25
  52.7 10.5 %collective-permute-start.4 = (bf16[1280,128]{1,0:T(8,128)(2,1)S(1)}, bf16[1280,128]{1,0:T(8,128)(2,1)S(1)}, u32[]{:S(2)}, u32[]{:S(2)}) collective-permute-start(bf16[1280,128]{1,0:T(8,128)(2,1)S(1)} %get-tuple-element.164.own_ref), channel_id=1, source_target_pairs={{0,1},{1,0},{2,3},{3,2},{4,5},{5,4},{6,7},{7,6},{8,9},{9,8},{10,11... | collective-permute-start | bytes 983048 | tf_op jit(solution)/shard_map/ppermute | solution.py:25
  60.4 7.4 %collective-permute-start.3 = (bf16[768,128]{1,0:T(8,128)(2,1)S(1)}, bf16[768,128]{1,0:T(8,128)(2,1)S(1)}, u32[]{:S(2)}, u32[]{:S(2)}) collective-permute-start(bf16[768,128]{1,0:T(8,128)(2,1)S(1)} %get-tuple-element.162.own_ref), channel_id=1, source_target_pairs={{0,1},{1,0},{2,3},{3,2},{4,5},{5,4},{6,7},{7,6},{8,9},{9,8},{10,11... | collective-permute-start | bytes 589832 | tf_op jit(solution)/shard_map/ppermute | solution.py:25
  69.0 2.9 collective-permute-start.5
  86.2 13.0 %all-to-all-start.3 = ((bf16[32,48,128]{2,1,0:T(8,128)(2,1)}), bf16[32,48,128]{2,1,0:T(8,128)(2,1)S(1)}, u32[]{:S(2)}, u32[]{:S(2)}) async-start(bf16[32,48,128]{2,1,0:T(8,128)(2,1)} %broadcast_in_dim.92), calls=%async_computation.3 | async-start | bytes 786432 | tf_op jit(solution)/shard_map/all_to_all | solution.py:258
  90.6 11.6 %collective-permute-start.2 = (f32[1,128]{1,0:T(1,128)S(1)}, f32[1,128]{1,0:T(1,128)S(1)}, u32[]{:S(2)}, u32[]{:S(2)}) collective-permute-start(f32[1,128]{1,0:T(1,128)S(1)} %bitcast.175), channel_id=1, source_target_pairs={{0,1},{1,0},{2,3},{3,2},{4,5},{5,4},{6,7},{7,6},{8,9},{9,8},{10,11... | collective-permute-start | bytes 1544 | tf_op jit(solution)/shard_map/ppermute | solution.py:25
  99.1 4.4 %collective-permute-start.6 = (bf16[1536,128]{1,0:T(8,128)(2,1)S(1)}, bf16[1536,128]{1,0:T(8,128)(2,1)S(1)}, u32[]{:S(2)}, u32[]{:S(2)}) collective-permute-start(bf16[1536,128]{1,0:T(8,128)(2,1)S(1)} %bitcast.145), channel_id=1, source_target_pairs={{0,2},{2,0},{1,3},{3,1},{4,6},{6,4},{5,7},{7,5},{8,10},{10,8},{9,1... | collective-permute-start | bytes 1179656 | tf_op jit(solution)/shard_map/ppermute | solution.py:25
  103.7 7.0 %copy-start.2 = (f32[3072,128]{1,0:T(8,128)S(1)}, f32[3072,128]{1,0:T(8,128)}, u32[]{:S(2)}) copy-start(f32[3072,128]{1,0:T(8,128)} %convert_element_type.144) | copy-start | bytes 4718596
  108.6 14.2 %collective-permute-start.9 = (bf16[1280,128]{1,0:T(8,128)(2,1)S(1)}, bf16[1280,128]{1,0:T(8,128)(2,1)S(1)}, u32[]{:S(2)}, u32[]{:S(2)}) collective-permute-start(bf16[1280,128]{1,0:T(8,128)(2,1)S(1)} %get-tuple-element.189.own_ref), channel_id=1, source_target_pairs={{0,1},{1,0},{2,3},{3,2},{4,5},{5,4},{6,7},{7,6},{8,9},{9,8},{10,11... | collective-permute-start | bytes 983048 | tf_op jit(solution)/shard_map/ppermute | solution.py:25
  111.2 7.9 %collective-permute-start.7 = (f32[1,128]{1,0:T(1,128)S(1)}, f32[1,128]{1,0:T(1,128)S(1)}, u32[]{:S(2)}, u32[]{:S(2)}) collective-permute-start(f32[1,128]{1,0:T(1,128)S(1)} %bitcast.173), channel_id=1, source_target_pairs={{0,1},{1,0},{2,3},{3,2},{4,5},{5,4},{6,7},{7,6},{8,9},{9,8},{10,11... | collective-permute-start | bytes 1544 | tf_op jit(solution)/shard_map/ppermute | solution.py:25
  115.6 7.1 %collective-permute-start.8 = (bf16[768,128]{1,0:T(8,128)(2,1)S(1)}, bf16[768,128]{1,0:T(8,128)(2,1)S(1)}, u32[]{:S(2)}, u32[]{:S(2)}) collective-permute-start(bf16[768,128]{1,0:T(8,128)(2,1)S(1)} %get-tuple-element.186.own_ref), channel_id=1, source_target_pairs={{0,1},{1,0},{2,3},{3,2},{4,5},{5,4},{6,7},{7,6},{8,9},{9,8},{10,11... | collective-permute-start | bytes 589832 | tf_op jit(solution)/shard_map/ppermute | solution.py:25
  127.1 3.2 collective-permute-start.10
  156.8 4.4 %collective-permute-start.11 = (bf16[1536,128]{1,0:T(8,128)(2,1)S(1)}, bf16[1536,128]{1,0:T(8,128)(2,1)S(1)}, u32[]{:S(2)}, u32[]{:S(2)}) collective-permute-start(bf16[1536,128]{1,0:T(8,128)(2,1)S(1)} %bitcast.147), channel_id=1, source_target_pairs={{0,2},{2,0},{1,3},{3,1},{4,6},{6,4},{5,7},{7,5},{8,10},{10,8},{9,1... | collective-permute-start | bytes 1179656 | tf_op jit(solution)/shard_map/ppermute | solution.py:25
  166.2 14.2 %collective-permute-start.14 = (bf16[1280,128]{1,0:T(8,128)(2,1)S(1)}, bf16[1280,128]{1,0:T(8,128)(2,1)S(1)}, u32[]{:S(2)}, u32[]{:S(2)}) collective-permute-start(bf16[1280,128]{1,0:T(8,128)(2,1)S(1)} %get-tuple-element.218.own_ref), channel_id=1, source_target_pairs={{0,1},{1,0},{2,3},{3,2},{4,5},{5,4},{6,7},{7,6},{8,9},{9,8},{10,11... | collective-permute-start | bytes 983048 | tf_op jit(solution)/shard_map/ppermute | solution.py:25
  168.7 8.0 %collective-permute-start.12 = (f32[1,128]{1,0:T(1,128)S(1)}, f32[1,128]{1,0:T(1,128)S(1)}, u32[]{:S(2)}, u32[]{:S(2)}) collective-permute-start(f32[1,128]{1,0:T(1,128)S(1)} %bitcast.165), channel_id=1, source_target_pairs={{0,1},{1,0},{2,3},{3,2},{4,5},{5,4},{6,7},{7,6},{8,9},{9,8},{10,11... | collective-permute-start | bytes 1544 | tf_op jit(solution)/shard_map/ppermute | solution.py:25
  173.2 7.2 %collective-permute-start.13 = (bf16[768,128]{1,0:T(8,128)(2,1)S(1)}, bf16[768,128]{1,0:T(8,128)(2,1)S(1)}, u32[]{:S(2)}, u32[]{:S(2)}) collective-permute-start(bf16[768,128]{1,0:T(8,128)(2,1)S(1)} %get-tuple-element.215.own_ref), channel_id=1, source_target_pairs={{0,1},{1,0},{2,3},{3,2},{4,5},{5,4},{6,7},{7,6},{8,9},{9,8},{10,11... | collective-permute-start | bytes 589832 | tf_op jit(solution)/shard_map/ppermute | solution.py:25
  184.7 3.2 collective-permute-start.15
  214.2 4.4 %collective-permute-start.16 = (bf16[1536,128]{1,0:T(8,128)(2,1)S(1)}, bf16[1536,128]{1,0:T(8,128)(2,1)S(1)}, u32[]{:S(2)}, u32[]{:S(2)}) collective-permute-start(bf16[1536,128]{1,0:T(8,128)(2,1)S(1)} %bitcast.148), channel_id=1, source_target_pairs={{0,2},{2,0},{1,3},{3,1},{4,6},{6,4},{5,7},{7,5},{8,10},{10,8},{9,1... | collective-permute-start | bytes 1179656 | tf_op jit(solution)/shard_map/ppermute | solution.py:25
  223.6 14.1 %collective-permute-start.19 = (bf16[1280,128]{1,0:T(8,128)(2,1)S(1)}, bf16[1280,128]{1,0:T(8,128)(2,1)S(1)}, u32[]{:S(2)}, u32[]{:S(2)}) collective-permute-start(bf16[1280,128]{1,0:T(8,128)(2,1)S(1)} %get-tuple-element.247.own_ref), channel_id=1, source_target_pairs={{0,1},{1,0},{2,3},{3,2},{4,5},{5,4},{6,7},{7,6},{8,9},{9,8},{10,11... | collective-permute-start | bytes 983048 | tf_op jit(solution)/shard_map/ppermute | solution.py:25
  226.1 8.0 %collective-permute-start.17 = (f32[1,128]{1,0:T(1,128)S(1)}, f32[1,128]{1,0:T(1,128)S(1)}, u32[]{:S(2)}, u32[]{:S(2)}) collective-permute-start(f32[1,128]{1,0:T(1,128)S(1)} %bitcast.167), channel_id=1, source_target_pairs={{0,1},{1,0},{2,3},{3,2},{4,5},{5,4},{6,7},{7,6},{8,9},{9,8},{10,11... | collective-permute-start | bytes 1544 | tf_op jit(solution)/shard_map/ppermute | solution.py:25
  227.2 5.4 %copy-start.3 = (f32[768,128]{1,0:T(8,128)S(1)}, f32[768,128]{1,0:T(8,128)}, u32[]{:S(2)}) copy-start(f32[768,128]{1,0:T(8,128)} %multiply_subtract_fusion.15) | copy-start | bytes 1179652
  230.6 7.1 %collective-permute-start.18 = (bf16[768,128]{1,0:T(8,128)(2,1)S(1)}, bf16[768,128]{1,0:T(8,128)(2,1)S(1)}, u32[]{:S(2)}, u32[]{:S(2)}) collective-permute-start(bf16[768,128]{1,0:T(8,128)(2,1)S(1)} %get-tuple-element.244.own_ref), channel_id=1, source_target_pairs={{0,1},{1,0},{2,3},{3,2},{4,5},{5,4},{6,7},{7,6},{8,9},{9,8},{10,11... | collective-permute-start | bytes 589832 | tf_op jit(solution)/shard_map/ppermute | solution.py:25
  242.0 3.2 collective-permute-start.20
  271.6 4.4 %collective-permute-start.21 = (bf16[1536,128]{1,0:T(8,128)(2,1)S(1)}, bf16[1536,128]{1,0:T(8,128)(2,1)S(1)}, u32[]{:S(2)}, u32[]{:S(2)}) collective-permute-start(bf16[1536,128]{1,0:T(8,128)(2,1)S(1)} %bitcast.149), channel_id=1, source_target_pairs={{0,2},{2,0},{1,3},{3,1},{4,6},{6,4},{5,7},{7,5},{8,10},{10,8},{9,1... | collective-permute-start | bytes 1179656 | tf_op jit(solution)/shard_map/ppermute | solution.py:25
  280.9 14.9 %collective-permute-start.24 = (bf16[1280,128]{1,0:T(8,128)(2,1)S(1)}, bf16[1280,128]{1,0:T(8,128)(2,1)S(1)}, u32[]{:S(2)}, u32[]{:S(2)}) collective-permute-start(bf16[1280,128]{1,0:T(8,128)(2,1)S(1)} %get-tuple-element.276.own_ref), channel_id=1, source_target_pairs={{0,1},{1,0},{2,3},{3,2},{4,5},{5,4},{6,7},{7,6},{8,9},{9,8},{10,11... | collective-permute-start | bytes 983048 | tf_op jit(solution)/shard_map/ppermute | solution.py:25
  286.8 9.0 %collective-permute-start.23 = (bf16[768,128]{1,0:T(8,128)(2,1)S(1)}, bf16[768,128]{1,0:T(8,128)(2,1)S(1)}, u32[]{:S(2)}, u32[]{:S(2)}) collective-permute-start(bf16[768,128]{1,0:T(8,128)(2,1)S(1)} %get-tuple-element.273.own_ref), channel_id=1, source_target_pairs={{0,1},{1,0},{2,3},{3,2},{4,5},{5,4},{6,7},{7,6},{8,9},{9,8},{10,11... | collective-permute-start | bytes 589832 | tf_op jit(solution)/shard_map/ppermute | solution.py:25
  287.9 7.7 %collective-permute-start.22 = (f32[1,128]{1,0:T(1,128)S(1)}, f32[1,128]{1,0:T(1,128)S(1)}, u32[]{:S(2)}, u32[]{:S(2)}) collective-permute-start(f32[1,128]{1,0:T(1,128)S(1)} %bitcast.169), channel_id=1, source_target_pairs={{0,1},{1,0},{2,3},{3,2},{4,5},{5,4},{6,7},{7,6},{8,9},{9,8},{10,11... | collective-permute-start | bytes 1544 | tf_op jit(solution)/shard_map/ppermute | solution.py:25
  300.1 2.8 collective-permute-start.25
  329.2 4.4 %collective-permute-start.26 = (bf16[1536,128]{1,0:T(8,128)(2,1)S(1)}, bf16[1536,128]{1,0:T(8,128)(2,1)S(1)}, u32[]{:S(2)}, u32[]{:S(2)}) collective-permute-start(bf16[1536,128]{1,0:T(8,128)(2,1)S(1)} %bitcast.146), channel_id=1, source_target_pairs={{0,2},{2,0},{1,3},{3,1},{4,6},{6,4},{5,7},{7,5},{8,10},{10,8},{9,1... | collective-permute-start | bytes 1179656 | tf_op jit(solution)/shard_map/ppermute | solution.py:25
  339.6 14.9 %collective-permute-start.29 = (bf16[1280,128]{1,0:T(8,128)(2,1)S(1)}, bf16[1280,128]{1,0:T(8,128)(2,1)S(1)}, u32[]{:S(2)}, u32[]{:S(2)}) collective-permute-start(bf16[1280,128]{1,0:T(8,128)(2,1)S(1)} %get-tuple-element.300), channel_id=1, source_target_pairs={{0,1},{1,0},{2,3},{3,2},{4,5},{5,4},{6,7},{7,6},{8,9},{9,8},{10,11... | collective-permute-start | bytes 983048 | tf_op jit(solution)/shard_map/ppermute | solution.py:25
  346.3 8.5 %collective-permute-start.28 = (bf16[768,128]{1,0:T(8,128)(2,1)S(1)}, bf16[768,128]{1,0:T(8,128)(2,1)S(1)}, u32[]{:S(2)}, u32[]{:S(2)}) collective-permute-start(bf16[768,128]{1,0:T(8,128)(2,1)S(1)} %get-tuple-element.301), channel_id=1, source_target_pairs={{0,1},{1,0},{2,3},{3,2},{4,5},{5,4},{6,7},{7,6},{8,9},{9,8},{10,11... | collective-permute-start | bytes 589832 | tf_op jit(solution)/shard_map/ppermute | solution.py:25
  347.4 6.9 %collective-permute-start.27 = (f32[1,128]{1,0:T(1,128)S(1)}, f32[1,128]{1,0:T(1,128)S(1)}, u32[]{:S(2)}, u32[]{:S(2)}) collective-permute-start(f32[1,128]{1,0:T(1,128)S(1)} %bitcast.171), channel_id=1, source_target_pairs={{0,1},{1,0},{2,3},{3,2},{4,5},{5,4},{6,7},{7,6},{8,9},{9,8},{10,11... | collective-permute-start | bytes 1544 | tf_op jit(solution)/shard_map/ppermute | solution.py:25
  354.5 0.7 copy-start.4
  368.4 1.0 copy-start.5

commit v6 on v5

--- a/solution.py
+++ b/solution.py
@@ -70,7 +70,8 @@
 
 def image_step(design, vector, begin, rows, keep, moved=None, alpha=None):
     width, fits = design.shape[1], vector.shape[1]
-    steps = rows // ROW_BLOCK
+    block = ROW_BLOCK if begin or not keep else 2 * ROW_BLOCK
+    steps = rows // block
 
     def kernel(d, v, *rest):
         if moved is not None:
@@ -79,12 +80,12 @@
             out, short, close, sems = rest
 
         def fetch(i):
-            where = aligned(i * ROW_BLOCK, ROW_BLOCK)
-            source = aligned(begin + i * ROW_BLOCK, ROW_BLOCK)
+            where = aligned(i * block, block)
+            source = aligned(begin + i * block, block)
             return pltpu.make_async_copy(d.at[source, :], close.at[where, :], sems.at[i])
 
         def work(i):
-            where = aligned(i * ROW_BLOCK, ROW_BLOCK)
+            where = aligned(i * block, block)
             product = jnp.dot(close[where, :], v[...], preferred_element_type=F32)
             if moved is not None:
                 product = u[where, :] - a[...] * product
@@ -379,8 +380,8 @@
             pairs = zip((short_first, short_second), (other_first, other_second), image)
             image = [a.astype(F32) + b.astype(F32) + ratio * q for a, b, q in pairs]
             norm = sum(jnp.sum(q * q, axis=0) for q in image)
-            copies = jnp.broadcast_to(norm, (lax.axis_size(ROWS), 1, fits))
-            copies = lax.all_to_all(copies, ROWS, split_axis=0, concat_axis=0, tiled=True)
+            norm = norm + swapped(norm, CORE)
+            copies = exchanged(jnp.broadcast_to(norm, (chips, 1, fits)))
             delta = copies.sum(axis=0)
             alpha = gamma / delta
     residual = [r - alpha * q for r, q in zip(residual, image)]

time: 372 us -> 369 us (level)
    all_to_all x1 -> x0, blocking collectives: 13.2 us -> none  [per_device(): lax.all_to_all(copies, ROWS, split_axis=0, concat_axis=0, tiled=True)]
    all_to_all x11 -> x12, blocking collectives: 148 us -> 158 us  [exchanged(): lax.all_to_all(pieces, CHIPS, split_axis=0, concat_axis=0, tiled=True)]
    ppermute x30 -> x31, starting transfers between devices: 58.7 us -> 60.2 us  [swapped(): return lax.ppermute(array, axis, ((0, 1), (1, 0)))]
    ppermute x30 -> x31, waiting for transfers between devices: 35.2 us -> 35.9 us  [swapped(): return lax.ppermute(array, axis, ((0, 1), (1, 0)))]
  transfers between devices with their start and end apart: 31 -> 32, of which waited for: 22 -> 23; matrix products, arithmetic and copies ran while one was open for 3% -> 3% of each run, Pallas kernels for 9% -> 9%
where the time goes in v6:
time: 369 us; the launch traced here: 368 us
  blocking collectives  158 us (43%)
  Pallas kernels  82.9 us (22%)
  starting transfers between devices  64.6 us (18%)
  waiting for transfers between devices  41.1 us (11%)
  other arithmetic  12.8 us (3%)
  local copies, waits for them, and re-layouts  4.18 us (1%)
    all_to_all x12, blocking collectives, exchanged(): lax.all_to_all(pieces, CHIPS, split_axis=0, concat_axis=0, tiled=True)  158 us
    pallas_call x29, Pallas kernels, called(): pl.pallas_call(kernel, in_specs=specs, out_specs=[NEAR] * len(outs), out_...  82.9 us
    ppermute x31, starting transfers between devices, swapped(): return lax.ppermute(array, axis, ((0, 1), (1, 0)))  60.2 us
    ppermute x31, waiting for transfers between devices, swapped(): return lax.ppermute(array, axis, ((0, 1), (1, 0)))  35.9 us
  transfers between devices with their start and end apart: 32, of which 23 were waited for; matrix products, arithmetic and copies ran while one was open for 3% of the time, Pallas kernels for 9%

profile of v6, /device:TPU:1, one launch (start us, length us, event | category | flops | bytes accessed | tf_op | source)
XLA Modules:
  0.0 368.1 jit_solution(18324521986377416224)
XLA Ops:
  1.7 3.8 %shard_map.51 = bf16[1536,128]{1,0:T(8,128)(2,1)S(1)} custom-call(s32[1]{0:T(128)S(6)} %sub.104.s, bf16[2048,3072]{1,0:T(8,128)(2,1)} %d.27, bf16[2048,128]{1,0:T(8,128)(2,1)S(1)} %copy-done), custom_call_target="tpu_custom_call" | custom-call | flops 805306368 | bytes 6291456 | tf_op jit(solution)/shard_map/pallas_call | solution.py:44
  6.9 3.8 %shard_map.50 = bf16[1536,128]{1,0:T(8,128)(2,1)S(1)} custom-call(s32[1]{0:T(128)} %bitcast.s, bf16[2048,3072]{1,0:T(8,128)(2,1)} %d.27, bf16[2048,128]{1,0:T(8,128)(2,1)S(1)} %copy-done.1), custom_call_target="tpu_custom_call" | custom-call | flops 805306368 | bytes 6291456 | tf_op jit(solution)/shard_map/pallas_call | solution.py:44
  10.9 18.1 %all_to_all.65 = bf16[32,48,128]{2,1,0:T(8,128)(2,1)S(1)} all-to-all(bf16[32,48,128]{2,1,0:T(8,128)(2,1)S(1)} %bitcast.151), channel_id=1, replica_groups=mesh['rows_0'=2,'rows_1'=4,'rows_2'=4,'rows_3'=2,'cols'=2] {'rows_0','ro..., dimensions={0} | all-to-all | bytes 786432 | tf_op jit(solution)/shard_map/all_to_all | solution.py:259
  29.2 12.7 %all_to_all.66 = bf16[32,48,128]{2,1,0:T(8,128)(2,1)S(1)} all-to-all(bf16[32,48,128]{2,1,0:T(8,128)(2,1)S(1)} %broadcast_in_dim.87), channel_id=1, replica_groups=mesh['rows_0'=2,'rows_1'=4,'rows_2'=4,'rows_3'=2,'cols'=2] {'rows_0','ro..., dimensions={0} | all-to-all | bytes 786432 | tf_op jit(solution)/shard_map/all_to_all | solution.py:259
  42.0 2.7 collective-permute-start.1
  47.9 4.3 %shard_map.52 = (f32[1280,128]{1,0:T(8,128)S(1)}, bf16[1280,128]{1,0:T(8,128)(2,1)S(1)}, bf16[1280,3072]{1,0:T(8,128)(2,1)S(1)}) custom-call(bf16[2048,3072]{1,0:T(8,128)(2,1)} %d.27, bf16[3072,128]{1,0:T(8,128)(2,1)S(1)} %pad_maximum_fusion.1.v), custom_call_target="tpu_custom_call" | custom-call | flops 1006632960 | bytes 7864320 | tf_op jit(solution)/shard_map/pallas_call | solution.py:44
  52.2 2.5 collective-permute-start.4
  56.5 3.3 shard_map.53
  60.4 2.2 collective-permute-done.4.other_ref
  62.7 2.9 shard_map.54
  71.6 13.0 %all_to_all.67 = bf16[32,56,128]{2,1,0:T(8,128)(2,1)S(1)} all-to-all(bf16[32,56,128]{2,1,0:T(8,128)(2,1)S(1)} %pad_maximum_fusion.7), channel_id=1, replica_groups=mesh['rows_0'=2,'rows_1'=4,'rows_2'=4,'rows_3'=2,'cols'=2] {'rows_0','ro..., dimensions={0} | all-to-all | bytes 917504 | tf_op jit(solution)/shard_map/all_to_all | solution.py:259
  85.6 4.4 %all-to-all-start.3 = ((bf16[32,48,128]{2,1,0:T(8,128)(2,1)}), bf16[32,48,128]{2,1,0:T(8,128)(2,1)S(1)}, u32[]{:S(2)}, u32[]{:S(2)}) async-start(bf16[32,48,128]{2,1,0:T(8,128)(2,1)} %broadcast_in_dim.92), calls=%async_computation.3 | async-start | bytes 786432 | tf_op jit(solution)/shard_map/all_to_all | solution.py:259
  93.4 5.2 %all-to-all-done.3 = bf16[32,48,128]{2,1,0:T(8,128)(2,1)S(1)} async-done(((bf16[32,48,128]{2,1,0:T(8,128)(2,1)}), bf16[32,48,128]{2,1,0:T(8,128)(2,1)S(1)}, u32[]{:S(2)}, u32[]{:S(2)}) %all-to-all-start.3) | async-done | bytes 393248 | tf_op jit(solution)/shard_map/all_to_all | solution.py:259
  98.6 3.0 collective-permute-start.6
  103.1 4.4 %shard_map.57 = (f32[1280,128]{1,0:T(8,128)S(1)}, bf16[1280,128]{1,0:T(8,128)(2,1)S(1)}, bf16[1280,3072]{1,0:T(8,128)(2,1)S(1)}) custom-call(bf16[2048,3072]{1,0:T(8,128)(2,1)} %d.27, bf16[3072,128]{1,0:T(8,128)(2,1)S(1)} %pad_maximum_fusion.2.v, f32[1280,128]{1,0:T(8,128)S(1)} %get-tuple-element.173.rest_0_, f32[1,128]{1,0:T(1,128)S(1)} %get-tuple-element.334.rest_1_), custom_call_target="tpu_custom_call" | custom-call | flops 1006632960 | bytes 7864320 | tf_op jit(solution)/shard_map/pallas_call | solution.py:44
  111.2 3.4 shard_map.58
  118.5 3.2 collective-permute-done.8.other_ref
  121.7 3.0 shard_map.59
  129.6 13.1 %all_to_all.68 = bf16[32,56,128]{2,1,0:T(8,128)(2,1)S(1)} all-to-all(bf16[32,56,128]{2,1,0:T(8,128)(2,1)S(1)} %pad_maximum_fusion.8), channel_id=1, replica_groups=mesh['rows_0'=2,'rows_1'=4,'rows_2'=4,'rows_3'=2,'cols'=2] {'rows_0','ro..., dimensions={0} | all-to-all | bytes 917504 | tf_op jit(solution)/shard_map/all_to_all | solution.py:259
  143.0 12.8 %all_to_all.69 = bf16[32,48,128]{2,1,0:T(8,128)(2,1)S(1)} all-to-all(bf16[32,48,128]{2,1,0:T(8,128)(2,1)S(1)} %broadcast_in_dim.97), channel_id=1, replica_groups=mesh['rows_0'=2,'rows_1'=4,'rows_2'=4,'rows_3'=2,'cols'=2] {'rows_0','ro..., dimensions={0} | all-to-all | bytes 786432 | tf_op jit(solution)/shard_map/all_to_all | solution.py:259
  155.7 3.0 collective-permute-start.11
  160.2 4.3 %shard_map.62 = (f32[1280,128]{1,0:T(8,128)S(1)}, bf16[1280,128]{1,0:T(8,128)(2,1)S(1)}, bf16[1280,3072]{1,0:T(8,128)(2,1)S(1)}) custom-call(bf16[2048,3072]{1,0:T(8,128)(2,1)} %d.27, bf16[3072,128]{1,0:T(8,128)(2,1)S(1)} %pad_maximum_fusion.3.v, f32[1280,128]{1,0:T(8,128)S(1)} %get-tuple-element.198.rest_0_, f32[1,128]{1,0:T(1,128)S(1)} %bitcast_divide_fusion.4.rest_1_), custom_call_target="tpu_custom_call" | custom-call | flops 1006632960 | bytes 7864320 | tf_op jit(solution)/shard_map/pallas_call | solution.py:44
  168.1 3.4 shard_map.63
  175.2 3.5 collective-permute-done.13.other_ref
  178.7 3.0 shard_map.64
  186.4 13.2 %all_to_all.70 = bf16[32,56,128]{2,1,0:T(8,128)(2,1)S(1)} all-to-all(bf16[32,56,128]{2,1,0:T(8,128)(2,1)S(1)} %pad_maximum_fusion.9), channel_id=1, replica_groups=mesh['rows_0'=2,'rows_1'=4,'rows_2'=4,'rows_3'=2,'cols'=2] {'rows_0','ro..., dimensions={0} | all-to-all | bytes 917504 | tf_op jit(solution)/shard_map/all_to_all | solution.py:259
  199.8 12.8 %all_to_all.71 = bf16[32,48,128]{2,1,0:T(8,128)(2,1)S(1)} all-to-all(bf16[32,48,128]{2,1,0:T(8,128)(2,1)S(1)} %broadcast_in_dim.102), channel_id=1, replica_groups=mesh['rows_0'=2,'rows_1'=4,'rows_2'=4,'rows_3'=2,'cols'=2] {'rows_0','ro..., dimensions={0} | all-to-all | bytes 786432 | tf_op jit(solution)/shard_map/all_to_all | solution.py:259
  212.5 3.0 collective-permute-start.16
  217.1 4.3 %shard_map.67 = (f32[1280,128]{1,0:T(8,128)S(1)}, bf16[1280,128]{1,0:T(8,128)(2,1)S(1)}, bf16[1280,3072]{1,0:T(8,128)(2,1)S(1)}) custom-call(bf16[2048,3072]{1,0:T(8,128)(2,1)} %d.27, bf16[3072,128]{1,0:T(8,128)(2,1)S(1)} %pad_maximum_fusion.4.v, f32[1280,128]{1,0:T(8,128)S(1)} %get-tuple-element.227.rest_0_, f32[1,128]{1,0:T(1,128)S(1)} %bitcast_divide_fusion.3.rest_1_), custom_call_target="tpu_custom_call" | custom-call | flops 1006632960 | bytes 7864320 | tf_op jit(solution)/shard_map/pallas_call | solution.py:44
  225.0 3.4 shard_map.68
  228.4 2.0 collective-permute-start.18
  232.0 3.5 collective-permute-done.18.other_ref
  235.5 3.0 shard_map.69
  243.2 13.2 %all_to_all.72 = bf16[32,56,128]{2,1,0:T(8,128)(2,1)S(1)} all-to-all(bf16[32,56,128]{2,1,0:T(8,128)(2,1)S(1)} %pad_maximum_fusion.10), channel_id=1, replica_groups=mesh['rows_0'=2,'rows_1'=4,'rows_2'=4,'rows_3'=2,'cols'=2] {'rows_0','ro..., dimensions={0} | all-to-all | bytes 917504 | tf_op jit(solution)/shard_map/all_to_all | solution.py:259
  256.6 12.8 %all_to_all.73 = bf16[32,48,128]{2,1,0:T(8,128)(2,1)S(1)} all-to-all(bf16[32,48,128]{2,1,0:T(8,128)(2,1)S(1)} %broadcast_in_dim.107), channel_id=1, replica_groups=mesh['rows_0'=2,'rows_1'=4,'rows_2'=4,'rows_3'=2,'cols'=2] {'rows_0','ro..., dimensions={0} | all-to-all | bytes 786432 | tf_op jit(solution)/shard_map/all_to_all | solution.py:259
  269.3 3.0 collective-permute-start.21
  273.9 4.3 %shard_map.72 = (f32[1280,128]{1,0:T(8,128)S(1)}, bf16[1280,128]{1,0:T(8,128)(2,1)S(1)}, bf16[1280,3072]{1,0:T(8,128)(2,1)S(1)}) custom-call(bf16[2048,3072]{1,0:T(8,128)(2,1)} %d.27, bf16[3072,128]{1,0:T(8,128)(2,1)S(1)} %pad_maximum_fusion.5.v, f32[1280,128]{1,0:T(8,128)S(1)} %get-tuple-element.256.rest_0_, f32[1,128]{1,0:T(1,128)S(1)} %bitcast_divide_fusion.2.rest_1_), custom_call_target="tpu_custom_call" | custom-call | flops 1006632960 | bytes 7864320 | tf_op jit(solution)/shard_map/pallas_call | solution.py:44
  278.1 2.0 collective-permute-start.24
  280.7 3.4 shard_map.73
  287.6 5.3 %collective-permute-done.22 = f32[1,128]{1,0:T(1,128)S(1)} collective-permute-done((f32[1,128]{1,0:T(1,128)S(1)}, f32[1,128]{1,0:T(1,128)S(1)}, u32[]{:S(2)}, u32[]{:S(2)}) %collective-permute-start.22) | collective-permute-done | bytes 544 | tf_op jit(solution)/shard_map/ppermute | solution.py:25
  293.1 3.0 shard_map.74
  300.3 13.1 %all_to_all.74 = bf16[32,56,128]{2,1,0:T(8,128)(2,1)S(1)} all-to-all(bf16[32,56,128]{2,1,0:T(8,128)(2,1)S(1)} %pad_maximum_fusion.11), channel_id=1, replica_groups=mesh['rows_0'=2,'rows_1'=4,'rows_2'=4,'rows_3'=2,'cols'=2] {'rows_0','ro..., dimensions={0} | all-to-all | bytes 917504 | tf_op jit(solution)/shard_map/all_to_all | solution.py:259
  313.7 12.8 %all_to_all.75 = bf16[32,48,128]{2,1,0:T(8,128)(2,1)S(1)} all-to-all(bf16[32,48,128]{2,1,0:T(8,128)(2,1)S(1)} %broadcast_in_dim.112), channel_id=1, replica_groups=mesh['rows_0'=2,'rows_1'=4,'rows_2'=4,'rows_3'=2,'cols'=2] {'rows_0','ro..., dimensions={0} | all-to-all | bytes 786432 | tf_op jit(solution)/shard_map/all_to_all | solution.py:259
  326.4 3.0 collective-permute-start.26
  330.9 5.8 %shard_map.77 = (f32[1280,128]{1,0:T(8,128)}, bf16[1280,128]{1,0:T(8,128)(2,1)S(1)}) custom-call(bf16[2048,3072]{1,0:T(8,128)(2,1)} %d.27, bf16[3072,128]{1,0:T(8,128)(2,1)S(1)} %pad_maximum_fusion.6.v, f32[1280,128]{1,0:T(8,128)S(1)} %get-tuple-element.285.rest_0_, f32[1,128]{1,0:T(1,128)S(1)} %bitcast_divide_fusion.1.rest_1_), custom_call_target="tpu_custom_call" | custom-call | flops 1006632960 | bytes 7864320 | tf_op jit(solution)/shard_map/pallas_call | solution.py:44
  339.3 4.2 %shard_map.78 = (f32[768,128]{1,0:T(8,128)}, bf16[768,128]{1,0:T(8,128)(2,1)S(1)}) custom-call(bf16[2048,3072]{1,0:T(8,128)(2,1)} %d.27, bf16[3072,128]{1,0:T(8,128)(2,1)S(1)} %pad_maximum_fusion.6.v, f32[768,128]{1,0:T(8,128)S(1)} %get-tuple-element.289.rest_0_, f32[1,128]{1,0:T(1,128)S(1)} %bitcast_divide_fusion.1.rest_1_), custom_call_target="tpu_custom_call" | custom-call | flops 603979776 | bytes 4718592 | tf_op jit(solution)/shard_map/pallas_call | solution.py:44
  346.9 4.6 %collective-permute-done.27 = f32[1,128]{1,0:T(1,128)S(1)} collective-permute-done((f32[1,128]{1,0:T(1,128)S(1)}, f32[1,128]{1,0:T(1,128)S(1)}, u32[]{:S(2)}, u32[]{:S(2)}) %collective-permute-start.27) | collective-permute-done | bytes 544 | tf_op jit(solution)/shard_map/ppermute | solution.py:25
  354.5 10.7 %all_to_all.76 = f32[32,1,128]{2,1,0:T(1,128)S(1)} all-to-all(f32[32,1,128]{2,1,0:T(1,128)S(1)} %broadcast_in_dim.114), channel_id=1, replica_groups=mesh['rows_0'=2,'rows_1'=4,'rows_2'=4,'rows_3'=2,'cols'=2] {'rows_0','ro..., dimensions={0} | all-to-all | bytes 32768 | tf_op jit(solution)/shard_map/all_to_all | solution.py:259
  (198 shorter events, 81.4 us)
Async XLA Ops:
  0.6 1.0 copy-start
  1.7 5.2 %copy-start.1 = (bf16[2048,128]{1,0:T(8,128)(2,1)S(1)}, bf16[2048,128]{1,0:T(8,128)(2,1)}, u32[]{:S(2)}) copy-start(bf16[2048,128]{1,0:T(8,128)(2,1)} %v.3) | copy-start | bytes 1572868
  5.5 5.3 %collective-permute-start = (bf16[1536,128]{1,0:T(8,128)(2,1)S(1)}, bf16[1536,128]{1,0:T(8,128)(2,1)S(1)}, u32[]{:S(2)}, u32[]{:S(2)}) collective-permute-start(bf16[1536,128]{1,0:T(8,128)(2,1)S(1)} %shard_map.51), channel_id=1, source_target_pairs={{0,2},{2,0},{1,3},{3,1},{4,6},{6,4},{5,7},{7,5},{8,10},{10,8},{9,1... | collective-permute-start | bytes 1179656 | tf_op jit(solution)/shard_map/ppermute | solution.py:25
  6.9 3.8 %copy-start.6 = (f32[3072]{0:T(1024)S(1)}, f32[3072]{0:T(1024)}, u32[]{:S(2)}) copy-start(f32[3072]{0:T(1024)} %param.5) | copy-start | bytes 36868
  42.0 4.1 %collective-permute-start.1 = (bf16[1536,128]{1,0:T(8,128)(2,1)S(1)}, bf16[1536,128]{1,0:T(8,128)(2,1)S(1)}, u32[]{:S(2)}, u32[]{:S(2)}) collective-permute-start(bf16[1536,128]{1,0:T(8,128)(2,1)S(1)} %bitcast.150), channel_id=1, source_target_pairs={{0,2},{2,0},{1,3},{3,1},{4,6},{6,4},{5,7},{7,5},{8,10},{10,8},{9,1... | collective-permute-start | bytes 1179656 | tf_op jit(solution)/shard_map/ppermute | solution.py:25
  52.2 10.5 %collective-permute-start.4 = (bf16[1280,128]{1,0:T(8,128)(2,1)S(1)}, bf16[1280,128]{1,0:T(8,128)(2,1)S(1)}, u32[]{:S(2)}, u32[]{:S(2)}) collective-permute-start(bf16[1280,128]{1,0:T(8,128)(2,1)S(1)} %get-tuple-element.164.own_ref), channel_id=1, source_target_pairs={{0,1},{1,0},{2,3},{3,2},{4,5},{5,4},{6,7},{7,6},{8,9},{9,8},{10,11... | collective-permute-start | bytes 983048 | tf_op jit(solution)/shard_map/ppermute | solution.py:25
  59.8 7.4 %collective-permute-start.3 = (bf16[768,128]{1,0:T(8,128)(2,1)S(1)}, bf16[768,128]{1,0:T(8,128)(2,1)S(1)}, u32[]{:S(2)}, u32[]{:S(2)}) collective-permute-start(bf16[768,128]{1,0:T(8,128)(2,1)S(1)} %get-tuple-element.162.own_ref), channel_id=1, source_target_pairs={{0,1},{1,0},{2,3},{3,2},{4,5},{5,4},{6,7},{7,6},{8,9},{9,8},{10,11... | collective-permute-start | bytes 589832 | tf_op jit(solution)/shard_map/ppermute | solution.py:25
  68.5 2.9 collective-permute-start.5
  85.6 13.0 %all-to-all-start.3 = ((bf16[32,48,128]{2,1,0:T(8,128)(2,1)}), bf16[32,48,128]{2,1,0:T(8,128)(2,1)S(1)}, u32[]{:S(2)}, u32[]{:S(2)}) async-start(bf16[32,48,128]{2,1,0:T(8,128)(2,1)} %broadcast_in_dim.92), calls=%async_computation.3 | async-start | bytes 786432 | tf_op jit(solution)/shard_map/all_to_all | solution.py:259
  90.0 11.6 %collective-permute-start.2 = (f32[1,128]{1,0:T(1,128)S(1)}, f32[1,128]{1,0:T(1,128)S(1)}, u32[]{:S(2)}, u32[]{:S(2)}) collective-permute-start(f32[1,128]{1,0:T(1,128)S(1)} %bitcast.175), channel_id=1, source_target_pairs={{0,1},{1,0},{2,3},{3,2},{4,5},{5,4},{6,7},{7,6},{8,9},{9,8},{10,11... | collective-permute-start | bytes 1544 | tf_op jit(solution)/shard_map/ppermute | solution.py:25
  98.6 4.4 %collective-permute-start.6 = (bf16[1536,128]{1,0:T(8,128)(2,1)S(1)}, bf16[1536,128]{1,0:T(8,128)(2,1)S(1)}, u32[]{:S(2)}, u32[]{:S(2)}) collective-permute-start(bf16[1536,128]{1,0:T(8,128)(2,1)S(1)} %bitcast.145), channel_id=1, source_target_pairs={{0,2},{2,0},{1,3},{3,1},{4,6},{6,4},{5,7},{7,5},{8,10},{10,8},{9,1... | collective-permute-start | bytes 1179656 | tf_op jit(solution)/shard_map/ppermute | solution.py:25
  103.1 6.4 %copy-start.2 = (f32[3072,128]{1,0:T(8,128)S(1)}, f32[3072,128]{1,0:T(8,128)}, u32[]{:S(2)}) copy-start(f32[3072,128]{1,0:T(8,128)} %convert_element_type.144) | copy-start | bytes 4718596
  107.5 14.2 %collective-permute-start.9 = (bf16[1280,128]{1,0:T(8,128)(2,1)S(1)}, bf16[1280,128]{1,0:T(8,128)(2,1)S(1)}, u32[]{:S(2)}, u32[]{:S(2)}) collective-permute-start(bf16[1280,128]{1,0:T(8,128)(2,1)S(1)} %get-tuple-element.189.own_ref), channel_id=1, source_target_pairs={{0,1},{1,0},{2,3},{3,2},{4,5},{5,4},{6,7},{7,6},{8,9},{9,8},{10,11... | collective-permute-start | bytes 983048 | tf_op jit(solution)/shard_map/ppermute | solution.py:25
  110.1 7.9 %collective-permute-start.7 = (f32[1,128]{1,0:T(1,128)S(1)}, f32[1,128]{1,0:T(1,128)S(1)}, u32[]{:S(2)}, u32[]{:S(2)}) collective-permute-start(f32[1,128]{1,0:T(1,128)S(1)} %bitcast.173), channel_id=1, source_target_pairs={{0,1},{1,0},{2,3},{3,2},{4,5},{5,4},{6,7},{7,6},{8,9},{9,8},{10,11... | collective-permute-start | bytes 1544 | tf_op jit(solution)/shard_map/ppermute | solution.py:25
  114.5 7.1 %collective-permute-start.8 = (bf16[768,128]{1,0:T(8,128)(2,1)S(1)}, bf16[768,128]{1,0:T(8,128)(2,1)S(1)}, u32[]{:S(2)}, u32[]{:S(2)}) collective-permute-start(bf16[768,128]{1,0:T(8,128)(2,1)S(1)} %get-tuple-element.186.own_ref), channel_id=1, source_target_pairs={{0,1},{1,0},{2,3},{3,2},{4,5},{5,4},{6,7},{7,6},{8,9},{9,8},{10,11... | collective-permute-start | bytes 589832 | tf_op jit(solution)/shard_map/ppermute | solution.py:25
  126.0 3.4 collective-permute-start.10
  155.7 4.4 %collective-permute-start.11 = (bf16[1536,128]{1,0:T(8,128)(2,1)S(1)}, bf16[1536,128]{1,0:T(8,128)(2,1)S(1)}, u32[]{:S(2)}, u32[]{:S(2)}) collective-permute-start(bf16[1536,128]{1,0:T(8,128)(2,1)S(1)} %bitcast.147), channel_id=1, source_target_pairs={{0,2},{2,0},{1,3},{3,1},{4,6},{6,4},{5,7},{7,5},{8,10},{10,8},{9,1... | collective-permute-start | bytes 1179656 | tf_op jit(solution)/shard_map/ppermute | solution.py:25
  164.5 14.2 %collective-permute-start.14 = (bf16[1280,128]{1,0:T(8,128)(2,1)S(1)}, bf16[1280,128]{1,0:T(8,128)(2,1)S(1)}, u32[]{:S(2)}, u32[]{:S(2)}) collective-permute-start(bf16[1280,128]{1,0:T(8,128)(2,1)S(1)} %get-tuple-element.218.own_ref), channel_id=1, source_target_pairs={{0,1},{1,0},{2,3},{3,2},{4,5},{5,4},{6,7},{7,6},{8,9},{9,8},{10,11... | collective-permute-start | bytes 983048 | tf_op jit(solution)/shard_map/ppermute | solution.py:25
  167.1 8.0 %collective-permute-start.12 = (f32[1,128]{1,0:T(1,128)S(1)}, f32[1,128]{1,0:T(1,128)S(1)}, u32[]{:S(2)}, u32[]{:S(2)}) collective-permute-start(f32[1,128]{1,0:T(1,128)S(1)} %bitcast.165), channel_id=1, source_target_pairs={{0,1},{1,0},{2,3},{3,2},{4,5},{5,4},{6,7},{7,6},{8,9},{9,8},{10,11... | collective-permute-start | bytes 1544 | tf_op jit(solution)/shard_map/ppermute | solution.py:25
  171.5 7.2 %collective-permute-start.13 = (bf16[768,128]{1,0:T(8,128)(2,1)S(1)}, bf16[768,128]{1,0:T(8,128)(2,1)S(1)}, u32[]{:S(2)}, u32[]{:S(2)}) collective-permute-start(bf16[768,128]{1,0:T(8,128)(2,1)S(1)} %get-tuple-element.215.own_ref), channel_id=1, source_target_pairs={{0,1},{1,0},{2,3},{3,2},{4,5},{5,4},{6,7},{7,6},{8,9},{9,8},{10,11... | collective-permute-start | bytes 589832 | tf_op jit(solution)/shard_map/ppermute | solution.py:25
  183.0 3.2 collective-permute-start.15
  212.5 4.4 %collective-permute-start.16 = (bf16[1536,128]{1,0:T(8,128)(2,1)S(1)}, bf16[1536,128]{1,0:T(8,128)(2,1)S(1)}, u32[]{:S(2)}, u32[]{:S(2)}) collective-permute-start(bf16[1536,128]{1,0:T(8,128)(2,1)S(1)} %bitcast.148), channel_id=1, source_target_pairs={{0,2},{2,0},{1,3},{3,1},{4,6},{6,4},{5,7},{7,5},{8,10},{10,8},{9,1... | collective-permute-start | bytes 1179656 | tf_op jit(solution)/shard_map/ppermute | solution.py:25
  221.3 14.1 %collective-permute-start.19 = (bf16[1280,128]{1,0:T(8,128)(2,1)S(1)}, bf16[1280,128]{1,0:T(8,128)(2,1)S(1)}, u32[]{:S(2)}, u32[]{:S(2)}) collective-permute-start(bf16[1280,128]{1,0:T(8,128)(2,1)S(1)} %get-tuple-element.247.own_ref), channel_id=1, source_target_pairs={{0,1},{1,0},{2,3},{3,2},{4,5},{5,4},{6,7},{7,6},{8,9},{9,8},{10,11... | collective-permute-start | bytes 983048 | tf_op jit(solution)/shard_map/ppermute | solution.py:25
  223.9 8.0 %collective-permute-start.17 = (f32[1,128]{1,0:T(1,128)S(1)}, f32[1,128]{1,0:T(1,128)S(1)}, u32[]{:S(2)}, u32[]{:S(2)}) collective-permute-start(f32[1,128]{1,0:T(1,128)S(1)} %bitcast.167), channel_id=1, source_target_pairs={{0,1},{1,0},{2,3},{3,2},{4,5},{5,4},{6,7},{7,6},{8,9},{9,8},{10,11... | collective-permute-start | bytes 1544 | tf_op jit(solution)/shard_map/ppermute | solution.py:25
  225.0 5.5 %copy-start.3 = (f32[768,128]{1,0:T(8,128)S(1)}, f32[768,128]{1,0:T(8,128)}, u32[]{:S(2)}) copy-start(f32[768,128]{1,0:T(8,128)} %multiply_subtract_fusion.15) | copy-start | bytes 1179652
  228.4 7.1 %collective-permute-start.18 = (bf16[768,128]{1,0:T(8,128)(2,1)S(1)}, bf16[768,128]{1,0:T(8,128)(2,1)S(1)}, u32[]{:S(2)}, u32[]{:S(2)}) collective-permute-start(bf16[768,128]{1,0:T(8,128)(2,1)S(1)} %get-tuple-element.244.own_ref), channel_id=1, source_target_pairs={{0,1},{1,0},{2,3},{3,2},{4,5},{5,4},{6,7},{7,6},{8,9},{9,8},{10,11... | collective-permute-start | bytes 589832 | tf_op jit(solution)/shard_map/ppermute | solution.py:25
  239.8 3.2 collective-permute-start.20
  269.3 4.4 %collective-permute-start.21 = (bf16[1536,128]{1,0:T(8,128)(2,1)S(1)}, bf16[1536,128]{1,0:T(8,128)(2,1)S(1)}, u32[]{:S(2)}, u32[]{:S(2)}) collective-permute-start(bf16[1536,128]{1,0:T(8,128)(2,1)S(1)} %bitcast.149), channel_id=1, source_target_pairs={{0,2},{2,0},{1,3},{3,1},{4,6},{6,4},{5,7},{7,5},{8,10},{10,8},{9,1... | collective-permute-start | bytes 1179656 | tf_op jit(solution)/shard_map/ppermute | solution.py:25
  278.1 14.9 %collective-permute-start.24 = (bf16[1280,128]{1,0:T(8,128)(2,1)S(1)}, bf16[1280,128]{1,0:T(8,128)(2,1)S(1)}, u32[]{:S(2)}, u32[]{:S(2)}) collective-permute-start(bf16[1280,128]{1,0:T(8,128)(2,1)S(1)} %get-tuple-element.276.own_ref), channel_id=1, source_target_pairs={{0,1},{1,0},{2,3},{3,2},{4,5},{5,4},{6,7},{7,6},{8,9},{9,8},{10,11... | collective-permute-start | bytes 983048 | tf_op jit(solution)/shard_map/ppermute | solution.py:25
  284.0 9.0 %collective-permute-start.23 = (bf16[768,128]{1,0:T(8,128)(2,1)S(1)}, bf16[768,128]{1,0:T(8,128)(2,1)S(1)}, u32[]{:S(2)}, u32[]{:S(2)}) collective-permute-start(bf16[768,128]{1,0:T(8,128)(2,1)S(1)} %get-tuple-element.273.own_ref), channel_id=1, source_target_pairs={{0,1},{1,0},{2,3},{3,2},{4,5},{5,4},{6,7},{7,6},{8,9},{9,8},{10,11... | collective-permute-start | bytes 589832 | tf_op jit(solution)/shard_map/ppermute | solution.py:25
  285.1 7.7 %collective-permute-start.22 = (f32[1,128]{1,0:T(1,128)S(1)}, f32[1,128]{1,0:T(1,128)S(1)}, u32[]{:S(2)}, u32[]{:S(2)}) collective-permute-start(f32[1,128]{1,0:T(1,128)S(1)} %bitcast.169), channel_id=1, source_target_pairs={{0,1},{1,0},{2,3},{3,2},{4,5},{5,4},{6,7},{7,6},{8,9},{9,8},{10,11... | collective-permute-start | bytes 1544 | tf_op jit(solution)/shard_map/ppermute | solution.py:25
  297.4 2.7 collective-permute-start.25
  326.4 4.4 %collective-permute-start.26 = (bf16[1536,128]{1,0:T(8,128)(2,1)S(1)}, bf16[1536,128]{1,0:T(8,128)(2,1)S(1)}, u32[]{:S(2)}, u32[]{:S(2)}) collective-permute-start(bf16[1536,128]{1,0:T(8,128)(2,1)S(1)} %bitcast.146), channel_id=1, source_target_pairs={{0,2},{2,0},{1,3},{3,1},{4,6},{6,4},{5,7},{7,5},{8,10},{10,8},{9,1... | collective-permute-start | bytes 1179656 | tf_op jit(solution)/shard_map/ppermute | solution.py:25
  336.8 14.9 %collective-permute-start.29 = (bf16[1280,128]{1,0:T(8,128)(2,1)S(1)}, bf16[1280,128]{1,0:T(8,128)(2,1)S(1)}, u32[]{:S(2)}, u32[]{:S(2)}) collective-permute-start(bf16[1280,128]{1,0:T(8,128)(2,1)S(1)} %get-tuple-element.300), channel_id=1, source_target_pairs={{0,1},{1,0},{2,3},{3,2},{4,5},{5,4},{6,7},{7,6},{8,9},{9,8},{10,11... | collective-permute-start | bytes 983048 | tf_op jit(solution)/shard_map/ppermute | solution.py:25
  343.5 8.4 %collective-permute-start.28 = (bf16[768,128]{1,0:T(8,128)(2,1)S(1)}, bf16[768,128]{1,0:T(8,128)(2,1)S(1)}, u32[]{:S(2)}, u32[]{:S(2)}) collective-permute-start(bf16[768,128]{1,0:T(8,128)(2,1)S(1)} %get-tuple-element.301), channel_id=1, source_target_pairs={{0,1},{1,0},{2,3},{3,2},{4,5},{5,4},{6,7},{7,6},{8,9},{9,8},{10,11... | collective-permute-start | bytes 589832 | tf_op jit(solution)/shard_map/ppermute | solution.py:25
  344.6 6.9 %collective-permute-start.27 = (f32[1,128]{1,0:T(1,128)S(1)}, f32[1,128]{1,0:T(1,128)S(1)}, u32[]{:S(2)}, u32[]{:S(2)}) collective-permute-start(f32[1,128]{1,0:T(1,128)S(1)} %bitcast.171), channel_id=1, source_target_pairs={{0,1},{1,0},{2,3},{3,2},{4,5},{5,4},{6,7},{7,6},{8,9},{9,8},{10,11... | collective-permute-start | bytes 1544 | tf_op jit(solution)/shard_map/ppermute | solution.py:25
  351.7 0.7 copy-start.4
  352.4 2.1 collective-permute-start.30
  365.3 1.0 copy-start.5
